TPU v7x, 256 devices: a 8x8x2 block of a 8x8x16 slice. The times are simulated.
256 devices in a mesh: groups: 2 (over z), segment: 16 (over y, core), head: 8 (over x).
Axes of the slice: x: 8, y: 8, z: 2, core: 2. Of those that a mesh axis runs over, the one named last changes fastest.
The devices are a block of a 8x8x16 slice.
Arguments:
- token_ids: int32 [6, 256], P('groups'), parts along dimension 0, may hold values from 0 to 151935, as said below
- embed_table: bfloat16 [151936, 256], P(('segment', 'head')), may hold values from -6 to 6
- arriving: bfloat16 [32, 256, 256], P(('groups', 'segment')), parts along dimension 0, may hold values from -16 to 16
- returning: bfloat16 [32, 256, 256], P(('groups', 'segment')), parts along dimension 0, may hold values from -6 to 6
- stashed: bfloat16 [32, 3, 256, 256], P(('groups', 'segment')), parts along dimension 0, may hold values from -16 to 16
- seed_grad: bfloat16 [6, 256, 256], P('groups'), parts along dimension 0, may hold values from -6 to 6
- expand: bfloat16 [16, 256, 2048], P('segment'), may hold values from -0.375 to 0.375
- compress: bfloat16 [16, 2048, 256], P('segment'), may hold values from -0.125 to 0.125
- norm_gain: float32 [16, 2048], P('segment'), may hold values from 0.1 to 1.9
- w_query: bfloat16 [16, 2048, 4096], P('segment', None, 'head'), may hold values from -0.125 to 0.125
- key_weight: bfloat16 [16, 2048, 512], P('segment'), may hold values from -0.125 to 0.125
- value_weight: bfloat16 [16, 2048, 512], P('segment'), may hold values from -0.125 to 0.125
- w_out: bfloat16 [16, 4096, 2048], P('segment', 'head'), may hold values from -0.09375 to 0.09375
Outputs:
- sent_forward: bfloat16 [32, 3, 256, 256], P(('groups', 'segment'), None, 'head'), parts along dimension 0
- sent_backward: bfloat16 [32, 3, 256, 256], P(('groups', 'segment'), None, 'head'), parts along dimension 0
There are 2 independent parts, one for each index of `groups`. A program takes and returns all parts, laid end to end along the dimension named above; an argument that names none is the same for every part. Nothing has to cross between parts.
Inputs may be any that keep to these rules, and one draw needn't show every extreme that they name: `token_ids`: every aligned block of 1187 ids is named by some token.
All inputs are finite; a program needn't handle non-finite values.
Results may differ from a plain program's by a relative error of at most 0.02.
Values may be sent and summed in bfloat16 or wider, within the bound.
No kernel may reach another device: no remote copies, remote signals or barrier semaphores. Data moves between devices by JAX's collectives and lax.ppermute only.
A program may use at most 128 MiB of HBM per device.

v0:
```python
import math

import jax
import jax.numpy as jnp
from jax import lax
from jax.sharding import PartitionSpec as P

QUERY_HEADS = 32
KEY_VALUE_HEADS = 4
HEAD_SIZE = 128


EPS = 1e-06


def rows_for(lines, length):
    spare = -len(lines) % length
    return jnp.pad(lines, [(0, spare)] + [(0, 0)] * (lines.ndim - 1))


def total_of(x, axis):
    lines = x.reshape(-1, *x.shape[1:][-1:])
    own = lax.psum_scatter(
        rows_for(lines, lax.axis_size(axis)), axis, scatter_dimension=0, tiled=True
    )
    whole = lax.all_gather(own, axis).reshape(-1, *lines.shape[1:])
    return lax.slice_in_dim(whole, 0, len(lines)).reshape(x.shape)


def split_up(x, dim, length):
    dims = x.shape
    tiles = x.reshape(*dims[:dim], length, dims[dim] // length, *dims[dim + 1 :])
    return jnp.moveaxis(tiles, dim, 0)


def summed_on_arrival(x, axis, dim):
    tiles = split_up(x, dim, lax.axis_size(axis))
    arrived = lax.all_to_all(tiles, axis, split_axis=0, concat_axis=0, tiled=True)
    return arrived.astype(jnp.float32).sum(axis=0)


def passed_along(x, axis, by):
    length = lax.axis_size(axis)
    pairs = [(i, i + by) for i in range(length) if 0 <= i + by < length]
    return lax.ppermute(x, axis, pairs)


def laid_out(tiles, dim):
    dims = list(tiles.shape[1:])
    dims[dim] *= tiles.shape[0]
    return jnp.moveaxis(tiles, 0, dim).reshape(dims)


def from_everyone(x, axis):
    copies = jnp.broadcast_to(x, (lax.axis_size(axis), *x.shape))
    return lax.all_to_all(copies, axis, split_axis=0, concat_axis=0, tiled=True)


def collect(x, axis, dim):
    return laid_out(from_everyone(x, axis), dim)


def rms_scale(matrix):
    return lax.rsqrt(jnp.mean(matrix * matrix, axis=-1, keepdims=True) + EPS)


def precise(former, latter):
    return jnp.dot(
        former, latter, precision=lax.Precision.HIGHEST, preferred_element_type=jnp.float32
    )


def precise_back(former, latter):
    return lax.dot_general(
        former,
        latter,
        (((1,), (1,)), ((), ())),
        precision=lax.Precision.HIGHEST,
        preferred_element_type=jnp.float32,
    )


def narrow_back(former, latter):
    return lax.dot_general(
        former, latter, (((1,), (1,)), ((), ())), preferred_element_type=jnp.float32
    )


def norm_back(upstream_in, grad_hat):
    scaling = rms_scale(upstream_in)
    return scaling * grad_hat - upstream_in * scaling**3 * jnp.mean(
        grad_hat * upstream_in, axis=-1, keepdims=True
    )


def section_inputs(coeffs, expand_here, gain_here, query_here, key_here, value_here):
    row_count = coeffs.shape[0]
    hidden = jnp.dot(coeffs, expand_here, preferred_element_type=jnp.float32)
    scaling = rms_scale(hidden)
    normed = (hidden * scaling * gain_here).astype(jnp.bfloat16)
    queries = jnp.dot(normed, query_here, preferred_element_type=jnp.float32).reshape(
        row_count, -1, HEAD_SIZE
    )
    key_rows = jnp.dot(normed, key_here, preferred_element_type=jnp.float32).reshape(
        row_count, -1, HEAD_SIZE
    )
    values = (
        jnp.dot(normed, value_here, preferred_element_type=jnp.float32)
        .astype(jnp.bfloat16)
        .reshape(row_count, -1, HEAD_SIZE)
    )
    q_hat = (queries * rms_scale(queries)).astype(jnp.bfloat16)
    k_hat = (key_rows * rms_scale(key_rows)).astype(jnp.bfloat16)
    return (hidden, scaling, queries, key_rows, q_hat, k_hat, values)


def probabilities(q_hat, k_hat):
    row_count, head_count, head_width = q_hat.shape
    kv_heads = k_hat.shape[1]
    grouped = q_hat.reshape(row_count, kv_heads, head_count // kv_heads, head_width)
    scores = jnp.einsum(
        "iknd,jkd->knij", grouped, k_hat, preferred_element_type=jnp.float32
    ) / math.sqrt(head_width)
    causal = jnp.arange(row_count)[None, :] <= jnp.arange(row_count)[:, None]
    weights = jnp.where(causal, jnp.exp(scores), 0.0)
    return weights / jnp.sum(weights, axis=-1, keepdims=True)


def section_forward(coeffs, expand_here, gain_here, query_here, key_here, value_here, out_folded):
    hidden, scaling, queries, key_rows, q_hat, k_hat, values = section_inputs(
        coeffs, expand_here, gain_here, query_here, key_here, value_here
    )
    weights = probabilities(q_hat, k_hat)
    attended = jnp.einsum(
        "knij,jkd->iknd", weights.astype(jnp.bfloat16), values, preferred_element_type=jnp.float32
    )
    attended = attended.reshape(coeffs.shape[0], -1).astype(jnp.bfloat16)
    return jnp.dot(attended, out_folded, preferred_element_type=jnp.float32)


def section_backward(
    coeffs, grads, expand_here, gain_here, query_here, key_here, value_here, out_folded
):
    row_count = coeffs.shape[0]
    hidden, scaling, queries, key_rows, q_hat, k_hat, values = section_inputs(
        coeffs, expand_here, gain_here, query_here, key_here, value_here
    )
    weights = probabilities(q_hat, k_hat)
    head_count = queries.shape[1]
    kv_heads = key_rows.shape[1]
    query_group_size = head_count // kv_heads
    grad_attended = narrow_back(grads, out_folded).astype(jnp.bfloat16)
    grad_attended = grad_attended.reshape(row_count, kv_heads, query_group_size, HEAD_SIZE)
    grad_weights = jnp.einsum(
        "iknd,jkd->knij", grad_attended, values, preferred_element_type=jnp.float32
    )
    grad_scores = (
        weights
        * (grad_weights - jnp.sum(grad_weights * weights, axis=-1, keepdims=True))
        / math.sqrt(HEAD_SIZE)
    )
    grad_scores = grad_scores.astype(jnp.bfloat16)
    grouped = q_hat.reshape(row_count, kv_heads, query_group_size, HEAD_SIZE)
    grad_qhat = jnp.einsum(
        "knij,jkd->iknd", grad_scores, k_hat, preferred_element_type=jnp.float32
    ).reshape(row_count, head_count, HEAD_SIZE)
    grad_khat = jnp.einsum(
        "knij,iknd->jkd", grad_scores, grouped, preferred_element_type=jnp.float32
    )
    grad_values = jnp.einsum(
        "knij,iknd->jkd",
        weights.astype(jnp.bfloat16),
        grad_attended,
        preferred_element_type=jnp.float32,
    )
    grad_values = grad_values.reshape(row_count, -1).astype(jnp.bfloat16)
    grad_queries = norm_back(queries, grad_qhat).reshape(row_count, -1).astype(jnp.bfloat16)
    grad_keys = norm_back(key_rows, grad_khat).reshape(row_count, -1).astype(jnp.bfloat16)
    grad_normed = (
        narrow_back(grad_queries, query_here)
        + narrow_back(grad_keys, key_here)
        + narrow_back(grad_values, value_here)
    )
    weighted = grad_normed * gain_here
    grad_hidden = scaling * weighted - hidden * scaling**3 * jnp.mean(
        weighted * hidden, axis=-1, keepdims=True
    )
    return narrow_back(grad_hidden.astype(jnp.bfloat16), expand_here)


def shards(
    token_ids,
    embed_table,
    arriving,
    returning,
    stashed,
    seed_grad,
    expand,
    compress,
    norm_gain,
    w_query,
    key_weight,
    value_weight,
    w_out,
):
    segment_index = lax.axis_index("segment")
    last_segment = lax.axis_size("segment") - 1
    head_index = lax.axis_index("head")
    heads_here = w_query.shape[2] // HEAD_SIZE
    query_group_size = QUERY_HEADS // KEY_VALUE_HEADS
    kv_here = (heads_here + query_group_size - 1) // query_group_size
    first_kv = head_index * heads_here // query_group_size
    expand_here = expand[0]
    gain_here = norm_gain[0]
    query_here = w_query[0]
    key_here = lax.dynamic_slice_in_dim(key_weight[0], first_kv * HEAD_SIZE, kv_here * HEAD_SIZE, 1)
    value_here = lax.dynamic_slice_in_dim(
        value_weight[0], first_kv * HEAD_SIZE, kv_here * HEAD_SIZE, 1
    )
    basis_folded = jnp.dot(expand_here, compress[0], preferred_element_type=jnp.float32)
    out_folded = jnp.dot(w_out[0], compress[0], preferred_element_type=jnp.float32).astype(
        jnp.bfloat16
    )
    table_rows = embed_table.shape[0]
    local_ids = token_ids.reshape(-1) - lax.axis_index(("segment", "head")) * table_rows
    inside = (local_ids >= 0) & (local_ids < table_rows)
    looked = jnp.take(embed_table, jnp.clip(local_ids, 0, table_rows - 1), axis=0).astype(
        jnp.float32
    )
    picked = jnp.where(inside[:, None], looked, 0.0)
    embedded = total_of(picked, ("segment", "head")).astype(jnp.bfloat16)
    tick_count = token_ids.shape[0]
    span_rows = token_ids.shape[1]
    embedded = embedded.reshape(tick_count, span_rows, -1)
    share_rows = span_rows // lax.axis_size("head")
    share_start = head_index * share_rows
    forward_recv = arriving[0]
    backward_recv = returning[0]
    history = []
    forward_shares = []
    backward_shares = []
    for tick_index in range(tick_count):
        more_ticks = tick_index + 1 < tick_count
        forward_in = jnp.where(segment_index == 0, embedded[tick_index], forward_recv)
        backward_in = jnp.where(segment_index == last_segment, seed_grad[tick_index], backward_recv)
        history.append(forward_in)
        delay_ticks = 2 * (last_segment - segment_index)
        replay = stashed[0, tick_index]
        for earlier in range(tick_index + 1):
            replay = jnp.where(delay_ticks == tick_index - earlier, history[earlier], replay)
        partial_value = section_forward(
            forward_in, expand_here, gain_here, query_here, key_here, value_here, out_folded
        )
        direct = precise(forward_in.astype(jnp.float32), basis_folded)
        summed = summed_on_arrival(partial_value.astype(jnp.bfloat16), "head", 0)
        own_rows = (summed + lax.dynamic_slice_in_dim(direct, share_start, share_rows, 0)).astype(
            jnp.bfloat16
        )
        forward_shares.append(own_rows)
        if more_ticks:
            arrived = passed_along(own_rows, "segment", 1)
            forward_recv = collect(arrived, "head", 0)
        partial_back = section_backward(
            replay,
            backward_in,
            expand_here,
            gain_here,
            query_here,
            key_here,
            value_here,
            out_folded,
        )
        direct_back = precise_back(backward_in.astype(jnp.float32), basis_folded)
        summed_back = summed_on_arrival(partial_back.astype(jnp.bfloat16), "head", 0)
        own_back = (
            summed_back + lax.dynamic_slice_in_dim(direct_back, share_start, share_rows, 0)
        ).astype(jnp.bfloat16)
        backward_shares.append(own_back)
        if more_ticks:
            arrived_back = passed_along(own_back, "segment", -1)
            backward_recv = collect(arrived_back, "head", 0)
    sent_forward = jnp.stack(forward_shares)[None]
    sent_backward = jnp.stack(backward_shares)[None]
    return (sent_forward, sent_backward)


def solution(mesh):
    return jax.shard_map(
        shards,
        mesh=mesh,
        in_specs=(
            P("groups", None),
            P(("segment", "head"), None),
            P(("groups", "segment"), None, None),
            P(("groups", "segment"), None, None),
            P(("groups", "segment"), None, None, None),
            P("groups", None, None),
            P("segment", None, None),
            P("segment", None, None),
            P("segment", None),
            P("segment", None, "head"),
            P("segment", None, None),
            P("segment", None, None),
            P("segment", "head", None),
        ),
        out_specs=(
            P(("groups", "segment"), None, "head", None),
            P(("groups", "segment"), None, "head", None),
        ),
        check_vma=False,
    )
```

profile of v0, /device:TPU:514, one launch (start us, length us, event | category | flops | bytes accessed | tf_op | source)
XLA Modules:
  0.0 754.2 jit_solution(15254184593532937981)
XLA Ops:
  3.0 3.2 gather_fusion
  6.5 269.4 %fusion = f32[8,256]{1,0:T(8,128)S(1)} fusion(f32[768,256]{1,0:T(8,128)S(1)} %convert_select_fusion), kind=kCustom, calls=%all-reduce-scatter | all-reduce-scatter fusion | flops 262145 | bytes 795648
  289.6 11.4 %collective-permute-start.26 = (bf16[8,256]{1,0:T(8,128)(2,1)}, bf16[8,256]{1,0:T(8,128)(2,1)S(1)}, u32[]{:S(2)}, u32[]{:S(2)}) collective-permute-start(bf16[8,256]{1,0:T(8,128)(2,1)} %convert.63), channel_id=1, source_target_pairs={{0,23},{1,24},{2,25},{3,26},{4,27},{5,28},{6,29},{7,30},{8,31},{9,... | collective-permute-start | bytes 12296
  301.1 5.0 collective-permute-start.25
  306.1 6.0 collective-permute-start.24
  317.9 3.3 collective-permute-start.20
  322.5 3.3 fusion.30
  328.2 3.8 collective-permute-start.17
  332.0 3.4 collective-permute-start.16
  335.4 3.2 collective-permute-start.15
  339.4 3.4 collective-permute-start.14
  349.4 3.3 collective-permute-start.10
  352.7 4.2 collective-permute-start.9
  360.5 4.6 collective-permute-start.7
  365.1 3.5 collective-permute-start.6
  374.9 4.0 copy.162
  381.4 24.4 %concatenate = bf16[262,256]{1,0:T(8,128)(2,1)S(1)} concatenate(bf16[6,256]{1,0:T(8,128)(2,1)} %copy-done.63, bf16[8,256]{1,0:T(8,128)(2,1)S(1)} %collective-permute-done.34, bf16[8,256]{1,0:T(8,128)(2,1)} %copy-done.64, bf16[8,256]{1,0:T(8,128)(2,1)} %copy-done.65, bf16[8,256]{1,0:T(8,128)(2,1)} %copy-done.66, bf16[8,256]{1,0:T(8,128)(2,1)} %copy-done.67, ...), dimensions={0} | concatenate | bytes 272384
  405.8 72.3 %all-gather.1 = bf16[128,6,256]{2,1,0:T(8,128)(2,1)} all-gather(bf16[1,6,256]{2,1,0:T(8,128)(2,1)S(1)} %dynamic-slice_bitcast_fusion), channel_id=2, replica_groups=mesh['groups'=2,'segment'=16,'head'=8] {'segment','head'}, dimensions={0}, use_global_device_ids=true | all-gather | bytes 396288 | tf_op jit(solution)/shard_map/all_gather | solution.py:26
  492.2 6.0 all-to-all-start
  499.2 7.3 all-to-all-done
  515.8 5.5 all-to-all-start.1
  521.3 3.3 multiply_reduce_fusion.5
  524.6 4.5 all-to-all-done.1
  541.1 5.3 all-to-all-start.2
  548.3 5.9 all-to-all-done.2
  559.7 5.7 all-to-all-start.3
  568.7 4.8 all-to-all-done.3
  588.1 3.6 fusion.47
  591.7 3.8 multiply_reduce_fusion.11
  611.6 5.9 all-to-all-start.5
  621.8 3.1 fusion.253
  624.9 2.9 convolution_convert_fusion.3
  627.9 3.2 fusion.257
  631.0 3.0 fusion.260
  640.3 7.3 all-to-all-start.6
  649.5 7.1 all-to-all-done.6
  662.0 3.6 fusion.45
  665.6 3.8 multiply_reduce_fusion.10
  676.8 5.5 all-to-all-start.7
  684.2 6.3 all-to-all-done.7
  690.5 5.4 all-to-all-start.4
  699.5 4.2 all-to-all-done.4
  706.6 5.6 all-to-all-start.8
  714.4 5.5 all-to-all-done.8
  725.3 3.7 fusion.43
  728.9 3.9 multiply_reduce_fusion.9
  740.2 4.7 all-to-all-start.9
  745.3 7.4 all-to-all-done.9
  (368 shorter events, 171.9 us)
Async XLA Ops:
  0.6 486.7 %copy-start = (bf16[1,2048,512]{2,1,0:T(8,128)(2,1)S(1)}, bf16[1,2048,512]{2,1,0:T(8,128)(2,1)}, u32[]{:S(2)}) copy-start(bf16[1,2048,512]{2,1,0:T(8,128)(2,1)} %param.24) | copy-start | bytes 6291460
  275.9 66.9 %copy-start.42 = (bf16[1,2048,256]{2,1,0:T(8,128)(2,1)S(1)}, bf16[1,2048,256]{2,1,0:T(8,128)(2,1)}, u32[]{:S(2)}) copy-start(bf16[1,2048,256]{2,1,0:T(8,128)(2,1)} %param.20) | copy-start | bytes 3145732
  276.5 9.1 %collective-permute-start.34 = (bf16[8,256]{1,0:T(8,128)(2,1)}, bf16[8,256]{1,0:T(8,128)(2,1)S(1)}, u32[]{:S(2)}, u32[]{:S(2)}) collective-permute-start(bf16[8,256]{1,0:T(8,128)(2,1)} %convert.63), channel_id=1, source_target_pairs={{0,31},{1,32},{2,33},{3,34},{4,35},{5,36},{6,37},{7,38},{8,39},{9,... | collective-permute-start | bytes 12296
  277.9 6.4 collective-permute-start.35
  279.2 7.7 %collective-permute-start.33 = (bf16[8,256]{1,0:T(8,128)(2,1)}, bf16[8,256]{1,0:T(8,128)(2,1)S(1)}, u32[]{:S(2)}, u32[]{:S(2)}) collective-permute-start(bf16[8,256]{1,0:T(8,128)(2,1)} %convert.63), channel_id=1, source_target_pairs={{0,30},{1,31},{2,32},{3,33},{4,34},{5,35},{6,36},{7,37},{8,38},{9,... | collective-permute-start | bytes 12296
  280.5 7.7 %collective-permute-start.32 = (bf16[8,256]{1,0:T(8,128)(2,1)}, bf16[8,256]{1,0:T(8,128)(2,1)S(1)}, u32[]{:S(2)}, u32[]{:S(2)}) collective-permute-start(bf16[8,256]{1,0:T(8,128)(2,1)} %convert.63), channel_id=1, source_target_pairs={{0,29},{1,30},{2,31},{3,32},{4,33},{5,34},{6,35},{7,36},{8,37},{9,... | collective-permute-start | bytes 12296
  282.8 6.8 collective-permute-start.31
  284.3 16.8 %collective-permute-start.30 = (bf16[8,256]{1,0:T(8,128)(2,1)}, bf16[8,256]{1,0:T(8,128)(2,1)S(1)}, u32[]{:S(2)}, u32[]{:S(2)}) collective-permute-start(bf16[8,256]{1,0:T(8,128)(2,1)} %convert.63), channel_id=1, source_target_pairs={{0,27},{1,28},{2,29},{3,30},{4,31},{5,32},{6,33},{7,34},{8,35},{9,... | collective-permute-start | bytes 12296
  285.6 20.4 %collective-permute-start.29 = (bf16[8,256]{1,0:T(8,128)(2,1)}, bf16[8,256]{1,0:T(8,128)(2,1)S(1)}, u32[]{:S(2)}, u32[]{:S(2)}) collective-permute-start(bf16[8,256]{1,0:T(8,128)(2,1)} %convert.63), channel_id=1, source_target_pairs={{0,26},{1,27},{2,28},{3,29},{4,30},{5,31},{6,32},{7,33},{8,34},{9,... | collective-permute-start | bytes 12296
  286.9 25.1 %collective-permute-start.28 = (bf16[8,256]{1,0:T(8,128)(2,1)}, bf16[8,256]{1,0:T(8,128)(2,1)S(1)}, u32[]{:S(2)}, u32[]{:S(2)}) collective-permute-start(bf16[8,256]{1,0:T(8,128)(2,1)} %convert.63), channel_id=1, source_target_pairs={{0,25},{1,26},{2,27},{3,28},{4,29},{5,30},{6,31},{7,32},{8,33},{9,... | collective-permute-start | bytes 12296
  288.3 26.5 %collective-permute-start.27 = (bf16[8,256]{1,0:T(8,128)(2,1)}, bf16[8,256]{1,0:T(8,128)(2,1)S(1)}, u32[]{:S(2)}, u32[]{:S(2)}) collective-permute-start(bf16[8,256]{1,0:T(8,128)(2,1)} %convert.63), channel_id=1, source_target_pairs={{0,24},{1,25},{2,26},{3,27},{4,28},{5,29},{6,30},{7,31},{8,32},{9,... | collective-permute-start | bytes 12296
  289.6 26.9 %collective-permute-start.26 = (bf16[8,256]{1,0:T(8,128)(2,1)}, bf16[8,256]{1,0:T(8,128)(2,1)S(1)}, u32[]{:S(2)}, u32[]{:S(2)}) collective-permute-start(bf16[8,256]{1,0:T(8,128)(2,1)} %convert.63), channel_id=1, source_target_pairs={{0,23},{1,24},{2,25},{3,26},{4,27},{5,28},{6,29},{7,30},{8,31},{9,... | collective-permute-start | bytes 12296
  301.1 16.8 %collective-permute-start.25 = (bf16[8,256]{1,0:T(8,128)(2,1)}, bf16[8,256]{1,0:T(8,128)(2,1)S(1)}, u32[]{:S(2)}, u32[]{:S(2)}) collective-permute-start(bf16[8,256]{1,0:T(8,128)(2,1)} %convert.63), channel_id=1, source_target_pairs={{0,22},{1,23},{2,24},{3,25},{4,26},{5,27},{6,28},{7,29},{8,30},{9,... | collective-permute-start | bytes 12296
  306.1 15.1 %collective-permute-start.24 = (bf16[8,256]{1,0:T(8,128)(2,1)}, bf16[8,256]{1,0:T(8,128)(2,1)S(1)}, u32[]{:S(2)}, u32[]{:S(2)}) collective-permute-start(bf16[8,256]{1,0:T(8,128)(2,1)} %convert.63), channel_id=1, source_target_pairs={{0,21},{1,22},{2,23},{3,24},{4,25},{5,26},{6,27},{7,28},{8,29},{9,... | collective-permute-start | bytes 12296
  312.1 13.7 %collective-permute-start.23 = (bf16[8,256]{1,0:T(8,128)(2,1)}, bf16[8,256]{1,0:T(8,128)(2,1)S(1)}, u32[]{:S(2)}, u32[]{:S(2)}) collective-permute-start(bf16[8,256]{1,0:T(8,128)(2,1)} %convert.63), channel_id=1, source_target_pairs={{0,20},{1,21},{2,22},{3,23},{4,24},{5,25},{6,26},{7,27},{8,28},{9,... | collective-permute-start | bytes 12296
  314.8 13.5 %collective-permute-start.22 = (bf16[8,256]{1,0:T(8,128)(2,1)}, bf16[8,256]{1,0:T(8,128)(2,1)S(1)}, u32[]{:S(2)}, u32[]{:S(2)}) collective-permute-start(bf16[8,256]{1,0:T(8,128)(2,1)} %convert.63), channel_id=1, source_target_pairs={{0,19},{1,20},{2,21},{3,22},{4,23},{5,24},{6,25},{7,26},{8,27},{9,... | collective-permute-start | bytes 12296
  316.6 15.4 %collective-permute-start.21 = (bf16[8,256]{1,0:T(8,128)(2,1)}, bf16[8,256]{1,0:T(8,128)(2,1)S(1)}, u32[]{:S(2)}, u32[]{:S(2)}) collective-permute-start(bf16[8,256]{1,0:T(8,128)(2,1)} %convert.63), channel_id=1, source_target_pairs={{0,18},{1,19},{2,20},{3,21},{4,22},{5,23},{6,24},{7,25},{8,26},{9,... | collective-permute-start | bytes 12296
  317.9 17.5 %collective-permute-start.20 = (bf16[8,256]{1,0:T(8,128)(2,1)}, bf16[8,256]{1,0:T(8,128)(2,1)S(1)}, u32[]{:S(2)}, u32[]{:S(2)}) collective-permute-start(bf16[8,256]{1,0:T(8,128)(2,1)} %convert.63), channel_id=1, source_target_pairs={{0,17},{1,18},{2,19},{3,20},{4,21},{5,22},{6,23},{7,24},{8,25},{9,... | collective-permute-start | bytes 12296
  321.2 17.5 %collective-permute-start.19 = (bf16[8,256]{1,0:T(8,128)(2,1)}, bf16[8,256]{1,0:T(8,128)(2,1)S(1)}, u32[]{:S(2)}, u32[]{:S(2)}) collective-permute-start(bf16[8,256]{1,0:T(8,128)(2,1)} %convert.63), channel_id=1, source_target_pairs={{0,16},{1,17},{2,18},{3,19},{4,20},{5,21},{6,22},{7,23},{8,24},{9,... | collective-permute-start | bytes 12296
  325.8 17.4 %collective-permute-start.18 = (bf16[8,256]{1,0:T(8,128)(2,1)}, bf16[8,256]{1,0:T(8,128)(2,1)}, u32[]{:S(2)}, u32[]{:S(2)}) collective-permute-start(bf16[8,256]{1,0:T(8,128)(2,1)} %convert.63), channel_id=1, source_target_pairs={{0,15},{1,16},{2,17},{3,18},{4,19},{5,20},{6,21},{7,22},{8,23},{9,... | collective-permute-start | bytes 12296
  328.2 17.3 %collective-permute-start.17 = (bf16[8,256]{1,0:T(8,128)(2,1)}, bf16[8,256]{1,0:T(8,128)(2,1)}, u32[]{:S(2)}, u32[]{:S(2)}) collective-permute-start(bf16[8,256]{1,0:T(8,128)(2,1)} %convert.63), channel_id=1, source_target_pairs={{0,14},{1,15},{2,16},{3,17},{4,18},{5,19},{6,20},{7,21},{8,22},{9,... | collective-permute-start | bytes 12296
  332.0 15.4 %collective-permute-start.16 = (bf16[8,256]{1,0:T(8,128)(2,1)}, bf16[8,256]{1,0:T(8,128)(2,1)}, u32[]{:S(2)}, u32[]{:S(2)}) collective-permute-start(bf16[8,256]{1,0:T(8,128)(2,1)} %convert.63), channel_id=1, source_target_pairs={{0,13},{1,14},{2,15},{3,16},{4,17},{5,18},{6,19},{7,20},{8,21},{9,... | collective-permute-start | bytes 12296
  335.4 14.0 %collective-permute-start.15 = (bf16[8,256]{1,0:T(8,128)(2,1)}, bf16[8,256]{1,0:T(8,128)(2,1)}, u32[]{:S(2)}, u32[]{:S(2)}) collective-permute-start(bf16[8,256]{1,0:T(8,128)(2,1)} %convert.63), channel_id=1, source_target_pairs={{0,12},{1,13},{2,14},{3,15},{4,16},{5,17},{6,18},{7,19},{8,20},{9,... | collective-permute-start | bytes 12296
  339.4 13.3 %collective-permute-start.14 = (bf16[8,256]{1,0:T(8,128)(2,1)}, bf16[8,256]{1,0:T(8,128)(2,1)}, u32[]{:S(2)}, u32[]{:S(2)}) collective-permute-start(bf16[8,256]{1,0:T(8,128)(2,1)} %convert.63), channel_id=1, source_target_pairs={{0,11},{1,12},{2,13},{3,14},{4,15},{5,16},{6,17},{7,18},{8,19},{9,... | collective-permute-start | bytes 12296
  343.2 15.6 %collective-permute-start.13 = (bf16[8,256]{1,0:T(8,128)(2,1)}, bf16[8,256]{1,0:T(8,128)(2,1)}, u32[]{:S(2)}, u32[]{:S(2)}) collective-permute-start(bf16[8,256]{1,0:T(8,128)(2,1)} %convert.63), channel_id=1, source_target_pairs={{0,10},{1,11},{2,12},{3,13},{4,14},{5,15},{6,16},{7,17},{8,18},{9,... | collective-permute-start | bytes 12296
  345.5 15.0 %collective-permute-start.12 = (bf16[8,256]{1,0:T(8,128)(2,1)}, bf16[8,256]{1,0:T(8,128)(2,1)}, u32[]{:S(2)}, u32[]{:S(2)}) collective-permute-start(bf16[8,256]{1,0:T(8,128)(2,1)} %convert.63), channel_id=1, source_target_pairs={{0,9},{1,10},{2,11},{3,12},{4,13},{5,14},{6,15},{7,16},{8,17},{9,1... | collective-permute-start | bytes 12296
  347.4 17.7 %collective-permute-start.11 = (bf16[8,256]{1,0:T(8,128)(2,1)}, bf16[8,256]{1,0:T(8,128)(2,1)}, u32[]{:S(2)}, u32[]{:S(2)}) collective-permute-start(bf16[8,256]{1,0:T(8,128)(2,1)} %convert.63), channel_id=1, source_target_pairs={{0,8},{1,9},{2,10},{3,11},{4,12},{5,13},{6,14},{7,15},{8,16},{9,17... | collective-permute-start | bytes 12296
  349.4 19.2 %collective-permute-start.10 = (bf16[8,256]{1,0:T(8,128)(2,1)}, bf16[8,256]{1,0:T(8,128)(2,1)}, u32[]{:S(2)}, u32[]{:S(2)}) collective-permute-start(bf16[8,256]{1,0:T(8,128)(2,1)} %convert.63), channel_id=1, source_target_pairs={{0,7},{1,8},{2,9},{3,10},{4,11},{5,12},{6,13},{7,14},{8,15},{9,16}... | collective-permute-start | bytes 12296
  352.7 18.7 %collective-permute-start.9 = (bf16[8,256]{1,0:T(8,128)(2,1)}, bf16[8,256]{1,0:T(8,128)(2,1)}, u32[]{:S(2)}, u32[]{:S(2)}) collective-permute-start(bf16[8,256]{1,0:T(8,128)(2,1)} %convert.63), channel_id=1, source_target_pairs={{0,6},{1,7},{2,8},{3,9},{4,10},{5,11},{6,12},{7,13},{8,14},{9,15},... | collective-permute-start | bytes 12296
  358.9 21.3 %collective-permute-start.8 = (bf16[8,256]{1,0:T(8,128)(2,1)}, bf16[8,256]{1,0:T(8,128)(2,1)S(1)}, u32[]{:S(2)}, u32[]{:S(2)}) collective-permute-start(bf16[8,256]{1,0:T(8,128)(2,1)} %convert.63), channel_id=1, source_target_pairs={{0,5},{1,6},{2,7},{3,8},{4,9},{5,10},{6,11},{7,12},{8,13},{9,14},{... | collective-permute-start | bytes 12296
  360.5 19.7 %collective-permute-start.7 = (bf16[8,256]{1,0:T(8,128)(2,1)}, bf16[8,256]{1,0:T(8,128)(2,1)S(1)}, u32[]{:S(2)}, u32[]{:S(2)}) collective-permute-start(bf16[8,256]{1,0:T(8,128)(2,1)} %convert.63), channel_id=1, source_target_pairs={{0,4},{1,5},{2,6},{3,7},{4,8},{5,9},{6,10},{7,11},{8,12},{9,13},{1... | collective-permute-start | bytes 12296
  365.1 15.1 %collective-permute-start.6 = (bf16[8,256]{1,0:T(8,128)(2,1)}, bf16[8,256]{1,0:T(8,128)(2,1)S(1)}, u32[]{:S(2)}, u32[]{:S(2)}) collective-permute-start(bf16[8,256]{1,0:T(8,128)(2,1)} %convert.63), channel_id=1, source_target_pairs={{0,3},{1,4},{2,5},{3,6},{4,7},{5,8},{6,9},{7,10},{8,11},{9,12},{10... | collective-permute-start | bytes 12296
  368.6 11.6 %collective-permute-start.5 = (bf16[8,256]{1,0:T(8,128)(2,1)}, bf16[8,256]{1,0:T(8,128)(2,1)S(1)}, u32[]{:S(2)}, u32[]{:S(2)}) collective-permute-start(bf16[8,256]{1,0:T(8,128)(2,1)} %convert.63), channel_id=1, source_target_pairs={{0,2},{1,3},{2,4},{3,5},{4,6},{5,7},{6,8},{7,9},{8,10},{9,11},{10,... | collective-permute-start | bytes 12296
  371.4 10.1 %collective-permute-start.4 = (bf16[8,256]{1,0:T(8,128)(2,1)}, bf16[8,256]{1,0:T(8,128)(2,1)}, u32[]{:S(2)}, u32[]{:S(2)}) collective-permute-start(bf16[8,256]{1,0:T(8,128)(2,1)} %convert.63), channel_id=1, source_target_pairs={{0,1},{1,2},{2,3},{3,4},{4,5},{5,6},{6,7},{7,8},{8,9},{9,10},{10,1... | collective-permute-start | bytes 12296
  492.2 14.2 %all-to-all-start = ((bf16[8,32,256]{2,1,0:T(8,128)(2,1)}), bf16[8,32,256]{2,1,0:T(8,128)(2,1)}, u32[]{:S(2)}, u32[]{:S(2)}) async-start(bf16[8,32,256]{2,1,0:T(8,128)(2,1)} %bitcast.590), calls=%async_computation | async-start | bytes 262144 | tf_op jit(solution)/shard_map/all_to_all | solution.py:38
  508.8 5.7 collective-permute-start
  515.8 13.3 %all-to-all-start.1 = ((bf16[8,32,256]{2,1,0:T(8,128)(2,1)}), bf16[8,32,256]{2,1,0:T(8,128)(2,1)}, u32[]{:S(2)}, u32[]{:S(2)}) async-start(bf16[8,32,256]{2,1,0:T(8,128)(2,1)} %broadcast_in_dim.68), calls=%async_computation.1 | async-start | bytes 262144 | tf_op jit(solution)/shard_map/all_to_all | solution.py:56
  541.1 13.1 %all-to-all-start.2 = ((bf16[8,32,256]{2,1,0:T(8,128)(2,1)}), bf16[8,32,256]{2,1,0:T(8,128)(2,1)}, u32[]{:S(2)}, u32[]{:S(2)}) async-start(bf16[8,32,256]{2,1,0:T(8,128)(2,1)} %bitcast.591), calls=%async_computation.2 | async-start | bytes 262144 | tf_op jit(solution)/shard_map/all_to_all | solution.py:38
  556.5 2.5 collective-permute-start.1
  559.7 13.7 %all-to-all-start.3 = ((bf16[8,32,256]{2,1,0:T(8,128)(2,1)}), bf16[8,32,256]{2,1,0:T(8,128)(2,1)}, u32[]{:S(2)}, u32[]{:S(2)}) async-start(bf16[8,32,256]{2,1,0:T(8,128)(2,1)} %broadcast_in_dim.69), calls=%async_computation.3 | async-start | bytes 262144 | tf_op jit(solution)/shard_map/all_to_all | solution.py:56
  611.6 22.4 %all-to-all-start.5 = ((bf16[8,32,256]{2,1,0:T(8,128)(2,1)}), bf16[8,32,256]{2,1,0:T(8,128)(2,1)}, u32[]{:S(2)}, u32[]{:S(2)}) async-start(bf16[8,32,256]{2,1,0:T(8,128)(2,1)} %bitcast.587), calls=%async_computation.5 | async-start | bytes 262144 | tf_op jit(solution)/shard_map/all_to_all | solution.py:38
  636.4 3.2 collective-permute-start.2
  640.3 16.3 %all-to-all-start.6 = ((bf16[8,32,256]{2,1,0:T(8,128)(2,1)}), bf16[8,32,256]{2,1,0:T(8,128)(2,1)}, u32[]{:S(2)}, u32[]{:S(2)}) async-start(bf16[8,32,256]{2,1,0:T(8,128)(2,1)} %broadcast_in_dim.71), calls=%async_computation.6 | async-start | bytes 262144 | tf_op jit(solution)/shard_map/all_to_all | solution.py:56
  676.8 13.8 %all-to-all-start.7 = ((bf16[8,32,256]{2,1,0:T(8,128)(2,1)}), bf16[8,32,256]{2,1,0:T(8,128)(2,1)}, u32[]{:S(2)}, u32[]{:S(2)}) async-start(bf16[8,32,256]{2,1,0:T(8,128)(2,1)} %bitcast.589), calls=%async_computation.7 | async-start | bytes 262144 | tf_op jit(solution)/shard_map/all_to_all | solution.py:38
  690.5 13.2 %all-to-all-start.4 = ((bf16[8,32,256]{2,1,0:T(8,128)(2,1)}), bf16[8,32,256]{2,1,0:T(8,128)(2,1)}, u32[]{:S(2)}, u32[]{:S(2)}) async-start(bf16[8,32,256]{2,1,0:T(8,128)(2,1)} %bitcast.586), calls=%async_computation.4 | async-start | bytes 262144 | tf_op jit(solution)/shard_map/all_to_all | solution.py:38
  698.2 7.0 collective-permute-start.3
  706.6 13.3 %all-to-all-start.8 = ((bf16[8,32,256]{2,1,0:T(8,128)(2,1)}), bf16[8,32,256]{2,1,0:T(8,128)(2,1)}, u32[]{:S(2)}, u32[]{:S(2)}) async-start(bf16[8,32,256]{2,1,0:T(8,128)(2,1)} %broadcast_in_dim.72), calls=%async_computation.8 | async-start | bytes 262144 | tf_op jit(solution)/shard_map/all_to_all | solution.py:56
  740.2 12.4 %all-to-all-start.9 = ((bf16[8,32,256]{2,1,0:T(8,128)(2,1)}), bf16[8,32,256]{2,1,0:T(8,128)(2,1)S(1)}, u32[]{:S(2)}, u32[]{:S(2)}) async-start(bf16[8,32,256]{2,1,0:T(8,128)(2,1)} %bitcast.588), calls=%async_computation.9 | async-start | bytes 262144 | tf_op jit(solution)/shard_map/all_to_all | solution.py:38
  (88 other events, 803.5 us)
where the time goes:
time: 765 us; the launch traced here: 754 us
  blocking collectives  342 us (45%)
  starting transfers between devices  153 us (20%)
  matrix products  108 us (14%)
  local copies, waits for them, and re-layouts  55.6 us (7%)
  waiting for transfers between devices  53 us (7%)
  other arithmetic  39.3 us (5%)
    unnamed x1, blocking collectives  269 us
    unnamed x32, starting transfers between devices  90.8 us
    all_gather x1, blocking collectives, total_of(): whole = lax.all_gather(own, axis).reshape(-1, *lines.shape[1:])  72.3 us
    unnamed x185, local copies, waits for them, and re-layouts  37 us
    all_to_all x6, starting transfers between devices, summed_on_arrival(): lax.all_to_all(tiles, axis, split_axis=0, concat_axis=0, tiled=True)  32.8 us
    all_to_all x6, waiting for transfers between devices, summed_on_arrival(): lax.all_to_all(tiles, axis, split_axis=0, concat_axis=0, tiled=True)  31 us
    dot_general x15, matrix products, narrow_back(): lax.dot_general(former, latter, (((1,), (1,)), ((), ())), preferred_eleme...  27.4 us
    all_to_all x4, starting transfers between devices, from_everyone(): return lax.all_to_all(copies, axis, split_axis=0, concat_axis=0, tiled=True)  24.1 us
  transfers between devices with their start and end apart: 46, of which 9 were waited for; matrix products, arithmetic and copies ran while one was open for 7% of the time, Pallas kernels for 0%

commit v1 on v0

v1 whole, which is shorter than its diff:
```python
import functools
import math

import jax
import jax.numpy as jnp
from jax import lax
from jax.experimental import pallas as pl
from jax.experimental.pallas import tpu as pltpu
from jax.sharding import PartitionSpec as P

QUERY_HEADS = 32
KEY_VALUE_HEADS = 4
HEAD_SIZE = 128

EPS = 1e-06
CHUNK = 512

VMEM = pl.BlockSpec(memory_space=pltpu.VMEM)
SMEM = pl.BlockSpec(memory_space=pltpu.SMEM)


def dot(former, latter):
    return jnp.dot(former, latter, preferred_element_type=jnp.float32)


def dot_back(former, latter):
    return lax.dot_general(
        former, latter, (((1,), (1,)), ((), ())), preferred_element_type=jnp.float32
    )


def dot_turned(former, latter):
    return lax.dot_general(
        former, latter, (((0,), (0,)), ((), ())), preferred_element_type=jnp.float32
    )


def rms_scale(matrix):
    return lax.rsqrt(jnp.mean(matrix * matrix, axis=-1, keepdims=True) + EPS)


def norm_back(upstream_in, grad_hat):
    scaling = rms_scale(upstream_in)
    return scaling * grad_hat - upstream_in * scaling**3 * jnp.mean(
        grad_hat * upstream_in, axis=-1, keepdims=True
    )


def spread(coeffs, expand_ref, gain_ref, query_ref, kv_ref, hidden_ref):
    width = expand_ref.shape[1]
    squares = jnp.zeros((coeffs.shape[0], 1), jnp.float32)
    for at in range(0, width, CHUNK):
        here = pl.ds(at, CHUNK)
        part = dot(coeffs, expand_ref[:, here])
        hidden_ref[:, here] = part
        squares += jnp.sum(part * part, axis=-1, keepdims=True)
    scaling = lax.rsqrt(squares / width + EPS)
    queries = jnp.zeros((coeffs.shape[0], query_ref.shape[1]), jnp.float32)
    kv = jnp.zeros((coeffs.shape[0], kv_ref.shape[1]), jnp.float32)
    for at in range(0, width, CHUNK):
        here = pl.ds(at, CHUNK)
        normed = (hidden_ref[:, here] * scaling * gain_ref[:, here]).astype(jnp.bfloat16)
        queries += dot(normed, query_ref[here, :])
        kv += dot(normed, kv_ref[here, :])
    return scaling, queries, kv[:, :HEAD_SIZE], kv[:, HEAD_SIZE:].astype(jnp.bfloat16)


def probabilities(q_hat, k_hat):
    rows = q_hat.shape[0]
    scores = dot_back(q_hat, k_hat) * (1.0 / math.sqrt(HEAD_SIZE))
    column = lax.broadcasted_iota(jnp.int32, (rows, rows), 1)
    row = lax.broadcasted_iota(jnp.int32, (rows, rows), 0)
    weights = jnp.where(column <= row, jnp.exp(scores), 0.0)
    return weights / jnp.sum(weights, axis=-1, keepdims=True)


def forward_kernel(
    coeffs_ref, expand_ref, gain_ref, query_ref, kv_ref, folded_ref, out_ref, hidden_ref
):
    scaling, queries, keys, values = spread(
        coeffs_ref[...], expand_ref, gain_ref, query_ref, kv_ref, hidden_ref
    )
    k_hat = (keys * rms_scale(keys)).astype(jnp.bfloat16)
    total = jnp.zeros(out_ref.shape, jnp.float32)
    for at in range(0, queries.shape[1], HEAD_SIZE):
        head = queries[:, at : at + HEAD_SIZE]
        q_hat = (head * rms_scale(head)).astype(jnp.bfloat16)
        low = probabilities(q_hat, k_hat).astype(jnp.bfloat16)
        attended = dot(low, values).astype(jnp.bfloat16)
        total += dot(attended, folded_ref[at : at + HEAD_SIZE, :])
    out_ref[...] = total.astype(out_ref.dtype)


def backward_kernel(
    flags_ref,
    stashed_ref,
    *refs,
):
    replays = refs[: flags_ref.shape[0]]
    (
        grads_ref,
        expand_ref,
        gain_ref,
        query_ref,
        kv_ref,
        folded_ref,
        out_ref,
        hidden_ref,
        weighted_ref,
    ) = refs[flags_ref.shape[0] :]
    coeffs = stashed_ref[...]
    for place, replay_ref in enumerate(replays):
        coeffs = jnp.where(flags_ref[place] != 0, replay_ref[...], coeffs)
    scaling, queries, keys, values = spread(
        coeffs, expand_ref, gain_ref, query_ref, kv_ref, hidden_ref
    )
    k_hat = (keys * rms_scale(keys)).astype(jnp.bfloat16)
    grads = grads_ref[...]
    grad_khat = jnp.zeros(keys.shape, jnp.float32)
    grad_values = jnp.zeros(keys.shape, jnp.float32)
    grad_queries = []
    for at in range(0, queries.shape[1], HEAD_SIZE):
        head = queries[:, at : at + HEAD_SIZE]
        q_hat = (head * rms_scale(head)).astype(jnp.bfloat16)
        weights = probabilities(q_hat, k_hat)
        grad_attended = dot_back(grads, folded_ref[at : at + HEAD_SIZE, :]).astype(jnp.bfloat16)
        grad_weights = dot_back(grad_attended, values)
        inner = jnp.sum(grad_weights * weights, axis=-1, keepdims=True)
        grad_scores = weights * (grad_weights - inner) * (1.0 / math.sqrt(HEAD_SIZE))
        grad_scores = grad_scores.astype(jnp.bfloat16)
        grad_qhat = dot(grad_scores, k_hat)
        grad_khat += dot_turned(grad_scores, q_hat)
        grad_values += dot_turned(weights.astype(jnp.bfloat16), grad_attended)
        grad_queries.append(norm_back(head, grad_qhat).astype(jnp.bfloat16))
    grad_queries = jnp.concatenate(grad_queries, axis=1)
    grad_kv = jnp.concatenate(
        [norm_back(keys, grad_khat).astype(jnp.bfloat16), grad_values.astype(jnp.bfloat16)], axis=1
    )
    width = expand_ref.shape[1]
    inner = jnp.zeros((coeffs.shape[0], 1), jnp.float32)
    for at in range(0, width, CHUNK):
        here = pl.ds(at, CHUNK)
        grad_normed = dot_back(grad_queries, query_ref[here, :]) + dot_back(grad_kv, kv_ref[here, :])
        weighted = grad_normed * gain_ref[:, here]
        weighted_ref[:, here] = weighted
        inner += jnp.sum(weighted * hidden_ref[:, here], axis=-1, keepdims=True)
    factor = scaling**3 * (inner / width)
    total = jnp.zeros(out_ref.shape, jnp.float32)
    for at in range(0, width, CHUNK):
        here = pl.ds(at, CHUNK)
        grad_hidden = scaling * weighted_ref[:, here] - hidden_ref[:, here] * factor
        total += dot_back(grad_hidden.astype(jnp.bfloat16), expand_ref[:, here])
    out_ref[...] = total.astype(out_ref.dtype)


def fold_kernel(expand_ref, compress_ref, out_weight_ref, basis_ref, folded_ref):
    basis_ref[...] = dot(expand_ref[...], compress_ref[...])
    folded_ref[...] = dot(out_weight_ref[...], compress_ref[...]).astype(folded_ref.dtype)


def finish_kernel(back, parts_ref, rows_ref, basis_ref, out_ref):
    direct = lax.dot_general(
        rows_ref[...].astype(jnp.float32),
        basis_ref[...],
        (((1,), (1 if back else 0,)), ((), ())),
        precision=lax.Precision.HIGHEST,
        preferred_element_type=jnp.float32,
    )
    summed = parts_ref[0].astype(jnp.float32)
    for place in range(1, parts_ref.shape[0]):
        summed += parts_ref[place].astype(jnp.float32)
    out_ref[...] = (summed + direct).astype(out_ref.dtype)


def in_vmem(body, outs, count, scratch=(), scalars=0, flops=0):
    return pl.pallas_call(
        body,
        out_shape=outs,
        in_specs=[SMEM] * scalars + [VMEM] * count,
        out_specs=jax.tree.map(lambda _: VMEM, outs),
        scratch_shapes=list(scratch),
        cost_estimate=pl.CostEstimate(flops=flops, bytes_accessed=2**20, transcendentals=0)
        if flops
        else None,
        compiler_params=pltpu.CompilerParams(vmem_limit_bytes=24 * 2**20),
    )


def shape_of(dims, kind):
    return jax.ShapeDtypeStruct(dims, kind)


def exchanged(x, axis):
    tiles = x.reshape(lax.axis_size(axis), -1, x.shape[-1])
    return lax.all_to_all(tiles, axis, split_axis=0, concat_axis=0, tiled=True)


def passed_along(x, axis, by):
    length = lax.axis_size(axis)
    pairs = [(i, i + by) for i in range(length) if 0 <= i + by < length]
    return lax.ppermute(x, axis, pairs)


def brought_to_first(x, axis):
    length = lax.axis_size(axis)
    step = 1
    while step < length:
        pairs = [(i, i - step) for i in range(step, length, 2 * step)]
        x = x + lax.ppermute(x, axis, pairs)
        step *= 2
    return x


def collect(x, axis):
    copies = jnp.broadcast_to(x, (lax.axis_size(axis), *x.shape))
    tiles = lax.all_to_all(copies, axis, split_axis=0, concat_axis=0, tiled=True)
    return tiles.reshape(-1, x.shape[-1])


def shards(
    token_ids,
    embed_table,
    arriving,
    returning,
    stashed,
    seed_grad,
    expand,
    compress,
    norm_gain,
    w_query,
    key_weight,
    value_weight,
    w_out,
):
    segment_index = lax.axis_index("segment")
    last_segment = lax.axis_size("segment") - 1
    head_index = lax.axis_index("head")
    is_first = segment_index == 0
    is_last = segment_index == last_segment
    ticks, span = token_ids.shape
    rank = embed_table.shape[1]
    share = span // lax.axis_size("head")
    start = head_index * share

    table_rows = embed_table.shape[0]
    first_row = lax.axis_index(("segment", "head")) * table_rows

    def picked(ids):
        local = ids - first_row
        inside = (local >= 0) & (local < table_rows)
        looked = jnp.take(embed_table, jnp.clip(local, 0, table_rows - 1), axis=0)
        return jnp.where(inside[:, None], looked, jnp.zeros((), looked.dtype))

    def own_rows_of(ids):
        return brought_to_first(exchanged(picked(ids), "head").sum(axis=0), "segment")

    embedded_rows = own_rows_of(token_ids[0])
    embedded = collect(embedded_rows, "head")
    later = exchanged(picked(token_ids[1:].reshape(-1)).reshape(ticks - 1, -1, share, rank).swapaxes(0, 1), "head")
    later = brought_to_first(later.reshape(-1, ticks - 1, share, rank).sum(axis=0), "segment")

    heads_here = w_query.shape[2] // HEAD_SIZE
    query_group_size = QUERY_HEADS // KEY_VALUE_HEADS
    first_kv = head_index * heads_here // query_group_size * HEAD_SIZE
    expand_here = expand[0]
    gain_here = norm_gain
    query_here = w_query[0]
    kv_here = jnp.concatenate(
        [
            lax.dynamic_slice_in_dim(key_weight[0], first_kv, HEAD_SIZE, 1),
            lax.dynamic_slice_in_dim(value_weight[0], first_kv, HEAD_SIZE, 1),
        ],
        axis=1,
    )
    width = expand_here.shape[1]
    low = jnp.bfloat16
    basis, folded = in_vmem(
        fold_kernel,
        (shape_of((rank, rank), jnp.float32), shape_of((w_out.shape[1], rank), low)),
        3,
    )(expand_here, compress[0], w_out[0])
    weights = (expand_here, gain_here, query_here, kv_here, folded)

    square = shape_of((span, rank), low)
    wide = pltpu.VMEM((span, width), jnp.float32)

    def forward(coeffs):
        return in_vmem(forward_kernel, square, 6, [wide])(coeffs, *weights)

    def backward(flags, stash, replays, grads):
        return in_vmem(backward_kernel, square, 7 + len(replays), [wide, wide], 1)(
            flags, stash, *replays, grads, *weights
        )

    def finish(partial, rows, back):
        return in_vmem(functools.partial(finish_kernel, back), shape_of((share, rank), low), 3)(
            exchanged(partial, "head"), rows, basis
        )

    def mine(x):
        return lax.dynamic_slice_in_dim(x, start, share, 0)

    forward_in = jnp.where(is_first, embedded, arriving[0])
    backward_in = jnp.where(is_last, seed_grad[0], returning[0])
    forward_rows = mine(forward_in)
    backward_rows = mine(backward_in)
    delay = 2 * (last_segment - segment_index)
    history = []
    apart = lax.axis_size("segment") > 2
    forward_shares = []
    backward_shares = []
    for tick in range(ticks):
        more = tick + 1 < ticks
        history.append(arriving[0] if tick == 0 and apart else forward_in)
        replays = [history[k] for k in range(tick + 1) if (tick - k) % 2 == 0]
        flags = jnp.stack(
            [(delay == tick - k).astype(jnp.int32) for k in range(tick + 1) if (tick - k) % 2 == 0]
        )
        out = finish(forward(forward_in), forward_rows, False)
        forward_shares.append(out)
        out_back = finish(
            backward(flags, stashed[0, tick], replays, backward_in), backward_rows, True
        )
        backward_shares.append(out_back)
        if more:
            arrived = passed_along(out, "segment", 1)
            forward_rows = jnp.where(is_first, later[tick], arrived)
            forward_in = collect(forward_rows, "head")
            arrived = passed_along(out_back, "segment", -1)
            backward_rows = jnp.where(is_last, mine(seed_grad[tick + 1]), arrived)
            backward_in = collect(backward_rows, "head")
    return (jnp.stack(forward_shares)[None], jnp.stack(backward_shares)[None])


def solution(mesh):
    return jax.shard_map(
        shards,
        mesh=mesh,
        in_specs=(
            P("groups", None),
            P(("segment", "head"), None),
            P(("groups", "segment"), None, None),
            P(("groups", "segment"), None, None),
            P(("groups", "segment"), None, None, None),
            P("groups", None, None),
            P("segment", None, None),
            P("segment", None, None),
            P("segment", None),
            P("segment", None, "head"),
            P("segment", None, None),
            P("segment", None, None),
            P("segment", "head", None),
        ),
        out_specs=(
            P(("groups", "segment"), None, "head", None),
            P(("groups", "segment"), None, "head", None),
        ),
        check_vma=False,
    )
```

time: 765 us -> 266 us (0.35); the launches traced: 754 us -> 263 us
  blocking collectives: 342 us -> 11.5 us
  matrix products: 108 us -> 0 us
  starting transfers between devices: 153 us -> 105 us
  Pallas kernels: 0 us -> 37.1 us
  other arithmetic: 39.3 us -> 17.1 us
  local copies, waits for them, and re-layouts: 55.6 us -> 38 us
    unnamed x1 -> x0, blocking collectives: 269 us -> none
    dot_general x62 -> x0, matrix products: 108 us -> none  [the longest x15 27.4 us: narrow_back(): lax.dot_general(former, latter, (((1,), (1,)), ((), ())), preferred_eleme...]
    unnamed x32 -> x0, starting transfers between devices: 90.8 us -> none
    all_gather x1 -> x0, blocking collectives: 72.3 us -> none  [total_of(): whole = lax.all_gather(own, axis).reshape(-1, *lines.shape[1:])]
    pallas_call x0 -> x13, Pallas kernels: none -> 37.1 us  [the longest x3 19.4 us: backward(): in_vmem(backward_kernel, square, 7 + len(replays), [wide, wide], 1)]
    all_to_all x10 -> x12, starting transfers between devices: 56.9 us -> 88.4 us  [the longest x8 64.4 us: exchanged(): return lax.all_to_all(tiles, axis, split_axis=0, concat_axis=0, tiled=True)]
    ppermute x0 -> x8, waiting for transfers between devices: none -> 16.2 us  [brought_to_first(): x = x + lax.ppermute(x, axis, pairs)]
    all_to_all x10 -> x12, waiting for transfers between devices: 52.9 us -> 37 us  [the longest x4 20.8 us: collect(): lax.all_to_all(copies, axis, split_axis=0, concat_axis=0, tiled=True)]
  transfers between devices with their start and end apart: 46 -> 24, of which waited for: 9 -> 14; matrix products, arithmetic and copies ran while one was open for 7% -> 8% of each run, Pallas kernels for 0% -> 9%
where the time goes in v1:
time: 266 us; the launch traced here: 263 us
  starting transfers between devices  105 us (39%)
  waiting for transfers between devices  53.3 us (20%)
  local copies, waits for them, and re-layouts  38 us (14%)
  Pallas kernels  37.1 us (14%)
  other arithmetic  17.1 us (6%)
  blocking collectives  11.5 us (4%)
    all_to_all x8, starting transfers between devices, exchanged(): return lax.all_to_all(tiles, axis, split_axis=0, concat_axis=0, tiled=True)  64.4 us
    unnamed x73, local copies, waits for them, and re-layouts  28.1 us
    all_to_all x4, starting transfers between devices, collect(): lax.all_to_all(copies, axis, split_axis=0, concat_axis=0, tiled=True)  24 us
    all_to_all x4, waiting for transfers between devices, collect(): lax.all_to_all(copies, axis, split_axis=0, concat_axis=0, tiled=True)  20.8 us
    pallas_call x3, Pallas kernels, backward(): in_vmem(backward_kernel, square, 7 + len(replays), [wide, wide], 1)  19.4 us
    ppermute x8, waiting for transfers between devices, brought_to_first(): x = x + lax.ppermute(x, axis, pairs)  16.2 us
    all_to_all x8, waiting for transfers between devices, exchanged(): return lax.all_to_all(tiles, axis, split_axis=0, concat_axis=0, tiled=True)  16.2 us
    all_to_all x1, blocking collectives, collect(): lax.all_to_all(copies, axis, split_axis=0, concat_axis=0, tiled=True)  11.5 us
  transfers between devices with their start and end apart: 24, of which 14 were waited for; matrix products, arithmetic and copies ran while one was open for 8% of the time, Pallas kernels for 9%

profile of v1, /device:TPU:514, one launch (start us, length us, event | category | flops | bytes accessed | tf_op | source)
XLA Modules:
  0.0 263.5 jit_solution(2076957999533750374)
XLA Ops:
  4.9 22.7 %all-to-all-start = ((bf16[8,32,256]{2,1,0:T(8,128)(2,1)}), bf16[8,32,256]{2,1,0:T(8,128)(2,1)S(1)}, u32[]{:S(2)}, u32[]{:S(2)}) async-start(bf16[8,32,256]{2,1,0:T(8,128)(2,1)} %select_select_fusion), calls=%async_computation | async-start | bytes 262144 | tf_op jit(solution)/shard_map/all_to_all | solution.py:195
  29.7 2.0 gather_fusion.1
  31.9 3.4 %all-to-all-done = bf16[8,32,256]{2,1,0:T(8,128)(2,1)S(1)} async-done(((bf16[8,32,256]{2,1,0:T(8,128)(2,1)}), bf16[8,32,256]{2,1,0:T(8,128)(2,1)S(1)}, u32[]{:S(2)}, u32[]{:S(2)}) %all-to-all-start) | async-done | bytes 131104 | tf_op jit(solution)/shard_map/all_to_all | solution.py:195
  35.3 1.3 collective-permute-start
  37.6 5.4 %all-to-all-start.3 = ((bf16[8,64,256]{2,1,0:T(8,128)(2,1)}), bf16[8,64,256]{2,1,0:T(8,128)(2,1)}, u32[]{:S(2)}, u32[]{:S(2)}) async-start(bf16[8,64,256]{2,1,0:T(8,128)(2,1)} %bitcast.16), calls=%async_computation.3 | async-start | bytes 524288 | tf_op jit(solution)/shard_map/all_to_all | solution.py:195
  43.0 1.4 collective-permute-start.1
  45.7 3.1 %collective-permute-done.1 = bf16[32,256]{1,0:T(8,128)(2,1)S(1)} collective-permute-done((bf16[32,256]{1,0:T(8,128)(2,1)S(1)}, bf16[32,256]{1,0:T(8,128)(2,1)S(1)}, u32[]{:S(2)}, u32[]{:S(2)}) %collective-permute-start.1) | collective-permute-done | bytes 16416 | tf_op jit(solution)/shard_map/ppermute | solution.py:209
  48.8 1.3 collective-permute-start.2
  51.3 4.1 %collective-permute-done.2 = bf16[32,256]{1,0:T(8,128)(2,1)S(1)} collective-permute-done((bf16[32,256]{1,0:T(8,128)(2,1)S(1)}, bf16[32,256]{1,0:T(8,128)(2,1)S(1)}, u32[]{:S(2)}, u32[]{:S(2)}) %collective-permute-start.2) | collective-permute-done | bytes 16416 | tf_op jit(solution)/shard_map/ppermute | solution.py:209
  55.4 1.3 collective-permute-start.3
  58.7 1.6 copy-done.15
  62.5 2.4 collective-permute-done.3
  65.6 7.3 %all-to-all-start.1 = ((bf16[8,32,256]{2,1,0:T(8,128)(2,1)}), bf16[8,32,256]{2,1,0:T(8,128)(2,1)}, u32[]{:S(2)}, u32[]{:S(2)}) async-start(bf16[8,32,256]{2,1,0:T(8,128)(2,1)} %broadcast_in_dim.71), calls=%async_computation.1 | async-start | bytes 262144 | tf_op jit(solution)/shard_map/all_to_all | solution.py:216
  72.9 1.8 slice_bitcast_fusion.2
  77.1 6.3 %shard_map.147 = bf16[256,256]{1,0:T(8,128)(2,1)S(1)} custom-call(s32[1]{0:T(128)} %bitcast.27.flags_ref, bf16[256,256]{1,0:T(8,128)(2,1)S(1)} %get-tuple-element.9.stashed_ref, bf16[256,256]{1,0:T(8,128)(2,1)S(1)} %bitcast.86, bf16[256,256]{1,0:T(8,128)(2,1)S(1)} %bitcast.91, bf16[256,2048]{1,0:T(8,128)(2,1)S(1)} %bitcast.77, f32[1,2048]{1,0:T(1,128)S(1)} %copy-done.30, ...), custom_call_target="tpu_custom_call" | custom-call | tf_op jit(solution)/shard_map/pallas_call | solution.py:291
  85.1 1.3 collective-permute-start.4
  86.4 7.2 %all-to-all-start.8 = ((bf16[8,32,256]{2,1,0:T(8,128)(2,1)}), bf16[8,32,256]{2,1,0:T(8,128)(2,1)}, u32[]{:S(2)}, u32[]{:S(2)}) async-start(bf16[8,32,256]{2,1,0:T(8,128)(2,1)} %bitcast.94), calls=%async_computation.8 | async-start | bytes 262144 | tf_op jit(solution)/shard_map/all_to_all | solution.py:195
  97.0 3.2 %shard_map.141 = bf16[256,256]{1,0:T(8,128)(2,1)S(1)} custom-call(bf16[256,256]{1,0:T(8,128)(2,1)S(1)} %bitcast_select_fusion.coeffs_ref, bf16[256,2048]{1,0:T(8,128)(2,1)S(1)} %bitcast.78, f32[1,2048]{1,0:T(1,128)S(1)} %copy-done.30, bf16[2048,512]{1,0:T(8,128)(2,1)S(1)} %bitcast.71, bf16[2048,256]{1,0:T(8,128)(2,1)S(1)} %copy-done.10, ...), custom_call_target="tpu_custom_call" | custom-call | tf_op jit(solution)/shard_map/pallas_call | solution.py:288
  101.8 6.9 %all-to-all-start.2 = ((bf16[8,32,256]{2,1,0:T(8,128)(2,1)}), bf16[8,32,256]{2,1,0:T(8,128)(2,1)}, u32[]{:S(2)}, u32[]{:S(2)}) async-start(bf16[8,32,256]{2,1,0:T(8,128)(2,1)} %bitcast.92), calls=%async_computation.2 | async-start | bytes 262144 | tf_op jit(solution)/shard_map/all_to_all | solution.py:195
  109.5 1.3 collective-permute-start.5
  112.1 1.3 collective-permute-start.10
  113.4 1.9 collective-permute-done.5
  115.4 1.3 collective-permute-start.6
  117.4 4.7 %collective-permute-done.6 = bf16[2,32,256]{2,1,0:T(8,128)(2,1)S(1)} collective-permute-done((bf16[2,32,256]{2,1,0:T(8,128)(2,1)S(1)}, bf16[2,32,256]{2,1,0:T(8,128)(2,1)S(1)}, u32[]{:S(2)}, u32[]{:S(2)}) %collective-permute-start.6) | collective-permute-done | bytes 32800 | tf_op jit(solution)/shard_map/ppermute | solution.py:209
  125.2 1.9 collective-permute-start.8
  128.5 7.2 %all-to-all-start.9 = ((bf16[8,32,256]{2,1,0:T(8,128)(2,1)}), bf16[8,32,256]{2,1,0:T(8,128)(2,1)S(1)}, u32[]{:S(2)}, u32[]{:S(2)}) async-start(bf16[8,32,256]{2,1,0:T(8,128)(2,1)} %broadcast_in_dim.79), calls=%async_computation.9 | async-start | bytes 262144 | tf_op jit(solution)/shard_map/all_to_all | solution.py:216
  137.1 6.2 %all-to-all-done.9 = bf16[8,32,256]{2,1,0:T(8,128)(2,1)S(1)} async-done(((bf16[8,32,256]{2,1,0:T(8,128)(2,1)}), bf16[8,32,256]{2,1,0:T(8,128)(2,1)S(1)}, u32[]{:S(2)}, u32[]{:S(2)}) %all-to-all-start.9) | async-done | bytes 131104 | tf_op jit(solution)/shard_map/all_to_all | solution.py:216
  144.0 11.5 %all_to_all.65 = bf16[8,32,256]{2,1,0:T(8,128)(2,1)S(1)} all-to-all(bf16[8,32,256]{2,1,0:T(8,128)(2,1)S(1)} %broadcast_in_dim.76), channel_id=1, replica_groups=mesh['groups'=2,'segment'=16,'head'=8] {'head'}, dimensions={0} | all-to-all | bytes 262144 | tf_op jit(solution)/shard_map/all_to_all | solution.py:216
  159.8 6.3 %shard_map.149 = bf16[256,256]{1,0:T(8,128)(2,1)S(1)} custom-call(s32[1]{0:T(128)} %bitcast.27.flags_ref, bf16[256,256]{1,0:T(8,128)(2,1)S(1)} %copy-done.25, bf16[256,256]{1,0:T(8,128)(2,1)S(1)} %bitcast.84, bf16[256,256]{1,0:T(8,128)(2,1)S(1)} %bitcast.93, bf16[256,2048]{1,0:T(8,128)(2,1)S(1)} %bitcast.79, f32[1,2048]{1,0:T(1,128)S(1)} %copy-done.30, ...), custom_call_target="tpu_custom_call" | custom-call | tf_op jit(solution)/shard_map/pallas_call | solution.py:291
  166.7 5.3 %all-to-all-start.10 = ((bf16[8,32,256]{2,1,0:T(8,128)(2,1)}), bf16[8,32,256]{2,1,0:T(8,128)(2,1)}, u32[]{:S(2)}, u32[]{:S(2)}) async-start(bf16[8,32,256]{2,1,0:T(8,128)(2,1)} %bitcast.96), calls=%async_computation.10 | async-start | bytes 262144 | tf_op jit(solution)/shard_map/all_to_all | solution.py:195
  174.5 3.2 %shard_map.143 = bf16[256,256]{1,0:T(8,128)(2,1)S(1)} custom-call(bf16[256,256]{1,0:T(8,128)(2,1)S(1)} %bitcast.85, bf16[256,2048]{1,0:T(8,128)(2,1)S(1)} %bitcast.80, f32[1,2048]{1,0:T(1,128)S(1)} %copy-done.30, bf16[2048,512]{1,0:T(8,128)(2,1)S(1)} %bitcast.73, bf16[2048,256]{1,0:T(8,128)(2,1)S(1)} %copy-done.12, ...), custom_call_target="tpu_custom_call" | custom-call | tf_op jit(solution)/shard_map/pallas_call | solution.py:288
  178.4 1.5 all-to-all-done.10.parts_ref
  179.9 5.8 %all-to-all-start.5 = ((bf16[8,32,256]{2,1,0:T(8,128)(2,1)}), bf16[8,32,256]{2,1,0:T(8,128)(2,1)S(1)}, u32[]{:S(2)}, u32[]{:S(2)}) async-start(bf16[8,32,256]{2,1,0:T(8,128)(2,1)} %bitcast.95), calls=%async_computation.5 | async-start | bytes 262144 | tf_op jit(solution)/shard_map/all_to_all | solution.py:195
  185.7 1.9 shard_map.150
  188.8 4.5 %all-to-all-done.5.parts_ref = bf16[8,32,256]{2,1,0:T(8,128)(2,1)S(1)} async-done(((bf16[8,32,256]{2,1,0:T(8,128)(2,1)}), bf16[8,32,256]{2,1,0:T(8,128)(2,1)S(1)}, u32[]{:S(2)}, u32[]{:S(2)}) %all-to-all-start.5) | async-done | bytes 131104 | tf_op jit(solution)/shard_map/all_to_all | solution.py:195
  194.1 1.9 collective-permute-start.9
  198.0 4.7 %all-to-all-start.11 = ((bf16[8,32,256]{2,1,0:T(8,128)(2,1)}), bf16[8,32,256]{2,1,0:T(8,128)(2,1)S(1)}, u32[]{:S(2)}, u32[]{:S(2)}) async-start(bf16[8,32,256]{2,1,0:T(8,128)(2,1)} %broadcast_in_dim.80), calls=%async_computation.11 | async-start | bytes 262144 | tf_op jit(solution)/shard_map/all_to_all | solution.py:216
  203.5 7.0 %all-to-all-done.11 = bf16[8,32,256]{2,1,0:T(8,128)(2,1)S(1)} async-done(((bf16[8,32,256]{2,1,0:T(8,128)(2,1)}), bf16[8,32,256]{2,1,0:T(8,128)(2,1)S(1)}, u32[]{:S(2)}, u32[]{:S(2)}) %all-to-all-start.11) | async-done | bytes 131104 | tf_op jit(solution)/shard_map/all_to_all | solution.py:216
  211.2 4.7 %all-to-all-start.6 = ((bf16[8,32,256]{2,1,0:T(8,128)(2,1)}), bf16[8,32,256]{2,1,0:T(8,128)(2,1)S(1)}, u32[]{:S(2)}, u32[]{:S(2)}) async-start(bf16[8,32,256]{2,1,0:T(8,128)(2,1)} %broadcast_in_dim.77), calls=%async_computation.6 | async-start | bytes 262144 | tf_op jit(solution)/shard_map/all_to_all | solution.py:216
  216.0 7.6 %all-to-all-done.6 = bf16[8,32,256]{2,1,0:T(8,128)(2,1)S(1)} async-done(((bf16[8,32,256]{2,1,0:T(8,128)(2,1)}), bf16[8,32,256]{2,1,0:T(8,128)(2,1)S(1)}, u32[]{:S(2)}, u32[]{:S(2)}) %all-to-all-start.6) | async-done | bytes 131104 | tf_op jit(solution)/shard_map/all_to_all | solution.py:216
  227.8 6.8 %shard_map.151 = bf16[256,256]{1,0:T(8,128)(2,1)S(1)} custom-call(s32[2]{0:T(128)S(1)} %pad_add_fusion.flags_ref, bf16[256,256]{1,0:T(8,128)(2,1)S(1)} %copy-done.29, bf16[256,256]{1,0:T(8,128)(2,1)S(1)} %bitcast.87, bf16[256,256]{1,0:T(8,128)(2,1)S(1)} %bitcast.88, bf16[256,256]{1,0:T(8,128)(2,1)S(1)} %bitcast.97, bf16[256,2048]{1,0:T(8,128)(2,1)S(1)} %bitcast.81, ...), custom_call_target="tpu_custom_call" | custom-call | tf_op jit(solution)/shard_map/pallas_call | solution.py:291
  235.3 5.3 %all-to-all-start.12 = ((bf16[8,32,256]{2,1,0:T(8,128)(2,1)}), bf16[8,32,256]{2,1,0:T(8,128)(2,1)}, u32[]{:S(2)}, u32[]{:S(2)}) async-start(bf16[8,32,256]{2,1,0:T(8,128)(2,1)} %bitcast.98), calls=%async_computation.12 | async-start | bytes 262144 | tf_op jit(solution)/shard_map/all_to_all | solution.py:195
  243.1 3.9 %shard_map.145 = bf16[256,256]{1,0:T(8,128)(2,1)} custom-call(bf16[256,256]{1,0:T(8,128)(2,1)S(1)} %bitcast.89, bf16[256,2048]{1,0:T(8,128)(2,1)S(1)} %bitcast.82, f32[1,2048]{1,0:T(1,128)S(1)} %copy-done.30, bf16[2048,512]{1,0:T(8,128)(2,1)S(1)} %bitcast.75, bf16[2048,256]{1,0:T(8,128)(2,1)S(1)} %copy-done.14, ...), custom_call_target="tpu_custom_call" | custom-call | tf_op jit(solution)/shard_map/pallas_call | solution.py:288
  247.0 1.5 all-to-all-done.12.parts_ref
  248.5 5.8 %all-to-all-start.7 = ((bf16[8,32,256]{2,1,0:T(8,128)(2,1)}), bf16[8,32,256]{2,1,0:T(8,128)(2,1)S(1)}, u32[]{:S(2)}, u32[]{:S(2)}) async-start(bf16[8,32,256]{2,1,0:T(8,128)(2,1)} %bitcast.24), calls=%async_computation.7 | async-start | bytes 262144 | tf_op jit(solution)/shard_map/all_to_all | solution.py:195
  255.5 1.3 maximum_bitcast_fusion.1
  256.8 5.0 %all-to-all-done.7.parts_ref = bf16[8,32,256]{2,1,0:T(8,128)(2,1)S(1)} async-done(((bf16[8,32,256]{2,1,0:T(8,128)(2,1)}), bf16[8,32,256]{2,1,0:T(8,128)(2,1)S(1)}, u32[]{:S(2)}, u32[]{:S(2)}) %all-to-all-start.7) | async-done | bytes 131104 | tf_op jit(solution)/shard_map/all_to_all | solution.py:195
  262.1 1.4 maximum_bitcast_fusion
  (136 shorter events, 55.6 us)
Async XLA Ops:
  0.6 2.4 copy-start
  4.9 30.4 %all-to-all-start = ((bf16[8,32,256]{2,1,0:T(8,128)(2,1)}), bf16[8,32,256]{2,1,0:T(8,128)(2,1)S(1)}, u32[]{:S(2)}, u32[]{:S(2)}) async-start(bf16[8,32,256]{2,1,0:T(8,128)(2,1)} %select_select_fusion), calls=%async_computation | async-start | bytes 262144 | tf_op jit(solution)/shard_map/all_to_all | solution.py:195
  35.3 7.6 %collective-permute-start = (bf16[32,256]{1,0:T(8,128)(2,1)S(1)}, bf16[32,256]{1,0:T(8,128)(2,1)S(1)}, u32[]{:S(2)}, u32[]{:S(2)}) collective-permute-start(bf16[32,256]{1,0:T(8,128)(2,1)S(1)} %reduce_sum.26), channel_id=1, source_target_pairs={{8,0},{24,16},{40,32},{56,48},{72,64},{88,80},{104,96},{120,112},{... | collective-permute-start | bytes 49160 | tf_op jit(solution)/shard_map/ppermute | solution.py:209
  37.6 27.4 %all-to-all-start.3 = ((bf16[8,64,256]{2,1,0:T(8,128)(2,1)}), bf16[8,64,256]{2,1,0:T(8,128)(2,1)}, u32[]{:S(2)}, u32[]{:S(2)}) async-start(bf16[8,64,256]{2,1,0:T(8,128)(2,1)} %bitcast.16), calls=%async_computation.3 | async-start | bytes 524288 | tf_op jit(solution)/shard_map/all_to_all | solution.py:195
  43.0 13.7 %copy-start.32 = (bf16[3,256,256]{2,1,0:T(8,128)(2,1)S(1)}, bf16[3,256,256]{2,1,0:T(8,128)(2,1)}, u32[]{:S(2)}) copy-start(bf16[3,256,256]{2,1,0:T(8,128)(2,1)} %param.18) | copy-start | bytes 1179652
  43.0 13.7 %copy-start.33 = (bf16[1,256,256]{2,1,0:T(8,128)(2,1)S(1)}, bf16[1,256,256]{2,1,0:T(8,128)(2,1)}, u32[]{:S(2)}) copy-start(bf16[1,256,256]{2,1,0:T(8,128)(2,1)} %param.16) | copy-start | bytes 393220
  43.0 5.8 %collective-permute-start.1 = (bf16[32,256]{1,0:T(8,128)(2,1)S(1)}, bf16[32,256]{1,0:T(8,128)(2,1)S(1)}, u32[]{:S(2)}, u32[]{:S(2)}) collective-permute-start(bf16[32,256]{1,0:T(8,128)(2,1)S(1)} %add.77), channel_id=1, source_target_pairs={{16,0},{48,32},{80,64},{112,96},{17,1},{49,33},{81,65},{113,97},{1... | collective-permute-start | bytes 49160 | tf_op jit(solution)/shard_map/ppermute | solution.py:209
  48.8 6.6 %collective-permute-start.2 = (bf16[32,256]{1,0:T(8,128)(2,1)S(1)}, bf16[32,256]{1,0:T(8,128)(2,1)S(1)}, u32[]{:S(2)}, u32[]{:S(2)}) collective-permute-start(bf16[32,256]{1,0:T(8,128)(2,1)S(1)} %add.78), channel_id=1, source_target_pairs={{32,0},{96,64},{33,1},{97,65},{34,2},{98,66},{35,3},{99,67},{36,4}... | collective-permute-start | bytes 49160 | tf_op jit(solution)/shard_map/ppermute | solution.py:209
  55.4 9.6 %collective-permute-start.3 = (bf16[32,256]{1,0:T(8,128)(2,1)S(1)}, bf16[32,256]{1,0:T(8,128)(2,1)S(1)}, u32[]{:S(2)}, u32[]{:S(2)}) collective-permute-start(bf16[32,256]{1,0:T(8,128)(2,1)S(1)} %add.79), channel_id=1, source_target_pairs={{64,0},{65,1},{66,2},{67,3},{68,4},{69,5},{70,6},{71,7},{192,128},... | collective-permute-start | bytes 49160 | tf_op jit(solution)/shard_map/ppermute | solution.py:209
  57.5 1.2 copy-start.2
  58.7 1.6 copy-start.15
  60.3 1.2 copy-start.17
  61.5 13.1 %copy-start.1 = (bf16[1,2048,512]{2,1,0:T(8,128)(2,1)S(1)}, bf16[1,2048,512]{2,1,0:T(8,128)(2,1)}, u32[]{:S(2)}) copy-start(bf16[1,2048,512]{2,1,0:T(8,128)(2,1)} %param.22) | copy-start | bytes 6291460
  61.5 13.1 %copy-start.16 = (bf16[1,256,256]{2,1,0:T(8,128)(2,1)S(1)}, bf16[1,256,256]{2,1,0:T(8,128)(2,1)}, u32[]{:S(2)}) copy-start(bf16[1,256,256]{2,1,0:T(8,128)(2,1)} %param.15) | copy-start | bytes 393220
  61.5 13.1 %copy-start.30 = (f32[1,2048]{1,0:T(1,128)S(1)}, f32[1,2048]{1,0:T(1,128)}, u32[]{:S(2)}) copy-start(f32[1,2048]{1,0:T(1,128)} %refs_4_.1) | copy-start | bytes 24580
  65.6 20.8 %all-to-all-start.1 = ((bf16[8,32,256]{2,1,0:T(8,128)(2,1)}), bf16[8,32,256]{2,1,0:T(8,128)(2,1)}, u32[]{:S(2)}, u32[]{:S(2)}) async-start(bf16[8,32,256]{2,1,0:T(8,128)(2,1)} %broadcast_in_dim.71), calls=%async_computation.1 | async-start | bytes 262144 | tf_op jit(solution)/shard_map/all_to_all | solution.py:216
  74.7 1.2 copy-start.3
  75.9 1.2 copy-start.9
  85.1 23.7 %collective-permute-start.4 = (bf16[2,32,256]{2,1,0:T(8,128)(2,1)S(1)}, bf16[2,32,256]{2,1,0:T(8,128)(2,1)}, u32[]{:S(2)}, u32[]{:S(2)}) collective-permute-start(bf16[2,32,256]{2,1,0:T(8,128)(2,1)S(1)} %bitcast.105), channel_id=1, source_target_pairs={{8,0},{24,16},{40,32},{56,48},{72,64},{88,80},{104,96},{120,112},{... | collective-permute-start | bytes 98312 | tf_op jit(solution)/shard_map/ppermute | solution.py:209
  86.4 15.4 %all-to-all-start.8 = ((bf16[8,32,256]{2,1,0:T(8,128)(2,1)}), bf16[8,32,256]{2,1,0:T(8,128)(2,1)}, u32[]{:S(2)}, u32[]{:S(2)}) async-start(bf16[8,32,256]{2,1,0:T(8,128)(2,1)} %bitcast.94), calls=%async_computation.8 | async-start | bytes 262144 | tf_op jit(solution)/shard_map/all_to_all | solution.py:195
  94.6 1.2 copy-start.4
  95.8 1.2 copy-start.10
  101.8 22.2 %all-to-all-start.2 = ((bf16[8,32,256]{2,1,0:T(8,128)(2,1)}), bf16[8,32,256]{2,1,0:T(8,128)(2,1)}, u32[]{:S(2)}, u32[]{:S(2)}) async-start(bf16[8,32,256]{2,1,0:T(8,128)(2,1)} %bitcast.92), calls=%async_computation.2 | async-start | bytes 262144 | tf_op jit(solution)/shard_map/all_to_all | solution.py:195
  109.5 5.8 %collective-permute-start.5 = (bf16[2,32,256]{2,1,0:T(8,128)(2,1)S(1)}, bf16[2,32,256]{2,1,0:T(8,128)(2,1)S(1)}, u32[]{:S(2)}, u32[]{:S(2)}) collective-permute-start(bf16[2,32,256]{2,1,0:T(8,128)(2,1)S(1)} %add.85), channel_id=1, source_target_pairs={{16,0},{48,32},{80,64},{112,96},{17,1},{49,33},{81,65},{113,97},{1... | collective-permute-start | bytes 98312 | tf_op jit(solution)/shard_map/ppermute | solution.py:209
  112.1 15.0 %collective-permute-start.10 = (bf16[32,256]{1,0:T(8,128)(2,1)S(1)}, bf16[32,256]{1,0:T(8,128)(2,1)S(1)}, u32[]{:S(2)}, u32[]{:S(2)}) collective-permute-start(bf16[32,256]{1,0:T(8,128)(2,1)S(1)} %shard_map.148), channel_id=1, source_target_pairs={{8,0},{16,8},{24,16},{32,24},{40,32},{48,40},{56,48},{64,56},{72,6... | collective-permute-start | bytes 49160 | tf_op jit(solution)/shard_map/ppermute | solution.py:201
  115.4 6.7 %collective-permute-start.6 = (bf16[2,32,256]{2,1,0:T(8,128)(2,1)S(1)}, bf16[2,32,256]{2,1,0:T(8,128)(2,1)S(1)}, u32[]{:S(2)}, u32[]{:S(2)}) collective-permute-start(bf16[2,32,256]{2,1,0:T(8,128)(2,1)S(1)} %add.86), channel_id=1, source_target_pairs={{32,0},{96,64},{33,1},{97,65},{34,2},{98,66},{35,3},{99,67},{36,4}... | collective-permute-start | bytes 98312 | tf_op jit(solution)/shard_map/ppermute | solution.py:209
  122.7 13.0 %collective-permute-start.7 = (bf16[2,32,256]{2,1,0:T(8,128)(2,1)}, bf16[2,32,256]{2,1,0:T(8,128)(2,1)}, u32[]{:S(2)}, u32[]{:S(2)}) collective-permute-start(bf16[2,32,256]{2,1,0:T(8,128)(2,1)} %add.87), channel_id=1, source_target_pairs={{64,0},{65,1},{66,2},{67,3},{68,4},{69,5},{70,6},{71,7},{192,128},... | collective-permute-start | bytes 98312 | tf_op jit(solution)/shard_map/ppermute | solution.py:209
  125.2 11.3 %copy-start.31 = (bf16[32,256]{1,0:T(8,128)(2,1)}, bf16[32,256]{1,0:T(8,128)(2,1)S(1)}, u32[]{:S(2)}) copy-start(bf16[32,256]{1,0:T(8,128)(2,1)S(1)} %shard_map.142) | copy-start | bytes 49156
  125.2 11.3 %collective-permute-start.8 = (bf16[32,256]{1,0:T(8,128)(2,1)S(1)}, bf16[32,256]{1,0:T(8,128)(2,1)}, u32[]{:S(2)}, u32[]{:S(2)}) collective-permute-start(bf16[32,256]{1,0:T(8,128)(2,1)S(1)} %shard_map.142), channel_id=1, source_target_pairs={{0,8},{8,16},{16,24},{24,32},{32,40},{40,48},{48,56},{56,64},{64,7... | collective-permute-start | bytes 49160 | tf_op jit(solution)/shard_map/ppermute | solution.py:201
  128.5 14.8 %all-to-all-start.9 = ((bf16[8,32,256]{2,1,0:T(8,128)(2,1)}), bf16[8,32,256]{2,1,0:T(8,128)(2,1)S(1)}, u32[]{:S(2)}, u32[]{:S(2)}) async-start(bf16[8,32,256]{2,1,0:T(8,128)(2,1)} %broadcast_in_dim.79), calls=%async_computation.9 | async-start | bytes 262144 | tf_op jit(solution)/shard_map/all_to_all | solution.py:216
  155.5 1.2 copy-start.5
  156.8 1.2 copy-start.11
  158.0 0.9 copy-start.21
  158.9 0.9 copy-start.25
  166.7 13.1 %all-to-all-start.10 = ((bf16[8,32,256]{2,1,0:T(8,128)(2,1)}), bf16[8,32,256]{2,1,0:T(8,128)(2,1)}, u32[]{:S(2)}, u32[]{:S(2)}) async-start(bf16[8,32,256]{2,1,0:T(8,128)(2,1)} %bitcast.96), calls=%async_computation.10 | async-start | bytes 262144 | tf_op jit(solution)/shard_map/all_to_all | solution.py:195
  172.1 1.2 copy-start.6
  173.3 1.2 copy-start.12
  179.9 13.4 %all-to-all-start.5 = ((bf16[8,32,256]{2,1,0:T(8,128)(2,1)}), bf16[8,32,256]{2,1,0:T(8,128)(2,1)S(1)}, u32[]{:S(2)}, u32[]{:S(2)}) async-start(bf16[8,32,256]{2,1,0:T(8,128)(2,1)} %bitcast.95), calls=%async_computation.5 | async-start | bytes 262144 | tf_op jit(solution)/shard_map/all_to_all | solution.py:195
  187.5 8.5 %collective-permute-start.11 = (bf16[32,256]{1,0:T(8,128)(2,1)}, bf16[32,256]{1,0:T(8,128)(2,1)S(1)}, u32[]{:S(2)}, u32[]{:S(2)}) collective-permute-start(bf16[32,256]{1,0:T(8,128)(2,1)} %shard_map.150), channel_id=1, source_target_pairs={{8,0},{16,8},{24,16},{32,24},{40,32},{48,40},{56,48},{64,56},{72,6... | collective-permute-start | bytes 49160 | tf_op jit(solution)/shard_map/ppermute | solution.py:201
  194.1 8.7 %collective-permute-start.9 = (bf16[32,256]{1,0:T(8,128)(2,1)}, bf16[32,256]{1,0:T(8,128)(2,1)}, u32[]{:S(2)}, u32[]{:S(2)}) collective-permute-start(bf16[32,256]{1,0:T(8,128)(2,1)} %shard_map.144), channel_id=1, source_target_pairs={{0,8},{8,16},{16,24},{24,32},{32,40},{40,48},{48,56},{56,64},{64,7... | collective-permute-start | bytes 49160 | tf_op jit(solution)/shard_map/ppermute | solution.py:201
  198.0 12.4 %all-to-all-start.11 = ((bf16[8,32,256]{2,1,0:T(8,128)(2,1)}), bf16[8,32,256]{2,1,0:T(8,128)(2,1)S(1)}, u32[]{:S(2)}, u32[]{:S(2)}) async-start(bf16[8,32,256]{2,1,0:T(8,128)(2,1)} %broadcast_in_dim.80), calls=%async_computation.11 | async-start | bytes 262144 | tf_op jit(solution)/shard_map/all_to_all | solution.py:216
  211.2 12.4 %all-to-all-start.6 = ((bf16[8,32,256]{2,1,0:T(8,128)(2,1)}), bf16[8,32,256]{2,1,0:T(8,128)(2,1)S(1)}, u32[]{:S(2)}, u32[]{:S(2)}) async-start(bf16[8,32,256]{2,1,0:T(8,128)(2,1)} %broadcast_in_dim.77), calls=%async_computation.6 | async-start | bytes 262144 | tf_op jit(solution)/shard_map/all_to_all | solution.py:216
  223.6 1.2 copy-start.7
  224.8 1.2 copy-start.13
  235.3 13.1 %all-to-all-start.12 = ((bf16[8,32,256]{2,1,0:T(8,128)(2,1)}), bf16[8,32,256]{2,1,0:T(8,128)(2,1)}, u32[]{:S(2)}, u32[]{:S(2)}) async-start(bf16[8,32,256]{2,1,0:T(8,128)(2,1)} %bitcast.98), calls=%async_computation.12 | async-start | bytes 262144 | tf_op jit(solution)/shard_map/all_to_all | solution.py:195
  240.7 1.2 copy-start.8
  241.9 1.2 copy-start.14
  248.5 13.4 %all-to-all-start.7 = ((bf16[8,32,256]{2,1,0:T(8,128)(2,1)}), bf16[8,32,256]{2,1,0:T(8,128)(2,1)S(1)}, u32[]{:S(2)}, u32[]{:S(2)}) async-start(bf16[8,32,256]{2,1,0:T(8,128)(2,1)} %bitcast.24), calls=%async_computation.7 | async-start | bytes 262144 | tf_op jit(solution)/shard_map/all_to_all | solution.py:195
  (12 other events, 8.3 us)

commit v2 on v1

v2 whole, which is shorter than its diff:
```python
import functools
import math

import jax
import jax.numpy as jnp
from jax import lax
from jax.experimental import pallas as pl
from jax.experimental.pallas import tpu as pltpu
from jax.sharding import PartitionSpec as P

QUERY_HEADS = 32
KEY_VALUE_HEADS = 4
HEAD_SIZE = 128

EPS = 1e-06
CHUNK = 512
LANES = 128
LOW = jnp.bfloat16
WIDE = jnp.float32

VMEM = pl.BlockSpec(memory_space=pltpu.VMEM)
SMEM = pl.BlockSpec(memory_space=pltpu.SMEM)
HBM = pl.BlockSpec(memory_space=pltpu.HBM)


def dot(former, latter):
    return jnp.dot(former, latter, preferred_element_type=WIDE)


def dot_back(former, latter):
    return lax.dot_general(former, latter, (((1,), (1,)), ((), ())), preferred_element_type=WIDE)


def dot_turned(former, latter):
    return lax.dot_general(former, latter, (((0,), (0,)), ((), ())), preferred_element_type=WIDE)


def rms_scale(matrix):
    return lax.rsqrt(jnp.mean(matrix * matrix, axis=-1, keepdims=True) + EPS)


def norm_back(upstream_in, grad_hat):
    scaling = rms_scale(upstream_in)
    return scaling * grad_hat - upstream_in * scaling**3 * jnp.mean(
        grad_hat * upstream_in, axis=-1, keepdims=True
    )


def looped(count, body, carry, rolled):
    if rolled:
        return lax.fori_loop(0, count, body, carry)
    for place in range(count):
        carry = body(place, carry)
    return carry


def block(place, length):
    at = place * length
    return pl.ds(at if isinstance(at, int) else pl.multiple_of(at, length), length)


class Weights:
    def __init__(self, where_ref, hbm, vmem, sems):
        expand, query, key, value, folded = hbm
        self.expand, self.query, self.kv, self.folded = vmem
        first = pl.multiple_of(where_ref[1], HEAD_SIZE)
        self.count = self.expand.shape[0]
        copies = []
        for place in range(self.count):
            copies.append((expand.at[:, block(place, CHUNK)], self.expand.at[place]))
        copies.append((key.at[:, pl.ds(first, HEAD_SIZE)], self.kv.at[:, pl.ds(0, HEAD_SIZE)]))
        copies.append(
            (value.at[:, pl.ds(first, HEAD_SIZE)], self.kv.at[:, pl.ds(HEAD_SIZE, HEAD_SIZE)])
        )
        for place in range(self.count):
            copies.append((query.at[block(place, CHUNK), :], self.query.at[place]))
        copies.append((folded, self.folded))
        self.copies = [
            pltpu.make_async_copy(source, target, sems.at[place])
            for place, (source, target) in enumerate(copies)
        ]

    def start(self):
        for copy in self.copies:
            copy.start()

    def wait(self, first=0, last=None):
        for copy in self.copies[first:last]:
            copy.wait()


def weight_scratch(width, rank, queries):
    count = width // CHUNK
    return [
        pltpu.VMEM((count, rank, CHUNK), LOW),
        pltpu.VMEM((count, CHUNK, queries), LOW),
        pltpu.VMEM((width, 2 * HEAD_SIZE), LOW),
        pltpu.VMEM((queries, rank), LOW),
        pltpu.SemaphoreType.DMA((2 * count + 3,)),
    ]


STATE = 6


def state_shapes(span, width, queries):
    heads = queries // HEAD_SIZE
    return [
        ((width // CHUNK, span, CHUNK), WIDE),
        ((span, LANES), WIDE),
        ((heads, span, HEAD_SIZE), WIDE),
        ((span, HEAD_SIZE), WIDE),
        ((span, HEAD_SIZE), LOW),
        ((heads, span, span), WIDE),
    ]


def spread(coeffs, weights, gain_ref, state, rolled):
    hidden, scale, queries, keys, values, _ = state
    count = weights.count
    span = coeffs.shape[0]
    if rolled:
        weights.wait()

    def first(place, squares):
        if not rolled:
            weights.wait(place, place + 1)
        part = dot(coeffs, weights.expand[place])
        hidden[place] = part
        return squares + jnp.sum(part * part, axis=-1, keepdims=True)

    squares = looped(count, first, jnp.zeros((span, 1), WIDE), rolled)
    scaling = lax.rsqrt(squares / (count * CHUNK) + EPS)
    scale[...] = jnp.broadcast_to(scaling, scale.shape)
    if not rolled:
        weights.wait(count, count + 2)

    def second(place, carry):
        wide_q, wide_kv = carry
        if not rolled:
            weights.wait(count + 2 + place, count + 3 + place)
        normed = (hidden[place] * scaling * gain_ref[place]).astype(LOW)
        return (
            wide_q + dot(normed, weights.query[place]),
            wide_kv + dot(normed, weights.kv[block(place, CHUNK), :]),
        )

    heads = queries.shape[0]
    wide_q, wide_kv = looped(
        count,
        second,
        (
            jnp.zeros((span, heads * HEAD_SIZE), WIDE),
            jnp.zeros((span, 2 * HEAD_SIZE), WIDE),
        ),
        rolled,
    )
    for head in range(heads):
        queries[head] = wide_q[:, head * HEAD_SIZE : (head + 1) * HEAD_SIZE]
    keys[...] = wide_kv[:, :HEAD_SIZE]
    values[...] = wide_kv[:, HEAD_SIZE:].astype(LOW)


def hat(matrix):
    return (matrix * rms_scale(matrix)).astype(LOW)


def probabilities(q_hat, k_hat):
    rows = q_hat.shape[0]
    scores = dot_back(q_hat, k_hat) * (1.0 / math.sqrt(HEAD_SIZE))
    column = lax.broadcasted_iota(jnp.int32, (rows, rows), 1)
    row = lax.broadcasted_iota(jnp.int32, (rows, rows), 0)
    weights = jnp.where(column <= row, jnp.exp(scores), 0.0)
    return weights / jnp.sum(weights, axis=-1, keepdims=True)


def attend(weights, state, keep, rolled):
    _, _, queries, keys, values, probs = state
    k_hat = hat(keys[...])
    if not rolled:
        weights.wait(len(weights.copies) - 1)

    def one(head, total):
        chances = probabilities(hat(queries[head]), k_hat)
        if keep:
            probs[head] = chances
        if total is None:
            return None
        attended = dot(chances.astype(LOW), values[...]).astype(LOW)
        return total + dot(attended, weights.folded[block(head, HEAD_SIZE), :])

    span = keys.shape[0]
    start = jnp.zeros((span, weights.folded.shape[1]), WIDE)
    return looped(queries.shape[0], one, start, rolled)


def keep_probabilities(state, rolled):
    _, _, queries, keys, _, probs = state
    k_hat = hat(keys[...])

    def one(head, carry):
        probs[head] = probabilities(hat(queries[head]), k_hat)
        return carry

    looped(queries.shape[0], one, 0, rolled)


def go_back(grads, weights, gain_ref, state, grad_q, weighted_ref, rolled):
    hidden, scale, queries, keys, values, probs = state
    keys_here = keys[...]
    k_hat = hat(keys_here)
    values_here = values[...]

    def one(head, carry):
        grad_khat, grad_values = carry
        upstream = queries[head]
        q_hat = hat(upstream)
        chances = probs[head]
        grad_attended = dot_back(grads, weights.folded[block(head, HEAD_SIZE), :]).astype(LOW)
        grad_chances = dot_back(grad_attended, values_here)
        inner = jnp.sum(grad_chances * chances, axis=-1, keepdims=True)
        grad_scores = chances * (grad_chances - inner) * (1.0 / math.sqrt(HEAD_SIZE))
        grad_scores = grad_scores.astype(LOW)
        grad_q[:, block(head, HEAD_SIZE)] = norm_back(upstream, dot(grad_scores, k_hat)).astype(LOW)
        return (
            grad_khat + dot_turned(grad_scores, q_hat),
            grad_values + dot_turned(chances.astype(LOW), grad_attended),
        )

    empty = jnp.zeros(keys_here.shape, WIDE)
    grad_khat, grad_values = looped(queries.shape[0], one, (empty, empty), rolled)
    grad_kv = jnp.concatenate(
        [norm_back(keys_here, grad_khat).astype(LOW), grad_values.astype(LOW)], axis=1
    )
    scaling = scale[:, :1]

    def third(place, inner):
        grad_normed = dot_back(grad_q[...], weights.query[place]) + dot_back(
            grad_kv, weights.kv[block(place, CHUNK), :]
        )
        weighted = grad_normed * gain_ref[place]
        weighted_ref[place] = weighted
        return inner + jnp.sum(weighted * hidden[place], axis=-1, keepdims=True)

    inner = looped(weights.count, third, jnp.zeros((keys_here.shape[0], 1), WIDE), rolled)
    factor = scaling**3 * (inner / (weights.count * CHUNK))

    def fourth(place, total):
        grad_hidden = scaling * weighted_ref[place] - hidden[place] * factor
        return total + dot_back(grad_hidden.astype(LOW), weights.expand[place])

    return looped(weights.count, fourth, jnp.zeros(grads.shape, WIDE), rolled)


def direct_of(rows, basis_ref, back):
    return lax.dot_general(
        rows.astype(WIDE),
        basis_ref[...],
        (((1,), (1 if back else 0,)), ((), ())),
        precision=lax.Precision.HIGHEST,
        preferred_element_type=WIDE,
    )


def own_rows(ref, where_ref, share):
    return ref[pl.ds(pl.multiple_of(where_ref[0], share), share), :]


def put_tiles(payload_ref, total, at):
    share = payload_ref.shape[1] // 2
    for place in range(payload_ref.shape[0]):
        payload_ref[place, pl.ds(at, share), :] = total[place * share : (place + 1) * share].astype(
            LOW
        )


def state_kernel(where_ref, gain_ref, plain_ref, other_ref, *refs):
    hbm, outs, scratch = refs[:5], refs[5 : 5 + STATE], refs[5 + STATE :]
    weights = Weights(where_ref, hbm, scratch[:4], scratch[4])
    weights.start()
    coeffs = jnp.where(where_ref[2] != 0, other_ref[...], plain_ref[...])
    spread(coeffs, weights, gain_ref, outs, True)
    keep_probabilities(outs, True)


def first_back_kernel(where_ref, gain_ref, basis_ref, plain_ref, other_ref, grads_ref, *refs):
    hbm, outs, scratch = refs[:5], refs[5:7], refs[7:]
    weights = Weights(where_ref, hbm, scratch[:4], scratch[4])
    weights.start()
    grad_q, weighted, *state = scratch[5:]
    coeffs = jnp.where(where_ref[2] != 0, other_ref[...], plain_ref[...])
    spread(coeffs, weights, gain_ref, state, True)
    keep_probabilities(state, True)
    out_ref, direct_ref = outs
    total = go_back(grads_ref[...], weights, gain_ref, state, grad_q, weighted, True)
    out_ref[...] = total.astype(LOW)
    direct_ref[...] = direct_of(own_rows(grads_ref, where_ref, direct_ref.shape[0]), basis_ref, True)


def first_forward_kernel(where_ref, gain_ref, basis_ref, rows_ref, arriving_ref, back_ref, *refs):
    hbm, outs, scratch = refs[:5], refs[5:7], refs[7:]
    weights = Weights(where_ref, hbm, scratch[:4], scratch[4])
    weights.start()
    coeffs_ref, *state = scratch[5:]
    share = rows_ref.shape[1]
    for place in range(rows_ref.shape[0]):
        here = pl.ds(place * share, share)
        coeffs_ref[here, :] = jnp.where(where_ref[2] != 0, rows_ref[place], arriving_ref[here, :])
    payload_ref, direct_ref = outs
    direct_ref[...] = direct_of(own_rows(coeffs_ref, where_ref, share), basis_ref, False)
    spread(coeffs_ref[...], weights, gain_ref, [*state, None], False)
    put_tiles(payload_ref, attend(weights, [*state, None], False, False), 0)
    put_tiles(payload_ref, back_ref[...], share)


def both_kernel(where_ref, gain_ref, basis_ref, rows_ref, *refs):
    kept, hbm, outs, scratch = refs[:STATE], refs[STATE : STATE + 5], refs[STATE + 5 : STATE + 8], refs[STATE + 8 :]
    weights = Weights(where_ref, hbm, scratch[:4], scratch[4])
    weights.start()
    kept_sems, coeffs_ref, grads_ref, grad_q, weighted, *state = scratch[5:]
    copies = [
        pltpu.make_async_copy(source, target.at[1], kept_sems.at[place])
        for place, (source, target) in enumerate(zip(kept, state))
    ]
    for copy in copies:
        copy.start()
    payload_ref, direct_ref, direct_back_ref = outs
    share = rows_ref.shape[1] // 2
    for place in range(rows_ref.shape[0]):
        here = pl.ds(place * share, share)
        coeffs_ref[here, :] = rows_ref[place, pl.ds(0, share), :]
        grads_ref[here, :] = rows_ref[place, pl.ds(share, share), :]
    direct_ref[...] = direct_of(own_rows(coeffs_ref, where_ref, share), basis_ref, False)
    direct_back_ref[...] = direct_of(own_rows(grads_ref, where_ref, share), basis_ref, True)
    mine = [ref.at[0] for ref in state]
    spread(coeffs_ref[...], weights, gain_ref, mine, False)
    put_tiles(payload_ref, attend(weights, mine, True, False), 0)
    for copy in copies:
        copy.wait()
    slot = jnp.where(where_ref[3] != 0, 0, 1)
    chosen = [ref.at[slot] for ref in state]
    total = go_back(grads_ref[...], weights, gain_ref, chosen, grad_q, weighted, False)
    put_tiles(payload_ref, total, share)


def fold_kernel(expand_ref, compress_ref, out_weight_ref, basis_ref, folded_ref):
    basis_ref[...] = dot(expand_ref[...], compress_ref[...])
    folded_ref[...] = dot(out_weight_ref[...], compress_ref[...]).astype(folded_ref.dtype)


def finish_kernel(parts_ref, direct_ref, direct_back_ref, out_ref, out_back_ref):
    share = direct_ref.shape[0]
    for at, direct, out in ((0, direct_ref, out_ref), (share, direct_back_ref, out_back_ref)):
        summed = parts_ref[0, pl.ds(at, share), :].astype(WIDE)
        for place in range(1, parts_ref.shape[0]):
            summed += parts_ref[place, pl.ds(at, share), :].astype(WIDE)
        out[...] = (summed + direct[...]).astype(LOW)


def last_kernel(count, parts_ref, direct_ref, direct_back_ref, *refs):
    share = direct_ref.shape[0]
    before, out_ref, out_back_ref = refs[: 2 * count], refs[2 * count], refs[2 * count + 1]
    for place in range(count):
        out_ref[0, place] = before[place][...]
        out_back_ref[0, place] = before[count + place][...]
    finish_kernel(
        parts_ref, direct_ref, direct_back_ref, out_ref.at[0, count], out_back_ref.at[0, count]
    )


def mix_kernel(tick, where_ref, got_ref, got_back_ref, later_ref, seed_ref, out_ref):
    share = got_ref.shape[0]
    rows = jnp.where(where_ref[4] != 0, later_ref[pl.ds((tick + 1) * share, share), :], got_ref[...])
    seeds = own_rows(seed_ref.at[tick + 1], where_ref, share)
    rows_back = jnp.where(where_ref[5] != 0, seeds, got_back_ref[...])
    for place in range(out_ref.shape[0]):
        out_ref[place, pl.ds(0, share), :] = rows
        out_ref[place, pl.ds(share, share), :] = rows_back


def shape_of(dims, kind):
    return jax.ShapeDtypeStruct(dims, kind)


def call(body, outs, specs, scratch=(), flops=0):
    return pl.pallas_call(
        body,
        out_shape=outs,
        in_specs=specs,
        out_specs=jax.tree.map(lambda _: VMEM, outs),
        scratch_shapes=list(scratch),
        cost_estimate=pl.CostEstimate(flops=flops, bytes_accessed=2**20, transcendentals=0),
        compiler_params=pltpu.CompilerParams(vmem_limit_bytes=40 * 2**20),
    )


def exchanged(tiles, axis):
    return lax.all_to_all(tiles, axis, split_axis=0, concat_axis=0, tiled=True)


def passed_along(x, axis, by):
    length = lax.axis_size(axis)
    pairs = [(i, i + by) for i in range(length) if 0 <= i + by < length]
    return lax.ppermute(x, axis, pairs)


def brought_to_first(x, axis, radix):
    length = lax.axis_size(axis)
    step = 1
    while step < length:
        got = []
        for times in range(1, radix):
            pairs = [
                (i + times * step, i)
                for i in range(0, length, radix * step)
                if i + times * step < length
            ]
            if pairs:
                got.append(lax.ppermute(x, axis, pairs))
        for other in got:
            x = x + other
        step *= radix
    return x


def picked_rows(ids, first_row, table, parts, share):
    ticks = ids.shape[0]
    local = ids.reshape(ticks, parts, share).swapaxes(0, 1).reshape(-1) - first_row
    inside = (local >= 0) & (local < table.shape[0])
    looked = jnp.take(table, local, axis=0, mode="clip")
    looked = jnp.where(inside[:, None], looked, jnp.zeros((), looked.dtype))
    return looked.reshape(parts, ticks * share, -1)


def shards(
    token_ids,
    embed_table,
    arriving,
    returning,
    stashed,
    seed_grad,
    expand,
    compress,
    norm_gain,
    w_query,
    key_weight,
    value_weight,
    w_out,
):
    segment_index = lax.axis_index("segment")
    last_segment = lax.axis_size("segment") - 1
    head_index = lax.axis_index("head")
    parts = lax.axis_size("head")
    ticks, span = token_ids.shape
    rank = embed_table.shape[1]
    width = expand.shape[2]
    queries = w_query.shape[2]
    share = span // parts

    heads_here = queries // HEAD_SIZE
    query_group_size = QUERY_HEADS // KEY_VALUE_HEADS
    first_kv = head_index * heads_here // query_group_size * HEAD_SIZE
    delay = 2 * (last_segment - segment_index)

    def where(*flags):
        entries = [head_index * share, first_kv, *flags]
        return jnp.stack([jnp.asarray(entry, jnp.int32) for entry in entries])

    first_row = lax.axis_index(("segment", "head")) * embed_table.shape[0]
    tiles = exchanged(picked_rows(token_ids, first_row, embed_table, parts, share), "head")
    rows = brought_to_first(tiles.sum(axis=0), "segment", 4)
    embedded = exchanged(jnp.broadcast_to(rows[:share], (parts, share, rank)), "head")

    gain = norm_gain.reshape(-1, 1, CHUNK)
    square = shape_of((span, rank), LOW)
    payload = shape_of((parts, 2 * share, rank), LOW)
    piece = shape_of((share, rank), LOW)
    wide_piece = shape_of((share, rank), WIDE)
    basis, folded = call(
        fold_kernel,
        (shape_of((rank, rank), WIDE), shape_of((queries, rank), LOW)),
        [VMEM] * 3,
        flops=2 * (rank + queries) * width * rank,
    )(expand[0], compress[0], w_out[0])
    weights = (expand[0], w_query[0], key_weight[0], value_weight[0], folded)
    base = weight_scratch(width, rank, queries)
    states = state_shapes(span, width, queries)
    bits = pltpu.VMEM((span, queries), LOW)
    weighted = pltpu.VMEM((width // CHUNK, span, CHUNK), WIDE)
    lines = pltpu.VMEM((span, rank), LOW)
    work = 2 * span * width * (rank + queries + 2 * HEAD_SIZE)

    def kept_of(tick):
        return call(
            state_kernel,
            [shape_of(*entry) for entry in states],
            [SMEM] + [VMEM] * 3 + [HBM] * 5,
            base,
            flops=work,
        )(
            where(jnp.where((delay == tick) & (tick > 0), 1, 0)),
            gain,
            stashed[0, tick],
            arriving[0],
            *weights,
        )

    is_last = jnp.where(segment_index == last_segment, 1, 0)
    is_first = jnp.where(segment_index == 0, 1, 0)
    backward_in = jnp.where(is_last != 0, seed_grad[0], returning[0])
    back, direct_back = call(
        first_back_kernel,
        (square, wide_piece),
        [SMEM] + [VMEM] * 5 + [HBM] * 5,
        [*base, bits, weighted] + [pltpu.VMEM(*entry) for entry in states],
        flops=2 * work,
    )(where(is_last), gain, basis, stashed[0, 0], arriving[0], backward_in, *weights)
    kept = [kept_of(tick) for tick in range(1, ticks)]

    out, direct = call(
        first_forward_kernel,
        (payload, wide_piece),
        [SMEM] + [VMEM] * 5 + [HBM] * 5,
        [*base, lines] + [pltpu.VMEM(*entry) for entry in states[:-1]],
        flops=work,
    )(where(is_first), gain, basis, embedded, arriving[0], back, *weights)

    flags = where(0, is_last, is_first, is_last)
    shares = []
    for tick in range(ticks):
        arrived = exchanged(out, "head")
        if tick + 1 == ticks:
            break
        sent, sent_back = call(finish_kernel, (piece, piece), [VMEM] * 3)(
            arrived, direct, direct_back
        )
        shares.append((sent, sent_back))
        mixed = call(functools.partial(mix_kernel, tick), payload, [SMEM] + [VMEM] * 4)(
            flags,
            passed_along(sent, "segment", 1),
            passed_along(sent_back, "segment", -1),
            rows,
            seed_grad,
        )
        out, direct, direct_back = call(
            both_kernel,
            (payload, wide_piece, wide_piece),
            [SMEM] + [VMEM] * 3 + [HBM] * (STATE + 5),
            [*base, pltpu.SemaphoreType.DMA((STATE,)), lines, lines, bits, weighted]
            + [pltpu.VMEM((2, *dims), kind) for dims, kind in states],
            flops=2 * work,
        )(flags, gain, basis, exchanged(mixed, "head"), *kept[tick], *weights)
    whole = shape_of((1, ticks, share, rank), LOW)
    return call(functools.partial(last_kernel, ticks - 1), (whole, whole), [VMEM] * (3 + 2 * (ticks - 1)))(
        arrived, direct, direct_back, *[pair[0] for pair in shares], *[pair[1] for pair in shares]
    )


def solution(mesh):
    return jax.shard_map(
        shards,
        mesh=mesh,
        in_specs=(
            P("groups", None),
            P(("segment", "head"), None),
            P(("groups", "segment"), None, None),
            P(("groups", "segment"), None, None),
            P(("groups", "segment"), None, None, None),
            P("groups", None, None),
            P("segment", None, None),
            P("segment", None, None),
            P("segment", None),
            P("segment", None, "head"),
            P("segment", None, None),
            P("segment", None, None),
            P("segment", "head", None),
        ),
        out_specs=(
            P(("groups", "segment"), None, "head", None),
            P(("groups", "segment"), None, "head", None),
        ),
        check_vma=False,
    )
```

time: 266 us -> 256 us (0.962)
  starting transfers between devices: 105 us -> 52.6 us
  blocking collectives: 11.5 us -> 52.3 us
  waiting for transfers between devices: 53.3 us -> 21.4 us
  local copies, waits for them, and re-layouts: 38 us -> 64.5 us
  Pallas kernels: 37.1 us -> 56.3 us
  other arithmetic: 17.1 us -> 3.96 us
    all_to_all x1 -> x3, blocking collectives: 11.5 us -> 52.3 us  [exchanged(): return lax.all_to_all(tiles, axis, split_axis=0, concat_axis=0, tiled=True)]
    unnamed x73 -> x136, local copies, waits for them, and re-layouts: 28.1 us -> 59.9 us
    all_to_all x8 -> x4, starting transfers between devices: 64.4 us -> 39 us  [exchanged(): return lax.all_to_all(tiles, axis, split_axis=0, concat_axis=0, tiled=True)]
    all_to_all x4 -> x0, starting transfers between devices: 24 us -> none  [collect(): lax.all_to_all(copies, axis, split_axis=0, concat_axis=0, tiled=True)]
    all_to_all x4 -> x0, waiting for transfers between devices: 20.8 us -> none  [collect(): lax.all_to_all(copies, axis, split_axis=0, concat_axis=0, tiled=True)]
    pallas_call x13 -> x12, Pallas kernels: 37.1 us -> 56.3 us  [the longest x2 22.1 us: shards(): call(both_kernel, (payload, wide_piece, wide_piece), [SMEM] + [VMEM] * 3...]
    all_to_all x8 -> x4, waiting for transfers between devices: 16.2 us -> 8.81 us  [exchanged(): return lax.all_to_all(tiles, axis, split_axis=0, concat_axis=0, tiled=True)]
    ppermute x8 -> x6, waiting for transfers between devices: 16.2 us -> 9.4 us  [brought_to_first(): got.append(lax.ppermute(x, axis, pairs))]
  transfers between devices with their start and end apart: 24 -> 14, of which waited for: 14 -> 7; matrix products, arithmetic and copies ran while one was open for 8% -> 1% of each run, Pallas kernels for 9% -> 10%
where the time goes in v2:
time: 256 us; the launch traced here: 252 us
  local copies, waits for them, and re-layouts  64.5 us (25%)
  Pallas kernels  56.3 us (22%)
  starting transfers between devices  52.6 us (21%)
  blocking collectives  52.3 us (20%)
  waiting for transfers between devices  21.4 us (8%)
  other arithmetic  3.96 us (2%)
    unnamed x136, local copies, waits for them, and re-layouts  59.9 us
    all_to_all x3, blocking collectives, exchanged(): return lax.all_to_all(tiles, axis, split_axis=0, concat_axis=0, tiled=True)  52.3 us
    all_to_all x4, starting transfers between devices, exchanged(): return lax.all_to_all(tiles, axis, split_axis=0, concat_axis=0, tiled=True)  39 us
    pallas_call x2, Pallas kernels, shards(): call(both_kernel, (payload, wide_piece, wide_piece), [SMEM] + [VMEM] * 3...  22.1 us
    pallas_call x1, Pallas kernels, shards(): call(first_back_kernel, (square, wide_piece), [SMEM] + [VMEM] * 5 + [HBM]...  12.2 us
    pallas_call x2, Pallas kernels, kept_of(): call(state_kernel, [shape_of(*entry) for entry in states], [SMEM] + [VMEM...  11.6 us
    ppermute x6, waiting for transfers between devices, brought_to_first(): got.append(lax.ppermute(x, axis, pairs))  9.4 us
    all_to_all x4, waiting for transfers between devices, exchanged(): return lax.all_to_all(tiles, axis, split_axis=0, concat_axis=0, tiled=True)  8.81 us
  transfers between devices with their start and end apart: 14, of which 7 were waited for; matrix products, arithmetic and copies ran while one was open for 1% of the time, Pallas kernels for 10%

profile of v2, /device:TPU:514, one launch (start us, length us, event | category | flops | bytes accessed | tf_op | source)
XLA Modules:
  0.0 252.1 jit_solution(221932013220559098)
XLA Ops:
  1.8 2.7 %gather_fusion = bf16[768,256]{1,0:T(8,128)(2,1)S(1)} fusion(bf16[1187,256]{1,0:T(8,128)(2,1)S(1)} %copy-done, s32[1024]{0:T(1024)S(1)} %pad_clamp_fusion), kind=kCustom, calls=%fused_computation | custom fusion | bytes 789504 | tf_op jit(solution)/shard_map/jit(_take)/gather | solution.py:430
  5.4 22.8 %all-to-all-start = ((bf16[8,96,256]{2,1,0:T(8,128)(2,1)}), bf16[8,96,256]{2,1,0:T(8,128)(2,1)S(1)}, u32[]{:S(2)}, u32[]{:S(2)}) async-start(bf16[8,96,256]{2,1,0:T(8,128)(2,1)} %broadcast_select_fusion), calls=%async_computation | async-start | bytes 786432 | tf_op jit(solution)/shard_map/all_to_all | solution.py:398
  29.8 8.8 %all-to-all-done = bf16[8,96,256]{2,1,0:T(8,128)(2,1)S(1)} async-done(((bf16[8,96,256]{2,1,0:T(8,128)(2,1)}), bf16[8,96,256]{2,1,0:T(8,128)(2,1)S(1)}, u32[]{:S(2)}, u32[]{:S(2)}) %all-to-all-start) | async-done | bytes 393248 | tf_op jit(solution)/shard_map/all_to_all | solution.py:398
  38.7 1.3 collective-permute-start.2
  40.0 1.3 collective-permute-start.1
  41.3 1.3 collective-permute-start
  44.1 1.9 collective-permute-done.1
  46.0 1.3 collective-permute-start.5
  47.3 1.3 collective-permute-start.4
  48.7 1.3 collective-permute-start.3
  50.6 3.6 %collective-permute-done.5 = bf16[96,256]{1,0:T(8,128)(2,1)S(1)} collective-permute-done((bf16[96,256]{1,0:T(8,128)(2,1)S(1)}, bf16[96,256]{1,0:T(8,128)(2,1)S(1)}, u32[]{:S(2)}, u32[]{:S(2)}) %collective-permute-start.5) | collective-permute-done | bytes 49184 | tf_op jit(solution)/shard_map/ppermute | solution.py:419
  54.2 3.1 %collective-permute-done.4 = bf16[96,256]{1,0:T(8,128)(2,1)S(1)} collective-permute-done((bf16[96,256]{1,0:T(8,128)(2,1)S(1)}, bf16[96,256]{1,0:T(8,128)(2,1)S(1)}, u32[]{:S(2)}, u32[]{:S(2)}) %collective-permute-start.4) | collective-permute-done | bytes 49184 | tf_op jit(solution)/shard_map/ppermute | solution.py:419
  58.0 5.4 %all-to-all-start.1 = ((bf16[8,32,256]{2,1,0:T(8,128)(2,1)}), bf16[8,32,256]{2,1,0:T(8,128)(2,1)}, u32[]{:S(2)}, u32[]{:S(2)}) async-start(bf16[8,32,256]{2,1,0:T(8,128)(2,1)} %broadcast_in_dim.20), calls=%async_computation.1 | async-start | bytes 262144 | tf_op jit(solution)/shard_map/all_to_all | solution.py:398
  64.6 1.6 copy-done.23
  69.7 1.6 copy-done.8
  72.2 12.2 %shard_map.141 = (bf16[256,256]{1,0:T(8,128)(2,1)S(1)}, f32[32,256]{1,0:T(8,128)S(1)}) custom-call(s32[3]{0:T(128)S(1)} %copy-done.65, f32[4,1,512]{2,1,0:T(1,128)S(1)} %bitcast.60, f32[256,256]{1,0:T(8,128)S(1)} %get-tuple-element.30.basis_ref, bf16[256,256]{1,0:T(8,128)(2,1)S(1)} %copy-done.37, bf16[256,256]{1,0:T(8,128)(2,1)S(1)} %bitcast.54, ...), custom_call_target="tpu_custom_call" | custom-call | flops 2147483648 | bytes 1048576 | tf_op jit(solution)/shard_map/pallas_call | solution.py:511
  85.7 1.6 copy-done.3
  87.2 1.6 copy-done.9
  88.8 1.2 copy-done.15
  91.0 6.0 %shard_map.142 = (bf16[8,64,256]{2,1,0:T(8,128)(2,1)S(1)}, f32[32,256]{1,0:T(8,128)S(1)}) custom-call(s32[3]{0:T(128)S(1)} %get-tuple-element.67.where_ref, f32[4,1,512]{2,1,0:T(1,128)S(1)} %bitcast.61, f32[256,256]{1,0:T(8,128)S(1)} %get-tuple-element.30.basis_ref, bf16[8,32,256]{2,1,0:T(8,128)(2,1)} %all-to-all-done.1.rows_ref, ...), custom_call_target="tpu_custom_call" | custom-call | flops 1073741824 | bytes 1048576 | tf_op jit(solution)/shard_map/pallas_call | solution.py:520
  97.0 16.2 %all_to_all.35.parts_ref = bf16[8,64,256]{2,1,0:T(8,128)(2,1)S(1)} all-to-all(bf16[8,64,256]{2,1,0:T(8,128)(2,1)S(1)} %get-tuple-element.33), channel_id=1, replica_groups=mesh['groups'=2,'segment'=16,'head'=8] {'head'}, dimensions={0} | all-to-all | bytes 524288 | tf_op jit(solution)/shard_map/all_to_all | solution.py:398
  113.9 1.9 collective-permute-start.6
  115.8 1.3 collective-permute-start.7
  117.2 2.0 collective-permute-done.7.got_back_ref
  121.7 5.4 %all-to-all-start.3 = ((bf16[8,64,256]{2,1,0:T(8,128)(2,1)}), bf16[8,64,256]{2,1,0:T(8,128)(2,1)}, u32[]{:S(2)}, u32[]{:S(2)}) async-start(bf16[8,64,256]{2,1,0:T(8,128)(2,1)} %copy-done.29), calls=%async_computation.3 | async-start | bytes 524288 | tf_op jit(solution)/shard_map/all_to_all | solution.py:398
  127.1 1.6 copy-done.4
  128.7 1.6 copy-done.10
  132.1 5.8 %shard_map.145 = (f32[4,256,512]{2,1,0:T(8,128)S(1)}, f32[256,128]{1,0:T(8,128)S(1)}, f32[4,256,128]{2,1,0:T(8,128)S(1)}, f32[256,128]{1,0:T(8,128)S(1)}, bf16[2...) custom-call(s32[3]{0:T(128)S(1)} %copy-done.64, f32[4,1,512]{2,1,0:T(1,128)S(1)} %bitcast.62, ...), custom_call_target="tpu_custom_call" | custom-call | flops 1073741824 | bytes 1048576 | tf_op jit(solution)/shard_map/pallas_call | solution.py:494
  137.9 1.3 copy-done.26
  142.9 1.6 copy-done.5
  144.5 1.6 copy-done.11
  147.4 1.6 copy-done.27
  153.9 11.1 %shard_map.146 = (bf16[8,64,256]{2,1,0:T(8,128)(2,1)S(1)}, f32[32,256]{1,0:T(8,128)S(1)}, f32[32,256]{1,0:T(8,128)S(1)}) custom-call(s32[6]{0:T(128)S(1)} %stack.48.where_ref, f32[4,1,512]{2,1,0:T(1,128)S(1)} %bitcast.63, f32[256,256]{1,0:T(8,128)S(1)} %get-tuple-element.30.basis_ref, bf16[8,64,256]{2,1,0:T(8,128)(2,1)} %all-to-all-done.3.rows_ref, ...), custom_call_target="tpu_custom_call" | custom-call | flops 2147483648 | bytes 1048576 | tf_op jit(solution)/shard_map/pallas_call | solution.py:545
  165.0 17.7 %all_to_all.36.parts_ref = bf16[8,64,256]{2,1,0:T(8,128)(2,1)S(1)} all-to-all(bf16[8,64,256]{2,1,0:T(8,128)(2,1)S(1)} %get-tuple-element.44), channel_id=1, replica_groups=mesh['groups'=2,'segment'=16,'head'=8] {'head'}, dimensions={0} | all-to-all | bytes 524288 | tf_op jit(solution)/shard_map/all_to_all | solution.py:398
  182.7 1.3 collective-permute-start.8
  184.6 1.3 collective-permute-start.9
  189.0 5.4 %all-to-all-start.5 = ((bf16[8,64,256]{2,1,0:T(8,128)(2,1)}), bf16[8,64,256]{2,1,0:T(8,128)(2,1)}, u32[]{:S(2)}, u32[]{:S(2)}) async-start(bf16[8,64,256]{2,1,0:T(8,128)(2,1)} %copy-done.28), calls=%async_computation.5 | async-start | bytes 524288 | tf_op jit(solution)/shard_map/all_to_all | solution.py:398
  194.4 1.6 copy-done.6
  196.0 1.6 copy-done.12
  197.6 1.2 copy-done.18
  199.5 5.8 %shard_map.149 = (f32[4,256,512]{2,1,0:T(8,128)S(1)}, f32[256,128]{1,0:T(8,128)S(1)}, f32[4,256,128]{2,1,0:T(8,128)S(1)}, f32[256,128]{1,0:T(8,128)S(1)}, bf16[2...) custom-call(s32[3]{0:T(128)S(1)} %copy-done.63, f32[4,1,512]{2,1,0:T(1,128)S(1)} %bitcast.64, ...), custom_call_target="tpu_custom_call" | custom-call | flops 1073741824 | bytes 1048576 | tf_op jit(solution)/shard_map/pallas_call | solution.py:494
  205.3 1.3 copy-done.24
  210.3 1.6 copy-done.7
  211.9 1.6 copy-done.13
  214.7 1.6 copy-done.25
  221.2 11.0 %shard_map.150 = (bf16[8,64,256]{2,1,0:T(8,128)(2,1)S(1)}, f32[32,256]{1,0:T(8,128)S(1)}, f32[32,256]{1,0:T(8,128)S(1)}) custom-call(s32[6]{0:T(128)S(1)} %stack.48.where_ref, f32[4,1,512]{2,1,0:T(1,128)S(1)} %bitcast.65, f32[256,256]{1,0:T(8,128)S(1)} %get-tuple-element.30.basis_ref, bf16[8,64,256]{2,1,0:T(8,128)(2,1)} %all-to-all-done.5.rows_ref, ...), custom_call_target="tpu_custom_call" | custom-call | flops 2147483648 | bytes 1048576 | tf_op jit(solution)/shard_map/pallas_call | solution.py:545
  232.3 18.4 %all_to_all.37.parts_ref = bf16[8,64,256]{2,1,0:T(8,128)(2,1)S(1)} all-to-all(bf16[8,64,256]{2,1,0:T(8,128)(2,1)S(1)} %get-tuple-element.55), channel_id=1, replica_groups=mesh['groups'=2,'segment'=16,'head'=8] {'head'}, dimensions={0} | all-to-all | bytes 524288 | tf_op jit(solution)/shard_map/all_to_all | solution.py:398
  250.7 1.4 shard_map.151
  (151 shorter events, 43.5 us)
Async XLA Ops:
  1.8 26.3 %copy-start.67 = (bf16[1,256,256]{2,1,0:T(8,128)(2,1)S(1)}, bf16[1,256,256]{2,1,0:T(8,128)(2,1)}, u32[]{:S(2)}) copy-start(bf16[1,256,256]{2,1,0:T(8,128)(2,1)} %param.16) | copy-start | bytes 393220
  1.8 27.3 %copy-start.66 = (bf16[1,3,256,256]{3,2,1,0:T(8,128)(2,1)S(1)}, bf16[1,3,256,256]{3,2,1,0:T(8,128)(2,1)}, u32[]{:S(2)}) copy-start(bf16[1,3,256,256]{3,2,1,0:T(8,128)(2,1)} %param.17) | copy-start | bytes 1179652
  5.4 33.3 %all-to-all-start = ((bf16[8,96,256]{2,1,0:T(8,128)(2,1)}), bf16[8,96,256]{2,1,0:T(8,128)(2,1)S(1)}, u32[]{:S(2)}, u32[]{:S(2)}) async-start(bf16[8,96,256]{2,1,0:T(8,128)(2,1)} %broadcast_select_fusion), calls=%async_computation | async-start | bytes 786432 | tf_op jit(solution)/shard_map/all_to_all | solution.py:398
  38.7 5.4 %collective-permute-start.2 = (bf16[96,256]{1,0:T(8,128)(2,1)S(1)}, bf16[96,256]{1,0:T(8,128)(2,1)S(1)}, u32[]{:S(2)}, u32[]{:S(2)}) collective-permute-start(bf16[96,256]{1,0:T(8,128)(2,1)S(1)} %reduce_sum.12), channel_id=1, source_target_pairs={{24,0},{56,32},{88,64},{120,96},{25,1},{57,33},{89,65},{121,97},{2... | collective-permute-start | bytes 147464 | tf_op jit(solution)/shard_map/ppermute | solution.py:419
  40.0 6.0 %collective-permute-start.1 = (bf16[96,256]{1,0:T(8,128)(2,1)S(1)}, bf16[96,256]{1,0:T(8,128)(2,1)S(1)}, u32[]{:S(2)}, u32[]{:S(2)}) collective-permute-start(bf16[96,256]{1,0:T(8,128)(2,1)S(1)} %reduce_sum.12), channel_id=1, source_target_pairs={{16,0},{48,32},{80,64},{112,96},{17,1},{49,33},{81,65},{113,97},{1... | collective-permute-start | bytes 147464 | tf_op jit(solution)/shard_map/ppermute | solution.py:419
  41.3 4.7 %collective-permute-start = (bf16[96,256]{1,0:T(8,128)(2,1)S(1)}, bf16[96,256]{1,0:T(8,128)(2,1)S(1)}, u32[]{:S(2)}, u32[]{:S(2)}) collective-permute-start(bf16[96,256]{1,0:T(8,128)(2,1)S(1)} %reduce_sum.12), channel_id=1, source_target_pairs={{8,0},{40,32},{72,64},{104,96},{9,1},{41,33},{73,65},{105,97},{10,... | collective-permute-start | bytes 147464 | tf_op jit(solution)/shard_map/ppermute | solution.py:419
  46.0 8.1 %collective-permute-start.5 = (bf16[96,256]{1,0:T(8,128)(2,1)S(1)}, bf16[96,256]{1,0:T(8,128)(2,1)S(1)}, u32[]{:S(2)}, u32[]{:S(2)}) collective-permute-start(bf16[96,256]{1,0:T(8,128)(2,1)S(1)} %add_add_fusion.1), channel_id=1, source_target_pairs={{96,0},{97,1},{98,2},{99,3},{100,4},{101,5},{102,6},{103,7},{224,1... | collective-permute-start | bytes 147464 | tf_op jit(solution)/shard_map/ppermute | solution.py:419
  47.3 9.9 %collective-permute-start.4 = (bf16[96,256]{1,0:T(8,128)(2,1)S(1)}, bf16[96,256]{1,0:T(8,128)(2,1)S(1)}, u32[]{:S(2)}, u32[]{:S(2)}) collective-permute-start(bf16[96,256]{1,0:T(8,128)(2,1)S(1)} %add_add_fusion.1), channel_id=1, source_target_pairs={{64,0},{65,1},{66,2},{67,3},{68,4},{69,5},{70,6},{71,7},{192,128},... | collective-permute-start | bytes 147464 | tf_op jit(solution)/shard_map/ppermute | solution.py:419
  48.7 8.6 %collective-permute-start.3 = (bf16[96,256]{1,0:T(8,128)(2,1)S(1)}, bf16[96,256]{1,0:T(8,128)(2,1)S(1)}, u32[]{:S(2)}, u32[]{:S(2)}) collective-permute-start(bf16[96,256]{1,0:T(8,128)(2,1)S(1)} %add_add_fusion.1), channel_id=1, source_target_pairs={{32,0},{33,1},{34,2},{35,3},{36,4},{37,5},{38,6},{39,7},{160,128},... | collective-permute-start | bytes 147464 | tf_op jit(solution)/shard_map/ppermute | solution.py:419
  58.0 10.5 %copy-start.22 = (bf16[1,256,256]{2,1,0:T(8,128)(2,1)S(1)}, bf16[1,256,256]{2,1,0:T(8,128)(2,1)}, u32[]{:S(2)}) copy-start(bf16[1,256,256]{2,1,0:T(8,128)(2,1)} %param.15) | copy-start | bytes 393220
  58.0 27.7 %all-to-all-start.1 = ((bf16[8,32,256]{2,1,0:T(8,128)(2,1)}), bf16[8,32,256]{2,1,0:T(8,128)(2,1)}, u32[]{:S(2)}, u32[]{:S(2)}) async-start(bf16[8,32,256]{2,1,0:T(8,128)(2,1)} %broadcast_in_dim.20), calls=%async_computation.1 | async-start | bytes 262144 | tf_op jit(solution)/shard_map/all_to_all | solution.py:398
  63.4 1.2 copy-start.14
  64.6 1.6 copy-start.23
  67.4 1.6 copy-start.1
  67.4 2.2 copy-start.2
  67.5 2.2 copy-start.42
  67.5 2.2 copy-start.65
  69.7 1.6 copy-start.8
  85.6 1.6 copy-start.3
  87.2 1.6 copy-start.9
  88.8 1.2 copy-start.15
  91.0 22.3 %copy-start.58 = (f32[32,256]{1,0:T(8,128)S(1)}, f32[32,256]{1,0:T(8,128)}, u32[]{:S(2)}) copy-start(f32[32,256]{1,0:T(8,128)} %copy-done.57) | copy-start | bytes 98308
  97.0 30.1 %copy-start.36 = (bf16[256,256]{1,0:T(8,128)(2,1)S(1)}, bf16[256,256]{1,0:T(8,128)(2,1)}, u32[]{:S(2)}) copy-start(bf16[256,256]{1,0:T(8,128)(2,1)} %get-tuple-element.64.plain_ref) | copy-start | bytes 393220
  113.9 3.3 %collective-permute-start.6 = (bf16[32,256]{1,0:T(8,128)(2,1)}, bf16[32,256]{1,0:T(8,128)(2,1)}, u32[]{:S(2)}, u32[]{:S(2)}) collective-permute-start(bf16[32,256]{1,0:T(8,128)(2,1)} %get-tuple-element.36.refs_0_), channel_id=1, source_target_pairs={{0,8},{8,16},{16,24},{24,32},{32,40},{40,48},{48,56},{56,64},{64,7... | collective-permute-start | bytes 49160 | tf_op jit(solution)/shard_map/ppermute | solution.py:404
  115.8 3.4 %collective-permute-start.7 = (bf16[32,256]{1,0:T(8,128)(2,1)}, bf16[32,256]{1,0:T(8,128)(2,1)}, u32[]{:S(2)}, u32[]{:S(2)}) collective-permute-start(bf16[32,256]{1,0:T(8,128)(2,1)} %get-tuple-element.37.refs_2_), channel_id=1, source_target_pairs={{8,0},{16,8},{24,16},{32,24},{40,32},{48,40},{56,48},{64,56},{72,6... | collective-permute-start | bytes 49160 | tf_op jit(solution)/shard_map/ppermute | solution.py:404
  121.7 21.2 %all-to-all-start.3 = ((bf16[8,64,256]{2,1,0:T(8,128)(2,1)}), bf16[8,64,256]{2,1,0:T(8,128)(2,1)}, u32[]{:S(2)}, u32[]{:S(2)}) async-start(bf16[8,64,256]{2,1,0:T(8,128)(2,1)} %copy-done.29), calls=%async_computation.3 | async-start | bytes 524288 | tf_op jit(solution)/shard_map/all_to_all | solution.py:398
  127.1 1.6 copy-start.4
  128.7 1.6 copy-start.10
  130.3 1.2 copy-start.16
  137.9 1.3 copy-start.26
  142.9 1.6 copy-start.5
  144.5 1.6 copy-start.11
  146.1 1.2 copy-start.17
  147.4 1.6 copy-start.27
  153.9 33.8 %copy-start.21 = (bf16[3,256,256]{2,1,0:T(8,128)(2,1)S(1)}, bf16[3,256,256]{2,1,0:T(8,128)(2,1)}, u32[]{:S(2)}) copy-start(bf16[3,256,256]{2,1,0:T(8,128)(2,1)} %seed_ref.3) | copy-start | bytes 1179652
  164.9 29.5 %copy-start.35 = (bf16[256,256]{1,0:T(8,128)(2,1)S(1)}, bf16[256,256]{1,0:T(8,128)(2,1)}, u32[]{:S(2)}) copy-start(bf16[256,256]{1,0:T(8,128)(2,1)} %get-tuple-element.62.plain_ref) | copy-start | bytes 393220
  182.7 3.8 %collective-permute-start.8 = (bf16[32,256]{1,0:T(8,128)(2,1)S(1)}, bf16[32,256]{1,0:T(8,128)(2,1)S(1)}, u32[]{:S(2)}, u32[]{:S(2)}) collective-permute-start(bf16[32,256]{1,0:T(8,128)(2,1)S(1)} %get-tuple-element.47.refs_1_), channel_id=1, source_target_pairs={{0,8},{8,16},{16,24},{24,32},{32,40},{40,48},{48,56},{56,64},{64,7... | collective-permute-start | bytes 49160 | tf_op jit(solution)/shard_map/ppermute | solution.py:404
  184.6 3.1 %collective-permute-start.9 = (bf16[32,256]{1,0:T(8,128)(2,1)S(1)}, bf16[32,256]{1,0:T(8,128)(2,1)S(1)}, u32[]{:S(2)}, u32[]{:S(2)}) collective-permute-start(bf16[32,256]{1,0:T(8,128)(2,1)S(1)} %get-tuple-element.48.refs_3_), channel_id=1, source_target_pairs={{8,0},{16,8},{24,16},{32,24},{40,32},{48,40},{56,48},{64,56},{72,6... | collective-permute-start | bytes 49160 | tf_op jit(solution)/shard_map/ppermute | solution.py:404
  189.0 21.3 %all-to-all-start.5 = ((bf16[8,64,256]{2,1,0:T(8,128)(2,1)}), bf16[8,64,256]{2,1,0:T(8,128)(2,1)}, u32[]{:S(2)}, u32[]{:S(2)}) async-start(bf16[8,64,256]{2,1,0:T(8,128)(2,1)} %copy-done.28), calls=%async_computation.5 | async-start | bytes 524288 | tf_op jit(solution)/shard_map/all_to_all | solution.py:398
  194.4 1.6 copy-start.6
  196.0 1.6 copy-start.12
  197.6 1.2 copy-start.18
  205.3 1.3 copy-start.24
  210.3 1.6 copy-start.7
  211.9 1.6 copy-start.13
  214.7 1.6 copy-start.25
  221.2 29.5 %copy-start.60 = (bf16[32,256]{1,0:T(8,128)(2,1)S(1)}, bf16[32,256]{1,0:T(8,128)(2,1)}, u32[]{:S(2)}) copy-start(bf16[32,256]{1,0:T(8,128)(2,1)} %copy-done.59) | copy-start | bytes 49156
  221.2 29.5 %copy-start.62 = (bf16[32,256]{1,0:T(8,128)(2,1)S(1)}, bf16[32,256]{1,0:T(8,128)(2,1)}, u32[]{:S(2)}) copy-start(bf16[32,256]{1,0:T(8,128)(2,1)} %copy-done.61) | copy-start | bytes 49156
  (34 other events, 28.9 us)

commit v3 on v2

v3 whole, which is shorter than its diff:
```python
import functools
import math

import jax
import jax.numpy as jnp
from jax import lax
from jax.experimental import pallas as pl
from jax.experimental.pallas import tpu as pltpu
from jax.sharding import PartitionSpec as P

QUERY_HEADS = 32
KEY_VALUE_HEADS = 4
HEAD_SIZE = 128

EPS = 1e-06
CHUNK = 512
LANES = 128
LOW = jnp.bfloat16
WIDE = jnp.float32

VMEM = pl.BlockSpec(memory_space=pltpu.VMEM)
SMEM = pl.BlockSpec(memory_space=pltpu.SMEM)
HBM = pl.BlockSpec(memory_space=pltpu.HBM)


def dot(former, latter):
    return jnp.dot(former, latter, preferred_element_type=WIDE)


def dot_back(former, latter):
    return lax.dot_general(former, latter, (((1,), (1,)), ((), ())), preferred_element_type=WIDE)


def dot_turned(former, latter):
    return lax.dot_general(former, latter, (((0,), (0,)), ((), ())), preferred_element_type=WIDE)


def rms_scale(matrix):
    return lax.rsqrt(jnp.mean(matrix * matrix, axis=-1, keepdims=True) + EPS)


def norm_back(upstream_in, grad_hat):
    scaling = rms_scale(upstream_in)
    return scaling * grad_hat - upstream_in * scaling**3 * jnp.mean(
        grad_hat * upstream_in, axis=-1, keepdims=True
    )


def block(place, length):
    at = place * length
    return pl.ds(at if isinstance(at, int) else pl.multiple_of(at, length), length)


STATE = 6


def state_shapes(span, width, queries):
    heads = queries // HEAD_SIZE
    return [
        ((width // CHUNK, span, CHUNK), WIDE),
        ((span, LANES), WIDE),
        ((heads, span, HEAD_SIZE), WIDE),
        ((span, HEAD_SIZE), WIDE),
        ((span, HEAD_SIZE), LOW),
        ((heads, span, span), WIDE),
    ]


def spread(coeffs, gain_ref, expand_ref, query_ref, kv_ref, state):
    hidden, scale, queries, keys, values, _ = state
    count = hidden.shape[0]
    span = coeffs.shape[0]
    squares = jnp.zeros((span, 1), WIDE)
    for place in range(count):
        part = dot(coeffs, expand_ref[:, block(place, CHUNK)])
        hidden[place] = part
        squares += jnp.sum(part * part, axis=-1, keepdims=True)
    scaling = lax.rsqrt(squares / (count * CHUNK) + EPS)
    scale[...] = jnp.broadcast_to(scaling, scale.shape)
    wide_q = jnp.zeros((span, query_ref.shape[1]), WIDE)
    wide_kv = jnp.zeros((span, kv_ref.shape[1]), WIDE)
    for place in range(count):
        normed = (hidden[place] * scaling * gain_ref[place]).astype(LOW)
        wide_q += dot(normed, query_ref[block(place, CHUNK), :])
        wide_kv += dot(normed, kv_ref[block(place, CHUNK), :])
    for head in range(queries.shape[0]):
        queries[head] = wide_q[:, head * HEAD_SIZE : (head + 1) * HEAD_SIZE]
    keys[...] = wide_kv[:, :HEAD_SIZE]
    values[...] = wide_kv[:, HEAD_SIZE:].astype(LOW)


def hat(matrix):
    return (matrix * rms_scale(matrix)).astype(LOW)


def probabilities(q_hat, k_hat):
    rows = q_hat.shape[0]
    scores = dot_back(q_hat, k_hat) * (1.0 / math.sqrt(HEAD_SIZE))
    column = lax.broadcasted_iota(jnp.int32, (rows, rows), 1)
    row = lax.broadcasted_iota(jnp.int32, (rows, rows), 0)
    weights = jnp.where(column <= row, jnp.exp(scores), 0.0)
    return weights / jnp.sum(weights, axis=-1, keepdims=True)


def attend(folded_ref, state):
    _, _, queries, keys, values, probs = state
    k_hat = hat(keys[...])
    total = None if folded_ref is None else jnp.zeros((keys.shape[0], folded_ref.shape[1]), WIDE)
    for head in range(queries.shape[0]):
        chances = probabilities(hat(queries[head]), k_hat)
        probs[head] = chances
        if folded_ref is not None:
            attended = dot(chances.astype(LOW), values[...]).astype(LOW)
            total += dot(attended, folded_ref[block(head, HEAD_SIZE), :])
    return total


def go_back(grads, gain_ref, expand_ref, query_ref, kv_ref, folded_ref, state, grad_q, weighted_ref):
    hidden, scale, queries, keys, values, probs = state
    count = hidden.shape[0]
    keys_here = keys[...]
    k_hat = hat(keys_here)
    values_here = values[...]
    grad_khat = jnp.zeros(keys_here.shape, WIDE)
    grad_values = jnp.zeros(keys_here.shape, WIDE)
    for head in range(queries.shape[0]):
        upstream = queries[head]
        q_hat = hat(upstream)
        chances = probs[head]
        grad_attended = dot_back(grads, folded_ref[block(head, HEAD_SIZE), :]).astype(LOW)
        grad_chances = dot_back(grad_attended, values_here)
        inner = jnp.sum(grad_chances * chances, axis=-1, keepdims=True)
        grad_scores = chances * (grad_chances - inner) * (1.0 / math.sqrt(HEAD_SIZE))
        grad_scores = grad_scores.astype(LOW)
        grad_q[:, block(head, HEAD_SIZE)] = norm_back(upstream, dot(grad_scores, k_hat)).astype(LOW)
        grad_khat += dot_turned(grad_scores, q_hat)
        grad_values += dot_turned(chances.astype(LOW), grad_attended)
    grad_kv = jnp.concatenate(
        [norm_back(keys_here, grad_khat).astype(LOW), grad_values.astype(LOW)], axis=1
    )
    scaling = scale[:, :1]
    inner = jnp.zeros((keys_here.shape[0], 1), WIDE)
    for place in range(count):
        grad_normed = dot_back(grad_q[...], query_ref[block(place, CHUNK), :]) + dot_back(
            grad_kv, kv_ref[block(place, CHUNK), :]
        )
        weighted = grad_normed * gain_ref[place]
        weighted_ref[place] = weighted
        inner += jnp.sum(weighted * hidden[place], axis=-1, keepdims=True)
    factor = scaling**3 * (inner / (count * CHUNK))
    total = jnp.zeros(grads.shape, WIDE)
    for place in range(count):
        grad_hidden = scaling * weighted_ref[place] - hidden[place] * factor
        total += dot_back(grad_hidden.astype(LOW), expand_ref[:, block(place, CHUNK)])
    return total


def direct_of(rows, basis_ref, back):
    return lax.dot_general(
        rows.astype(WIDE),
        basis_ref[...],
        (((1,), (1 if back else 0,)), ((), ())),
        precision=lax.Precision.HIGHEST,
        preferred_element_type=WIDE,
    )


def own_rows(ref, share):
    at = lax.axis_index("head") * share
    return ref[pl.ds(pl.multiple_of(at, share), share), :]


def place_in_line():
    return lax.axis_index("segment"), lax.axis_size("segment") - 1


def put_tiles(payload_ref, total, at):
    share = payload_ref.shape[1] // 2
    for place in range(payload_ref.shape[0]):
        payload_ref[place, pl.ds(at, share), :] = total[place * share : (place + 1) * share].astype(
            LOW
        )


def take_tiles(rows_ref, at, other_ref, use_other, out_ref):
    share = rows_ref.shape[1] // 2
    for place in range(rows_ref.shape[0]):
        here = pl.ds(place * share, share)
        out_ref[here, :] = jnp.where(
            use_other, other_ref[here, :], rows_ref[place, pl.ds(at, share), :]
        )


def state_kernel(
    tick_ref, gain_ref, order_ref, stash_ref, other_ref, expand_ref, query_ref, kv_ref, *refs
):
    state, token_ref = [ref.at[1] for ref in refs[:STATE]], refs[STATE]
    segment, last = place_in_line()
    use_other = 2 * (last - segment) == tick_ref[0]
    coeffs = jnp.where(use_other, other_ref[...], stash_ref[...])
    spread(coeffs, gain_ref, expand_ref, query_ref, kv_ref, state)
    attend(None, state)
    token_ref[...] = jnp.zeros(token_ref.shape, LOW)


def forward_kernel(
    tick_ref, gain_ref, basis_ref, rows_ref, other_ref, expand_ref, query_ref, kv_ref, folded_ref, *refs
):
    payload_ref, direct_ref, coeffs_ref = refs[1 + STATE], refs[2 + 2 * STATE], refs[3 + 2 * STATE]
    state = [ref.at[0] for ref in refs[2 + STATE : 2 + 2 * STATE]]
    segment, _ = place_in_line()
    use_other = (tick_ref[0] == 0) & (segment != 0)
    take_tiles(rows_ref, 0, other_ref, use_other, coeffs_ref)
    direct_ref[...] = direct_of(own_rows(coeffs_ref, direct_ref.shape[0]), basis_ref, False)
    spread(coeffs_ref[...], gain_ref, expand_ref, query_ref, kv_ref, state)
    put_tiles(payload_ref, attend(folded_ref, state), 0)


def backward_kernel(
    tick_ref, gain_ref, basis_ref, rows_ref, other_ref, expand_ref, query_ref, kv_ref, folded_ref, *refs
):
    kept = refs[1 : 1 + STATE]
    payload_ref, direct_ref, token_ref, grads_ref, grad_q, weighted = refs[1 + STATE :]
    share = direct_ref.shape[0]
    segment, last = place_in_line()
    take_tiles(rows_ref, share, other_ref, tick_ref[0] == 0, grads_ref)
    direct_ref[...] = direct_of(own_rows(grads_ref, share), basis_ref, True)
    slot = jnp.where((tick_ref[0] != 0) & (segment == last), 0, 1)
    state = [ref.at[slot] for ref in kept]
    total = go_back(
        grads_ref[...], gain_ref, expand_ref, query_ref, kv_ref, folded_ref, state, grad_q, weighted
    )
    put_tiles(payload_ref, total, share)
    token_ref[...] = jnp.zeros(token_ref.shape, LOW)


def fold_kernel(expand_ref, compress_ref, out_weight_ref, key_ref, value_ref, basis_ref, folded_ref, kv_ref, sems):
    heads_here = out_weight_ref.shape[0] // HEAD_SIZE
    first = lax.axis_index("head") * heads_here * KEY_VALUE_HEADS // QUERY_HEADS * HEAD_SIZE
    here = pl.ds(pl.multiple_of(first, HEAD_SIZE), HEAD_SIZE)
    copies = [
        pltpu.make_async_copy(
            ref.at[:, here], kv_ref.at[:, pl.ds(place * HEAD_SIZE, HEAD_SIZE)], sems.at[place]
        )
        for place, ref in enumerate((key_ref, value_ref))
    ]
    for copy in copies:
        copy.start()
    basis_ref[...] = dot(expand_ref[...], compress_ref[...])
    folded_ref[...] = dot(out_weight_ref[...], compress_ref[...]).astype(folded_ref.dtype)
    for copy in copies:
        copy.wait()


def finish_kernel(parts_ref, direct_ref, direct_back_ref, out_ref, out_back_ref):
    share = direct_ref.shape[0]
    for at, direct, out in ((0, direct_ref, out_ref), (share, direct_back_ref, out_back_ref)):
        summed = parts_ref[0, pl.ds(at, share), :].astype(WIDE)
        for place in range(1, parts_ref.shape[0]):
            summed += parts_ref[place, pl.ds(at, share), :].astype(WIDE)
        out[...] = (summed + direct[...]).astype(LOW)


def last_kernel(count, parts_ref, direct_ref, direct_back_ref, *refs):
    share = direct_ref.shape[0]
    before, out_ref, out_back_ref = refs[: 2 * count], refs[2 * count], refs[2 * count + 1]
    for place in range(count):
        out_ref[0, place] = before[place][...]
        out_back_ref[0, place] = before[count + place][...]
    finish_kernel(
        parts_ref, direct_ref, direct_back_ref, out_ref.at[0, count], out_back_ref.at[0, count]
    )


def mix_kernel(tick_ref, got_ref, got_back_ref, later_ref, seed_ref, out_ref):
    share = got_ref.shape[0]
    tick = tick_ref[0]
    segment, last = place_in_line()
    later = later_ref[pl.ds(pl.multiple_of(tick * share, share), share), :]
    rows = jnp.where(segment == 0, later, got_ref[...])
    rows_back = jnp.where(segment == last, own_rows(seed_ref.at[tick], share), got_back_ref[...])
    for place in range(out_ref.shape[0]):
        out_ref[place, pl.ds(0, share), :] = rows
        out_ref[place, pl.ds(share, share), :] = rows_back


def shape_of(dims, kind):
    return jax.ShapeDtypeStruct(dims, kind)


def call(body, outs, specs, scratch=(), flops=0, aliases=None, limit=8):
    kernel = pl.pallas_call(
        body,
        out_shape=outs,
        in_specs=specs,
        out_specs=jax.tree.map(lambda _: VMEM, outs),
        scratch_shapes=list(scratch),
        input_output_aliases=aliases or {},
        cost_estimate=pl.CostEstimate(flops=flops, bytes_accessed=2**20, transcendentals=0),
        compiler_params=pltpu.CompilerParams(vmem_limit_bytes=limit * 2**20),
    )

    def run(*args):
        return kernel(
            *[
                pltpu.with_memory_space_constraint(arg, pltpu.HBM) if spec is HBM else arg
                for spec, arg in zip(specs, args)
            ]
        )

    return run


def exchanged(tiles, axis):
    return lax.all_to_all(tiles, axis, split_axis=0, concat_axis=0, tiled=True)


def passed_along(x, axis, by):
    length = lax.axis_size(axis)
    pairs = [(i, i + by) for i in range(length) if 0 <= i + by < length]
    return lax.ppermute(x, axis, pairs)


def brought_to_first(x, axis, radix, fillers):
    length = lax.axis_size(axis)
    step = 1
    while step < length:
        got = []
        for times in range(1, radix):
            pairs = [
                (i + times * step, i)
                for i in range(0, length, radix * step)
                if i + times * step < length
            ]
            if pairs:
                got.append(lax.ppermute(x, axis, pairs))
        beside = fillers.pop(0)(x) if fillers else None
        for other in got:
            x = x + other
        if beside is not None:
            x = x + beside[0, 0]
        step *= radix
    for filler in fillers:
        x = x + filler(x)[0, 0]
    return x


def picked_rows(ids, first_row, table, parts, share):
    ticks = ids.shape[0]
    local = ids.reshape(ticks, parts, share).swapaxes(0, 1).reshape(-1) - first_row
    inside = (local >= 0) & (local < table.shape[0])
    looked = jnp.take(table, local, axis=0, mode="clip")
    looked = jnp.where(inside[:, None], looked, jnp.zeros((), looked.dtype))
    return looked.reshape(parts, ticks * share, -1)


def shards(
    token_ids,
    embed_table,
    arriving,
    returning,
    stashed,
    seed_grad,
    expand,
    compress,
    norm_gain,
    w_query,
    key_weight,
    value_weight,
    w_out,
):
    segment_index = lax.axis_index("segment")
    last_segment = lax.axis_size("segment") - 1
    head_index = lax.axis_index("head")
    parts = lax.axis_size("head")
    ticks, span = token_ids.shape
    rank = embed_table.shape[1]
    width = expand.shape[2]
    queries = w_query.shape[2]
    share = span // parts

    def number(tick):
        return jnp.full((1,), tick, jnp.int32)

    first_row = lax.axis_index(("segment", "head")) * embed_table.shape[0]
    tiles = exchanged(picked_rows(token_ids, first_row, embed_table, parts, share), "head")

    gain = norm_gain.reshape(-1, 1, CHUNK)
    payload = shape_of((parts, 2 * share, rank), LOW)
    piece = shape_of((share, rank), LOW)
    wide_piece = shape_of((share, rank), WIDE)
    token = shape_of((16, 128), LOW)
    basis, folded, kv = call(
        fold_kernel,
        (
            shape_of((rank, rank), WIDE),
            shape_of((queries, rank), LOW),
            shape_of((width, 2 * HEAD_SIZE), LOW),
        ),
        [VMEM] * 3 + [HBM] * 2,
        [pltpu.SemaphoreType.DMA((2,))],
        flops=2 * (rank + queries) * width * rank,
    )(expand[0], compress[0], w_out[0], key_weight[0], value_weight[0])
    weights = (expand[0], w_query[0], kv, folded)
    states = [((2, *dims), kind) for dims, kind in state_shapes(span, width, queries)]
    state_outs = tuple(shape_of(*entry) for entry in states)
    work = 2 * span * width * (rank + queries + 2 * HEAD_SIZE)
    lines = pltpu.VMEM((span, rank), LOW)

    def kept_of(tick, order):
        *state, done = call(
            state_kernel,
            (*state_outs, token),
            [SMEM] + [VMEM] * 7,
            flops=work,
        )(number(tick), gain, order, stashed[0, tick], arriving[0], *weights[:3])
        return state, done

    def forward(tick, rows, other, out, state):
        out, *state, direct = call(
            forward_kernel,
            (payload, *state_outs, wide_piece),
            [SMEM] + [VMEM] * (9 + STATE),
            [lines],
            flops=work,
            aliases={9 + place: place for place in range(1 + STATE)},
        )(number(tick), gain, basis, rows, other, *weights, out, *state)
        return out, state, direct

    def backward(tick, rows, other, out, state):
        return call(
            backward_kernel,
            (payload, wide_piece, token),
            [SMEM] + [VMEM] * (9 + STATE),
            [lines, pltpu.VMEM((span, queries), LOW), pltpu.VMEM((width // CHUNK, span, CHUNK), WIDE)],
            flops=work,
            aliases={9: 0},
        )(number(tick), gain, basis, rows, other, *weights, out, *state)

    segment_index = lax.axis_index("segment")
    is_last = segment_index == lax.axis_size("segment") - 1
    backward_in = jnp.where(is_last, seed_grad[0], returning[0])
    state, _ = kept_of(0, jnp.zeros((ticks * share, rank), LOW))
    empty = jnp.zeros(payload.shape, LOW)
    out, direct_back, done = backward(0, empty, backward_in, empty, state)

    kept = []

    def filler(tick, order):
        state, done = kept_of(tick, order)
        kept.append(state)
        return done

    rows = brought_to_first(
        tiles.sum(axis=0) + done[0, 0],
        "segment",
        4,
        [functools.partial(filler, tick) for tick in range(1, ticks)],
    )
    gathered = exchanged(jnp.broadcast_to(rows[: 2 * share], payload.shape), "head")

    shares = []
    out, kept[0], direct = forward(0, gathered, arriving[0], out, kept[0])
    for tick in range(1, ticks):
        sent, sent_back = call(finish_kernel, (piece, piece), [VMEM] * 3, limit=4)(
            exchanged(out, "head"), direct, direct_back
        )
        shares.append((sent, sent_back))
        mixed = call(mix_kernel, payload, [SMEM] + [VMEM] * 4, limit=4)(
            number(tick),
            passed_along(sent, "segment", 1),
            passed_along(sent_back, "segment", -1),
            rows,
            seed_grad,
        )
        gathered = exchanged(mixed, "head")
        out, state, direct = forward(tick, gathered, arriving[0], out, kept[tick - 1])
        out, direct_back, _ = backward(tick, gathered, arriving[0], out, state)
    whole = shape_of((1, ticks, share, rank), LOW)
    return call(
        functools.partial(last_kernel, ticks - 1),
        (whole, whole),
        [VMEM] * (3 + 2 * (ticks - 1)),
        limit=4,
    )(
        exchanged(out, "head"),
        direct,
        direct_back,
        *[pair[0] for pair in shares],
        *[pair[1] for pair in shares],
    )


def solution(mesh):
    return jax.shard_map(
        shards,
        mesh=mesh,
        in_specs=(
            P("groups", None),
            P(("segment", "head"), None),
            P(("groups", "segment"), None, None),
            P(("groups", "segment"), None, None),
            P(("groups", "segment"), None, None, None),
            P("groups", None, None),
            P("segment", None, None),
            P("segment", None, None),
            P("segment", None),
            P("segment", None, "head"),
            P("segment", None, None),
            P("segment", None, None),
            P("segment", "head", None),
        ),
        out_specs=(
            P(("groups", "segment"), None, "head", None),
            P(("groups", "segment"), None, "head", None),
        ),
        check_vma=False,
    )
```

time: 256 us -> 199 us (0.78)
  local copies, waits for them, and re-layouts: 64.5 us -> 18.2 us
  blocking collectives: 52.3 us -> 88.8 us
  Pallas kernels: 56.3 us -> 34 us
  starting transfers between devices: 52.6 us -> 36.6 us
  waiting for transfers between devices: 21.4 us -> 9.59 us
  other arithmetic: 3.96 us -> 7.74 us
    unnamed x136 -> x44, local copies, waits for them, and re-layouts: 59.9 us -> 11.8 us
    all_to_all x3 -> x6, blocking collectives: 52.3 us -> 88.8 us  [exchanged(): return lax.all_to_all(tiles, axis, split_axis=0, concat_axis=0, tiled=True)]
    pallas_call x12 -> x15, Pallas kernels: 56.3 us -> 34 us  [run(): kernel(*[pltpu.with_memory_space_constraint(arg, pltpu.HBM) if spec is HB...]
    all_to_all x4 -> x1, starting transfers between devices: 39 us -> 23.4 us  [exchanged(): return lax.all_to_all(tiles, axis, split_axis=0, concat_axis=0, tiled=True)]
    all_to_all x4 -> x1, waiting for transfers between devices: 8.81 us -> 0.01 us  [exchanged(): return lax.all_to_all(tiles, axis, split_axis=0, concat_axis=0, tiled=True)]
    ppermute x6, waiting for transfers between devices: 9.4 us -> 4.14 us  [brought_to_first(): got.append(lax.ppermute(x, axis, pairs))]
    add x2 -> x3, other arithmetic: 0.03 us -> 3.47 us  [the longest x2 2.02 us: brought_to_first(): x = x + beside[0, 0]]
  transfers between devices with their start and end apart: 14 -> 11, of which waited for: 7 -> 4; matrix products, arithmetic and copies ran while one was open for 1% -> 2% of each run, Pallas kernels for 10% -> 7%
where the time goes in v3:
time: 199 us; the launch traced here: 196 us
  blocking collectives  88.8 us (45%)
  starting transfers between devices  36.6 us (18%)
  Pallas kernels  34 us (17%)
  local copies, waits for them, and re-layouts  18.2 us (9%)
  waiting for transfers between devices  9.59 us (5%)
  other arithmetic  7.74 us (4%)
    all_to_all x6, blocking collectives, exchanged(): return lax.all_to_all(tiles, axis, split_axis=0, concat_axis=0, tiled=True)  88.8 us
    pallas_call x15, Pallas kernels, run(): kernel(*[pltpu.with_memory_space_constraint(arg, pltpu.HBM) if spec is HB...  34 us
    all_to_all x1, starting transfers between devices, exchanged(): return lax.all_to_all(tiles, axis, split_axis=0, concat_axis=0, tiled=True)  23.4 us
    unnamed x44, local copies, waits for them, and re-layouts  11.8 us
    ppermute x6, starting transfers between devices, brought_to_first(): got.append(lax.ppermute(x, axis, pairs))  8.02 us
    ppermute x4, waiting for transfers between devices, passed_along(): return lax.ppermute(x, axis, pairs)  5.45 us
    ppermute x4, starting transfers between devices, passed_along(): return lax.ppermute(x, axis, pairs)  5.23 us
    ppermute x6, waiting for transfers between devices, brought_to_first(): got.append(lax.ppermute(x, axis, pairs))  4.14 us
  transfers between devices with their start and end apart: 11, of which 4 were waited for; matrix products, arithmetic and copies ran while one was open for 2% of the time, Pallas kernels for 7%

profile of v3, /device:TPU:514, one launch (start us, length us, event | category | flops | bytes accessed | tf_op | source)
XLA Modules:
  0.0 196.0 jit_solution(6828590475719976840)
XLA Ops:
  1.8 2.7 %gather_fusion = bf16[768,256]{1,0:T(8,128)(2,1)S(1)} fusion(bf16[1187,256]{1,0:T(8,128)(2,1)S(1)} %copy-done, s32[1024]{0:T(1024)S(1)} %pad_clamp_fusion), kind=kCustom, calls=%fused_computation | custom fusion | bytes 789504 | tf_op jit(solution)/shard_map/jit(_take)/gather | solution.py:352
  4.4 0.9 broadcast_select_fusion
  5.4 23.4 %all-to-all-start = ((bf16[8,96,256]{2,1,0:T(8,128)(2,1)}), bf16[8,96,256]{2,1,0:T(8,128)(2,1)}, u32[]{:S(2)}, u32[]{:S(2)}) async-start(bf16[8,96,256]{2,1,0:T(8,128)(2,1)} %broadcast_select_fusion), calls=%async_computation | async-start | bytes 786432 | tf_op jit(solution)/shard_map/all_to_all | solution.py:315
  28.7 1.2 copy-done.2
  29.9 1.6 copy-done.15
  31.5 1.2 copy-done.16
  32.8 2.1 %shard_map.140 = (f32[256,256]{1,0:T(8,128)S(1)}, bf16[512,256]{1,0:T(8,128)(2,1)S(1)}, bf16[2048,256]{1,0:T(8,128)(2,1)S(1)}) custom-call(bf16[256,2048]{1,0:T(8,128)(2,1)S(1)} %bitcast.35, bf16[2048,256]{1,0:T(8,128)(2,1)S(1)} %bitcast.54, bf16[512,2048]{1,0:T(8,128)(2,1)S(1)} %bitcast.53, bf16[2048,512]{1,0:T(8,128)(2,1)} %bitcast.64, ...), custom_call_target="tpu_custom_call" | custom-call | flops 805306368 | bytes 1048576 | tf_op jit(solution)/shard_map/pallas_call | solution.py:304
  34.9 1.0 copy-done.7
  35.9 1.8 slice_bitcast_fusion
  37.7 1.2 copy-done.3
  38.9 1.2 copy-done.8
  40.1 3.0 %shard_map.141 = (f32[2,4,256,512]{3,2,1,0:T(8,128)S(1)}, f32[2,256,128]{2,1,0:T(8,128)S(1)}, f32[2,4,256,128]{3,2,1,0:T(8,128)S(1)}, f32[2,256,128]{2,1,0:T(8,1...) custom-call(s32[1]{0:T(128)} %constant.13.clone.1.tick_ref, ...), custom_call_target="tpu_custom_call" | custom-call | flops 1073741824 | bytes 1048576 | tf_op jit(solution)/shard_map/pallas_call | solution.py:304
  43.1 0.9 select_bitcast_fusion.other_ref
  44.1 4.2 %shard_map.142 = (bf16[8,64,256]{2,1,0:T(8,128)(2,1)S(1)}, f32[32,256]{1,0:T(8,128)S(1)}, bf16[16,128]{1,0:T(8,128)(2,1)S(1)}) custom-call(s32[1]{0:T(128)} %constant.13.clone.1.tick_ref, f32[4,1,512]{2,1,0:T(1,128)S(1)} %bitcast.56, f32[256,256]{1,0:T(8,128)S(1)} %get-tuple-element.60.basis_ref, ...), custom_call_target="tpu_custom_call", output_to_operand_aliasing={{0}: (9, {})} | custom-call | flops 1073741824 | bytes 1048576 | tf_op jit(solution)/shard_map/pallas_call | solution.py:304
  48.8 1.7 reduce_sum.12
  50.5 1.4 broadcast_add_fusion.order_ref
  51.9 1.3 collective-permute-start.2
  53.2 1.3 collective-permute-start.1
  54.5 1.3 collective-permute-start
  55.9 1.2 copy-done.5
  57.1 1.2 copy-done.10
  58.3 0.9 copy-done.13
  59.2 0.9 copy-done.19
  60.1 2.5 %shard_map.143 = (f32[2,4,256,512]{3,2,1,0:T(8,128)S(1)}, f32[2,256,128]{2,1,0:T(8,128)S(1)}, f32[2,4,256,128]{3,2,1,0:T(8,128)S(1)}, f32[2,256,128]{2,1,0:T(8,1...) custom-call(s32[1]{0:T(128)} %constant.12.clone.1.tick_ref, ...), custom_call_target="tpu_custom_call" | custom-call | flops 1073741824 | bytes 1048576 | tf_op jit(solution)/shard_map/pallas_call | solution.py:304
  63.2 1.4 add_add_fusion.1.order_ref
  64.6 1.3 collective-permute-start.5
  65.9 1.3 collective-permute-start.4
  67.2 1.5 collective-permute-start.3
  68.7 2.4 %shard_map.144 = (f32[2,4,256,512]{3,2,1,0:T(8,128)S(1)}, f32[2,256,128]{2,1,0:T(8,128)S(1)}, f32[2,4,256,128]{3,2,1,0:T(8,128)S(1)}, f32[2,256,128]{2,1,0:T(8,1...) custom-call(s32[1]{0:T(128)} %constant.11.clone.1.tick_ref, ...), custom_call_target="tpu_custom_call" | custom-call | flops 1073741824 | bytes 1048576 | tf_op jit(solution)/shard_map/pallas_call | solution.py:304
  71.7 1.0 collective-permute-done.5
  72.7 3.1 %collective-permute-done.4 = bf16[96,256]{1,0:T(8,128)(2,1)S(1)} collective-permute-done((bf16[96,256]{1,0:T(8,128)(2,1)S(1)}, bf16[96,256]{1,0:T(8,128)(2,1)S(1)}, u32[]{:S(2)}, u32[]{:S(2)}) %collective-permute-start.4) | collective-permute-done | bytes 49184 | tf_op jit(solution)/shard_map/ppermute | solution.py:336
  76.5 16.1 %all_to_all.35.rows_ref = bf16[8,64,256]{2,1,0:T(8,128)(2,1)S(1)} all-to-all(bf16[8,64,256]{2,1,0:T(8,128)(2,1)S(1)} %broadcast_in_dim.28), channel_id=1, replica_groups=mesh['groups'=2,'segment'=16,'head'=8] {'head'}, dimensions={0} | all-to-all | bytes 524288 | tf_op jit(solution)/shard_map/all_to_all | solution.py:315
  92.6 3.3 %shard_map.145 = (bf16[8,64,256]{2,1,0:T(8,128)(2,1)S(1)}, f32[2,4,256,512]{3,2,1,0:T(8,128)S(1)}, f32[2,256,128]{2,1,0:T(8,128)S(1)}, f32[2,4,256,128]{3,2,1,0:...) custom-call(s32[1]{0:T(128)} %constant.13.clone.1.tick_ref, ...), custom_call_target="tpu_custom_call", output_to_operand_aliasing={{0}: (9, {}), {1}: (10, {}), {2}: (11, {}), {3}: (12, {}), ... | custom-call | flops 1073741824 | bytes 1048576 | tf_op jit(solution)/shard_map/pallas_call | solution.py:304
  95.9 13.0 %all_to_all.36.parts_ref = bf16[8,64,256]{2,1,0:T(8,128)(2,1)S(1)} all-to-all(bf16[8,64,256]{2,1,0:T(8,128)(2,1)S(1)} %get-tuple-element.79.refs_0_), channel_id=1, replica_groups=mesh['groups'=2,'segment'=16,'head'=8] {'head'}, dimensions={0} | all-to-all | bytes 524288 | tf_op jit(solution)/shard_map/all_to_all | solution.py:315
  108.9 1.3 collective-permute-start.6
  110.3 1.3 collective-permute-start.7
  111.6 1.8 collective-permute-done.7.got_back_ref
  113.4 14.9 %all_to_all.37.rows_ref = bf16[8,64,256]{2,1,0:T(8,128)(2,1)S(1)} all-to-all(bf16[8,64,256]{2,1,0:T(8,128)(2,1)S(1)} %shard_map.147), channel_id=1, replica_groups=mesh['groups'=2,'segment'=16,'head'=8] {'head'}, dimensions={0} | all-to-all | bytes 524288 | tf_op jit(solution)/shard_map/all_to_all | solution.py:315
  128.3 3.3 %shard_map.148 = (bf16[8,64,256]{2,1,0:T(8,128)(2,1)S(1)}, f32[2,4,256,512]{3,2,1,0:T(8,128)S(1)}, f32[2,256,128]{2,1,0:T(8,128)S(1)}, f32[2,4,256,128]{3,2,1,0:...) custom-call(s32[1]{0:T(128)} %constant.12.clone.1.tick_ref, ...), custom_call_target="tpu_custom_call", output_to_operand_aliasing={{0}: (9, {}), {1}: (10, {}), {2}: (11, {}), {3}: (12, {}), ... | custom-call | flops 1073741824 | bytes 1048576 | tf_op jit(solution)/shard_map/pallas_call | solution.py:304
  131.6 4.6 %shard_map.149 = (bf16[8,64,256]{2,1,0:T(8,128)(2,1)S(1)}, f32[32,256]{1,0:T(8,128)S(1)}, bf16[16,128]{1,0:T(8,128)(2,1)}) custom-call(s32[1]{0:T(128)} %constant.12.clone.1.tick_ref, f32[4,1,512]{2,1,0:T(1,128)S(1)} %bitcast.61, f32[256,256]{1,0:T(8,128)S(1)} %get-tuple-element.60.basis_ref, ...), custom_call_target="tpu_custom_call", output_to_operand_aliasing={{0}: (9, {})} | custom-call | flops 1073741824 | bytes 1048576 | tf_op jit(solution)/shard_map/pallas_call | solution.py:304
  136.2 14.8 %all_to_all.38.parts_ref = bf16[8,64,256]{2,1,0:T(8,128)(2,1)S(1)} all-to-all(bf16[8,64,256]{2,1,0:T(8,128)(2,1)S(1)} %get-tuple-element.97.refs_0_), channel_id=1, replica_groups=mesh['groups'=2,'segment'=16,'head'=8] {'head'}, dimensions={0} | all-to-all | bytes 524288 | tf_op jit(solution)/shard_map/all_to_all | solution.py:315
  151.0 1.3 collective-permute-start.8
  152.3 1.3 collective-permute-start.9
  153.7 3.7 %collective-permute-done.9.got_back_ref = bf16[32,256]{1,0:T(8,128)(2,1)S(1)} collective-permute-done((bf16[32,256]{1,0:T(8,128)(2,1)S(1)}, bf16[32,256]{1,0:T(8,128)(2,1)S(1)}, u32[]{:S(2)}, u32[]{:S(2)}) %collective-permute-start.9) | collective-permute-done | bytes 16416 | tf_op jit(solution)/shard_map/ppermute | solution.py:321
  157.4 13.5 %all_to_all.39.rows_ref = bf16[8,64,256]{2,1,0:T(8,128)(2,1)S(1)} all-to-all(bf16[8,64,256]{2,1,0:T(8,128)(2,1)S(1)} %shard_map.151), channel_id=1, replica_groups=mesh['groups'=2,'segment'=16,'head'=8] {'head'}, dimensions={0} | all-to-all | bytes 524288 | tf_op jit(solution)/shard_map/all_to_all | solution.py:315
  170.9 3.3 %shard_map.152 = (bf16[8,64,256]{2,1,0:T(8,128)(2,1)S(1)}, f32[2,4,256,512]{3,2,1,0:T(8,128)S(1)}, f32[2,256,128]{2,1,0:T(8,128)S(1)}, f32[2,4,256,128]{3,2,1,0:...) custom-call(s32[1]{0:T(128)} %constant.11.clone.1.tick_ref, ...), custom_call_target="tpu_custom_call", output_to_operand_aliasing={{0}: (9, {}), {1}: (10, {}), {2}: (11, {}), {3}: (12, {}), ... | custom-call | flops 1073741824 | bytes 1048576 | tf_op jit(solution)/shard_map/pallas_call | solution.py:304
  174.2 4.6 %shard_map.153 = (bf16[8,64,256]{2,1,0:T(8,128)(2,1)S(1)}, f32[32,256]{1,0:T(8,128)S(1)}, bf16[16,128]{1,0:T(8,128)(2,1)}) custom-call(s32[1]{0:T(128)} %constant.11.clone.1.tick_ref, f32[4,1,512]{2,1,0:T(1,128)S(1)} %bitcast.63, f32[256,256]{1,0:T(8,128)S(1)} %get-tuple-element.60.basis_ref, ...), custom_call_target="tpu_custom_call", output_to_operand_aliasing={{0}: (9, {})} | custom-call | flops 1073741824 | bytes 1048576 | tf_op jit(solution)/shard_map/pallas_call | solution.py:304
  178.8 16.5 %all_to_all.40.parts_ref = bf16[8,64,256]{2,1,0:T(8,128)(2,1)S(1)} all-to-all(bf16[8,64,256]{2,1,0:T(8,128)(2,1)S(1)} %get-tuple-element.115), channel_id=1, replica_groups=mesh['groups'=2,'segment'=16,'head'=8] {'head'}, dimensions={0} | all-to-all | bytes 524288 | tf_op jit(solution)/shard_map/all_to_all | solution.py:315
  (63 shorter events, 4.4 us)
Async XLA Ops:
  0.6 1.1 copy-start
  5.4 43.4 %all-to-all-start = ((bf16[8,96,256]{2,1,0:T(8,128)(2,1)}), bf16[8,96,256]{2,1,0:T(8,128)(2,1)}, u32[]{:S(2)}, u32[]{:S(2)}) async-start(bf16[8,96,256]{2,1,0:T(8,128)(2,1)} %broadcast_select_fusion), calls=%async_computation | async-start | bytes 786432 | tf_op jit(solution)/shard_map/all_to_all | solution.py:315
  28.7 1.2 copy-start.2
  29.9 1.6 copy-start.15
  31.5 1.2 copy-start.16
  32.8 4.9 %copy-start.1 = (bf16[1,2048,512]{2,1,0:T(8,128)(2,1)S(1)}, bf16[1,2048,512]{2,1,0:T(8,128)(2,1)}, u32[]{:S(2)}) copy-start(bf16[1,2048,512]{2,1,0:T(8,128)(2,1)} %param.22) | copy-start | bytes 6291460
  32.8 4.9 %copy-start.12 = (bf16[1,256,256]{2,1,0:T(8,128)(2,1)S(1)}, bf16[1,256,256]{2,1,0:T(8,128)(2,1)}, u32[]{:S(2)}) copy-start(bf16[1,256,256]{2,1,0:T(8,128)(2,1)} %param.15) | copy-start | bytes 393220
  32.8 4.9 %copy-start.17 = (f32[1,2048]{1,0:T(1,128)S(1)}, f32[1,2048]{1,0:T(1,128)}, u32[]{:S(2)}) copy-start(f32[1,2048]{1,0:T(1,128)} %param.21) | copy-start | bytes 24580
  34.9 1.0 copy-start.7
  37.6 1.2 copy-start.3
  38.9 1.2 copy-start.8
  40.1 3.0 %copy-start.21 = (bf16[1,256,256]{2,1,0:T(8,128)(2,1)S(1)}, bf16[1,256,256]{2,1,0:T(8,128)(2,1)}, u32[]{:S(2)}) copy-start(bf16[1,256,256]{2,1,0:T(8,128)(2,1)} %param.16) | copy-start | bytes 393220
  40.1 4.0 %copy-start.4 = (bf16[1,256,2048]{2,1,0:T(8,128)(2,1)S(1)}, bf16[1,256,2048]{2,1,0:T(8,128)(2,1)}, u32[]{:S(2)}) copy-start(bf16[1,256,2048]{2,1,0:T(8,128)(2,1)} %param.19) | copy-start | bytes 3145732
  40.1 4.0 %copy-start.9 = (bf16[2048,256]{1,0:T(8,128)(2,1)S(1)}, bf16[2048,256]{1,0:T(8,128)(2,1)}, u32[]{:S(2)}) copy-start(bf16[2048,256]{1,0:T(8,128)(2,1)} %copy-done.7) | copy-start | bytes 3145732
  51.9 11.3 %collective-permute-start.2 = (bf16[96,256]{1,0:T(8,128)(2,1)S(1)}, bf16[96,256]{1,0:T(8,128)(2,1)S(1)}, u32[]{:S(2)}, u32[]{:S(2)}) collective-permute-start(bf16[96,256]{1,0:T(8,128)(2,1)S(1)} %broadcast_add_fusion.order_ref), channel_id=1, source_target_pairs={{24,0},{56,32},{88,64},{120,96},{25,1},{57,33},{89,65},{121,97},{2... | collective-permute-start | bytes 147464 | tf_op jit(solution)/shard_map/ppermute | solution.py:336
  53.2 10.0 %collective-permute-start.1 = (bf16[96,256]{1,0:T(8,128)(2,1)S(1)}, bf16[96,256]{1,0:T(8,128)(2,1)S(1)}, u32[]{:S(2)}, u32[]{:S(2)}) collective-permute-start(bf16[96,256]{1,0:T(8,128)(2,1)S(1)} %broadcast_add_fusion.order_ref), channel_id=1, source_target_pairs={{16,0},{48,32},{80,64},{112,96},{17,1},{49,33},{81,65},{113,97},{1... | collective-permute-start | bytes 147464 | tf_op jit(solution)/shard_map/ppermute | solution.py:336
  54.5 8.7 %collective-permute-start = (bf16[96,256]{1,0:T(8,128)(2,1)S(1)}, bf16[96,256]{1,0:T(8,128)(2,1)S(1)}, u32[]{:S(2)}, u32[]{:S(2)}) collective-permute-start(bf16[96,256]{1,0:T(8,128)(2,1)S(1)} %broadcast_add_fusion.order_ref), channel_id=1, source_target_pairs={{8,0},{40,32},{72,64},{104,96},{9,1},{41,33},{73,65},{105,97},{10,... | collective-permute-start | bytes 147464 | tf_op jit(solution)/shard_map/ppermute | solution.py:336
  55.8 1.2 copy-start.5
  57.1 1.2 copy-start.10
  58.3 0.9 copy-start.13
  59.2 0.9 copy-start.19
  60.1 3.1 %copy-start.20 = (bf16[96,256]{1,0:T(8,128)(2,1)S(1)}, bf16[96,256]{1,0:T(8,128)(2,1)}, u32[]{:S(2)}) copy-start(bf16[96,256]{1,0:T(8,128)(2,1)} %reduce_sum.12) | copy-start | bytes 147460
  60.1 8.6 %copy-start.6 = (bf16[1,256,2048]{2,1,0:T(8,128)(2,1)S(1)}, bf16[1,256,2048]{2,1,0:T(8,128)(2,1)}, u32[]{:S(2)}) copy-start(bf16[1,256,2048]{2,1,0:T(8,128)(2,1)} %param.19) | copy-start | bytes 3145732
  60.1 8.6 %copy-start.11 = (bf16[2048,256]{1,0:T(8,128)(2,1)S(1)}, bf16[2048,256]{1,0:T(8,128)(2,1)}, u32[]{:S(2)}) copy-start(bf16[2048,256]{1,0:T(8,128)(2,1)} %copy-done.7) | copy-start | bytes 3145732
  60.1 8.6 %copy-start.18 = (bf16[256,256]{1,0:T(8,128)(2,1)S(1)}, bf16[256,256]{1,0:T(8,128)(2,1)}, u32[]{:S(2)}) copy-start(bf16[256,256]{1,0:T(8,128)(2,1)} %get-tuple-element.120.stash_ref) | copy-start | bytes 393220
  64.6 8.1 %collective-permute-start.5 = (bf16[96,256]{1,0:T(8,128)(2,1)S(1)}, bf16[96,256]{1,0:T(8,128)(2,1)S(1)}, u32[]{:S(2)}, u32[]{:S(2)}) collective-permute-start(bf16[96,256]{1,0:T(8,128)(2,1)S(1)} %add_add_fusion.1.order_ref), channel_id=1, source_target_pairs={{96,0},{97,1},{98,2},{99,3},{100,4},{101,5},{102,6},{103,7},{224,1... | collective-permute-start | bytes 147464 | tf_op jit(solution)/shard_map/ppermute | solution.py:336
  65.9 9.9 %collective-permute-start.4 = (bf16[96,256]{1,0:T(8,128)(2,1)S(1)}, bf16[96,256]{1,0:T(8,128)(2,1)S(1)}, u32[]{:S(2)}, u32[]{:S(2)}) collective-permute-start(bf16[96,256]{1,0:T(8,128)(2,1)S(1)} %add_add_fusion.1.order_ref), channel_id=1, source_target_pairs={{64,0},{65,1},{66,2},{67,3},{68,4},{69,5},{70,6},{71,7},{192,128},... | collective-permute-start | bytes 147464 | tf_op jit(solution)/shard_map/ppermute | solution.py:336
  67.2 8.6 %collective-permute-start.3 = (bf16[96,256]{1,0:T(8,128)(2,1)S(1)}, bf16[96,256]{1,0:T(8,128)(2,1)S(1)}, u32[]{:S(2)}, u32[]{:S(2)}) collective-permute-start(bf16[96,256]{1,0:T(8,128)(2,1)S(1)} %add_add_fusion.1.order_ref), channel_id=1, source_target_pairs={{32,0},{33,1},{34,2},{35,3},{36,4},{37,5},{38,6},{39,7},{160,128},... | collective-permute-start | bytes 147464 | tf_op jit(solution)/shard_map/ppermute | solution.py:336
  92.6 20.8 %copy-start.14 = (bf16[3,256,256]{2,1,0:T(8,128)(2,1)S(1)}, bf16[3,256,256]{2,1,0:T(8,128)(2,1)}, u32[]{:S(2)}) copy-start(bf16[3,256,256]{2,1,0:T(8,128)(2,1)} %seed_ref.3) | copy-start | bytes 1179652
  108.9 2.6 %collective-permute-start.6 = (bf16[32,256]{1,0:T(8,128)(2,1)S(1)}, bf16[32,256]{1,0:T(8,128)(2,1)S(1)}, u32[]{:S(2)}, u32[]{:S(2)}) collective-permute-start(bf16[32,256]{1,0:T(8,128)(2,1)S(1)} %get-tuple-element.82.refs_0_), channel_id=1, source_target_pairs={{0,8},{8,16},{16,24},{24,32},{32,40},{40,48},{48,56},{56,64},{64,7... | collective-permute-start | bytes 49160 | tf_op jit(solution)/shard_map/ppermute | solution.py:321
  110.3 3.1 %collective-permute-start.7 = (bf16[32,256]{1,0:T(8,128)(2,1)S(1)}, bf16[32,256]{1,0:T(8,128)(2,1)S(1)}, u32[]{:S(2)}, u32[]{:S(2)}) collective-permute-start(bf16[32,256]{1,0:T(8,128)(2,1)S(1)} %get-tuple-element.83.refs_2_), channel_id=1, source_target_pairs={{8,0},{16,8},{24,16},{32,24},{40,32},{48,40},{56,48},{64,56},{72,6... | collective-permute-start | bytes 49160 | tf_op jit(solution)/shard_map/ppermute | solution.py:321
  151.0 2.6 %collective-permute-start.8 = (bf16[32,256]{1,0:T(8,128)(2,1)S(1)}, bf16[32,256]{1,0:T(8,128)(2,1)S(1)}, u32[]{:S(2)}, u32[]{:S(2)}) collective-permute-start(bf16[32,256]{1,0:T(8,128)(2,1)S(1)} %get-tuple-element.100.refs_1_), channel_id=1, source_target_pairs={{0,8},{8,16},{16,24},{24,32},{32,40},{40,48},{48,56},{56,64},{64,7... | collective-permute-start | bytes 49160 | tf_op jit(solution)/shard_map/ppermute | solution.py:321
  152.3 5.0 %collective-permute-start.9 = (bf16[32,256]{1,0:T(8,128)(2,1)S(1)}, bf16[32,256]{1,0:T(8,128)(2,1)S(1)}, u32[]{:S(2)}, u32[]{:S(2)}) collective-permute-start(bf16[32,256]{1,0:T(8,128)(2,1)S(1)} %get-tuple-element.101.refs_3_), channel_id=1, source_target_pairs={{8,0},{16,8},{24,16},{32,24},{40,32},{48,40},{56,48},{64,56},{72,6... | collective-permute-start | bytes 49160 | tf_op jit(solution)/shard_map/ppermute | solution.py:321

commit v4 on v3

--- a/solution.py
+++ b/solution.py
@@ -15,6 +15,7 @@
 EPS = 1e-06
 CHUNK = 512
 LANES = 128
+RADIX = 4
 LOW = jnp.bfloat16
 WIDE = jnp.float32
 
@@ -194,13 +195,13 @@
 def state_kernel(
     tick_ref, gain_ref, order_ref, stash_ref, other_ref, expand_ref, query_ref, kv_ref, *refs
 ):
-    state, token_ref = [ref.at[1] for ref in refs[:STATE]], refs[STATE]
+    state = [ref.at[1] for ref in refs[:STATE]]
     segment, last = place_in_line()
     use_other = 2 * (last - segment) == tick_ref[0]
-    coeffs = jnp.where(use_other, other_ref[...], stash_ref[...])
+    coeffs = jnp.where(use_other, other_ref[...], stash_ref[tick_ref[0]])
     spread(coeffs, gain_ref, expand_ref, query_ref, kv_ref, state)
     attend(None, state)
-    token_ref[...] = jnp.zeros(token_ref.shape, LOW)
+    refs[STATE][...] = jnp.zeros(refs[STATE].shape, LOW)
 
 
 def forward_kernel(
@@ -217,15 +218,29 @@
 
 
 def backward_kernel(
-    tick_ref, gain_ref, basis_ref, rows_ref, other_ref, expand_ref, query_ref, kv_ref, folded_ref, *refs
+    tick_ref,
+    gain_ref,
+    basis_ref,
+    rows_ref,
+    returning_ref,
+    seed_ref,
+    expand_ref,
+    query_ref,
+    kv_ref,
+    folded_ref,
+    *refs,
 ):
     kept = refs[1 : 1 + STATE]
     payload_ref, direct_ref, token_ref, grads_ref, grad_q, weighted = refs[1 + STATE :]
     share = direct_ref.shape[0]
     segment, last = place_in_line()
-    take_tiles(rows_ref, share, other_ref, tick_ref[0] == 0, grads_ref)
+    first_tick = tick_ref[0] == 0
+    for place in range(rows_ref.shape[0]):
+        here = pl.ds(place * share, share)
+        given = jnp.where(segment == last, seed_ref[0, here, :], returning_ref[here, :])
+        grads_ref[here, :] = jnp.where(first_tick, given, rows_ref[place, pl.ds(share, share), :])
     direct_ref[...] = direct_of(own_rows(grads_ref, share), basis_ref, True)
-    slot = jnp.where((tick_ref[0] != 0) & (segment == last), 0, 1)
+    slot = jnp.where(jnp.logical_not(first_tick) & (segment == last), 0, 1)
     state = [ref.at[slot] for ref in kept]
     total = go_back(
         grads_ref[...], gain_ref, expand_ref, query_ref, kv_ref, folded_ref, state, grad_q, weighted
@@ -234,7 +249,55 @@
     token_ref[...] = jnp.zeros(token_ref.shape, LOW)
 
 
-def fold_kernel(expand_ref, compress_ref, out_weight_ref, key_ref, value_ref, basis_ref, folded_ref, kv_ref, sems):
+def pick_kernel(ids_ref, table_ref, out_ref):
+    rows = table_ref.shape[0]
+    full = rows // LANES * LANES
+    ticks, span = ids_ref.shape
+    share = out_ref.shape[1] // ticks
+    own = lax.axis_index("segment") * lax.axis_size("head") + lax.axis_index("head")
+    lane = lax.broadcasted_iota(jnp.int32, (LANES, LANES), 1).astype(WIDE)
+
+    def chosen(names, at):
+        return jnp.where(names == lane + float(at), 1.0, 0.0).astype(LOW)
+
+    for tick in range(ticks):
+        for at in range(0, span, LANES):
+            local = (ids_ref[tick : tick + 1, at : at + LANES] - own * rows).astype(WIDE)
+            names = jnp.broadcast_to(local, (LANES, LANES)).T
+            hits = jnp.concatenate([chosen(names, k) for k in range(0, full, LANES)], axis=1)
+            found = dot(hits, table_ref[pl.ds(0, full), :])
+            if rows > full:
+                found += dot(
+                    chosen(names, full)[:, : rows - full], table_ref[pl.ds(full, rows - full), :]
+                )
+            for place in range(LANES // share):
+                out_ref[at // share + place, pl.ds(tick * share, share), :] = found[
+                    place * share : (place + 1) * share
+                ].astype(LOW)
+
+
+def sum_kernel(parts_ref, out_ref, order_ref):
+    total = parts_ref[0]
+    for place in range(1, parts_ref.shape[0]):
+        total += parts_ref[place]
+    out_ref[...] = total
+    order_ref[...] = total[: order_ref.shape[0]]
+
+
+def join_kernel(count, rows_ref, *refs):
+    got, (token_ref, out_ref, *tiles) = refs[:count], refs[count:]
+    total = rows_ref[...]
+    for ref in got:
+        total += ref[...]
+    out_ref[...] = total
+    for ref in tiles:
+        for place in range(ref.shape[0]):
+            ref[place] = total[: ref.shape[1]]
+
+
+def fold_kernel(
+    order_ref, expand_ref, compress_ref, out_weight_ref, key_ref, value_ref, basis_ref, folded_ref, kv_ref, sems
+):
     heads_here = out_weight_ref.shape[0] // HEAD_SIZE
     first = lax.axis_index("head") * heads_here * KEY_VALUE_HEADS // QUERY_HEADS * HEAD_SIZE
     here = pl.ds(pl.multiple_of(first, HEAD_SIZE), HEAD_SIZE)
@@ -272,7 +335,7 @@
     )
 
 
-def mix_kernel(tick_ref, got_ref, got_back_ref, later_ref, seed_ref, out_ref):
+def mix_kernel(tick_ref, got_ref, got_back_ref, later_ref, seed_ref, token_ref, out_ref):
     share = got_ref.shape[0]
     tick = tick_ref[0]
     segment, last = place_in_line()
@@ -321,37 +384,18 @@
     return lax.ppermute(x, axis, pairs)
 
 
-def brought_to_first(x, axis, radix, fillers):
+def sent_down(x, axis, radix, step):
     length = lax.axis_size(axis)
-    step = 1
-    while step < length:
-        got = []
-        for times in range(1, radix):
-            pairs = [
-                (i + times * step, i)
-                for i in range(0, length, radix * step)
-                if i + times * step < length
-            ]
-            if pairs:
-                got.append(lax.ppermute(x, axis, pairs))
-        beside = fillers.pop(0)(x) if fillers else None
-        for other in got:
-            x = x + other
-        if beside is not None:
-            x = x + beside[0, 0]
-        step *= radix
-    for filler in fillers:
-        x = x + filler(x)[0, 0]
-    return x
-
-
-def picked_rows(ids, first_row, table, parts, share):
-    ticks = ids.shape[0]
-    local = ids.reshape(ticks, parts, share).swapaxes(0, 1).reshape(-1) - first_row
-    inside = (local >= 0) & (local < table.shape[0])
-    looked = jnp.take(table, local, axis=0, mode="clip")
-    looked = jnp.where(inside[:, None], looked, jnp.zeros((), looked.dtype))
-    return looked.reshape(parts, ticks * share, -1)
+    got = []
+    for times in range(1, radix):
+        pairs = [
+            (i + times * step, i)
+            for i in range(0, length, radix * step)
+            if i + times * step < length
+        ]
+        if pairs:
+            got.append(lax.ppermute(x, axis, pairs))
+    return got
 
 
 def shards(
@@ -369,9 +413,8 @@
     value_weight,
     w_out,
 ):
-    segment_index = lax.axis_index("segment")
-    last_segment = lax.axis_size("segment") - 1
-    head_index = lax.axis_index("head")
+    if lax.axis_size("segment") != RADIX**2:
+        raise ValueError("segments")
     parts = lax.axis_size("head")
     ticks, span = token_ids.shape
     rank = embed_table.shape[1]
@@ -382,30 +425,34 @@
     def number(tick):
         return jnp.full((1,), tick, jnp.int32)
 
-    first_row = lax.axis_index(("segment", "head")) * embed_table.shape[0]
-    tiles = exchanged(picked_rows(token_ids, first_row, embed_table, parts, share), "head")
-
     gain = norm_gain.reshape(-1, 1, CHUNK)
     payload = shape_of((parts, 2 * share, rank), LOW)
     piece = shape_of((share, rank), LOW)
     wide_piece = shape_of((share, rank), WIDE)
+    lot = shape_of((ticks * share, rank), LOW)
     token = shape_of((16, 128), LOW)
-    basis, folded, kv = call(
-        fold_kernel,
-        (
-            shape_of((rank, rank), WIDE),
-            shape_of((queries, rank), LOW),
-            shape_of((width, 2 * HEAD_SIZE), LOW),
-        ),
-        [VMEM] * 3 + [HBM] * 2,
-        [pltpu.SemaphoreType.DMA((2,))],
-        flops=2 * (rank + queries) * width * rank,
-    )(expand[0], compress[0], w_out[0], key_weight[0], value_weight[0])
-    weights = (expand[0], w_query[0], kv, folded)
     states = [((2, *dims), kind) for dims, kind in state_shapes(span, width, queries)]
     state_outs = tuple(shape_of(*entry) for entry in states)
     work = 2 * span * width * (rank + queries + 2 * HEAD_SIZE)
     lines = pltpu.VMEM((span, rank), LOW)
+
+    picked = call(pick_kernel, shape_of((parts, ticks * share, rank), LOW), [VMEM] * 2, flops=work)(
+        token_ids, embed_table
+    )
+    rows, order = call(sum_kernel, (lot, piece), [VMEM], limit=4)(exchanged(picked, "head"))
+
+    def folding(order):
+        return call(
+            fold_kernel,
+            (
+                shape_of((rank, rank), WIDE),
+                shape_of((queries, rank), LOW),
+                shape_of((width, 2 * HEAD_SIZE), LOW),
+            ),
+            [VMEM] * 4 + [HBM] * 2,
+            [pltpu.SemaphoreType.DMA((2,))],
+            flops=2 * (rank + queries) * width * rank,
+        )(order, expand[0], compress[0], w_out[0], key_weight[0], value_weight[0])
 
     def kept_of(tick, order):
         *state, done = call(
@@ -413,10 +460,10 @@
             (*state_outs, token),
             [SMEM] + [VMEM] * 7,
             flops=work,
-        )(number(tick), gain, order, stashed[0, tick], arriving[0], *weights[:3])
+        )(number(tick), gain, order, stashed[0], arriving[0], *weights[:3])
         return state, done
 
-    def forward(tick, rows, other, out, state):
+    def forward(tick, gathered, out, state):
         out, *state, direct = call(
             forward_kernel,
             (payload, *state_outs, wide_piece),
@@ -424,58 +471,51 @@
             [lines],
             flops=work,
             aliases={9 + place: place for place in range(1 + STATE)},
-        )(number(tick), gain, basis, rows, other, *weights, out, *state)
+        )(number(tick), gain, basis, gathered, arriving[0], *weights, out, *state)
         return out, state, direct
 
-    def backward(tick, rows, other, out, state):
+    def backward(tick, gathered, out, state):
         return call(
             backward_kernel,
             (payload, wide_piece, token),
-            [SMEM] + [VMEM] * (9 + STATE),
+            [SMEM] + [VMEM] * (10 + STATE),
             [lines, pltpu.VMEM((span, queries), LOW), pltpu.VMEM((width // CHUNK, span, CHUNK), WIDE)],
             flops=work,
-            aliases={9: 0},
-        )(number(tick), gain, basis, rows, other, *weights, out, *state)
-
-    segment_index = lax.axis_index("segment")
-    is_last = segment_index == lax.axis_size("segment") - 1
-    backward_in = jnp.where(is_last, seed_grad[0], returning[0])
-    state, _ = kept_of(0, jnp.zeros((ticks * share, rank), LOW))
-    empty = jnp.zeros(payload.shape, LOW)
-    out, direct_back, done = backward(0, empty, backward_in, empty, state)
-
-    kept = []
-
-    def filler(tick, order):
-        state, done = kept_of(tick, order)
-        kept.append(state)
-        return done
-
-    rows = brought_to_first(
-        tiles.sum(axis=0) + done[0, 0],
-        "segment",
-        4,
-        [functools.partial(filler, tick) for tick in range(1, ticks)],
-    )
-    gathered = exchanged(jnp.broadcast_to(rows[: 2 * share], payload.shape), "head")
+            aliases={10: 0},
+        )(number(tick), gain, basis, gathered, returning[0], seed_grad, *weights, out, *state)
+
+    got = sent_down(rows, "segment", RADIX, 1)
+    basis, folded, kv = folding(order)
+    weights = (expand[0], w_query[0], kv, folded)
+    state, done = kept_of(0, order)
+    rows, spare, out = call(
+        functools.partial(join_kernel, len(got)),
+        (lot, payload, payload),
+        [VMEM] * (2 + len(got)),
+        limit=4,
+    )(rows, *got, done)
+    got = sent_down(rows, "segment", RADIX, RADIX)
+    out, direct_back, done = backward(0, spare, out, state)
+    rows, tiles = call(
+        functools.partial(join_kernel, len(got)), (lot, payload), [VMEM] * (2 + len(got)), limit=4
+    )(rows, *got, done)
+    out, state, direct = forward(0, exchanged(tiles, "head"), out, state)
 
     shares = []
-    out, kept[0], direct = forward(0, gathered, arriving[0], out, kept[0])
     for tick in range(1, ticks):
         sent, sent_back = call(finish_kernel, (piece, piece), [VMEM] * 3, limit=4)(
             exchanged(out, "head"), direct, direct_back
         )
         shares.append((sent, sent_back))
-        mixed = call(mix_kernel, payload, [SMEM] + [VMEM] * 4, limit=4)(
-            number(tick),
-            passed_along(sent, "segment", 1),
-            passed_along(sent_back, "segment", -1),
-            rows,
-            seed_grad,
+        arrived = passed_along(sent, "segment", 1)
+        arrived_back = passed_along(sent_back, "segment", -1)
+        state, done = kept_of(tick, sent)
+        mixed = call(mix_kernel, payload, [SMEM] + [VMEM] * 5, limit=4)(
+            number(tick), arrived, arrived_back, rows, seed_grad, done
         )
         gathered = exchanged(mixed, "head")
-        out, state, direct = forward(tick, gathered, arriving[0], out, kept[tick - 1])
-        out, direct_back, _ = backward(tick, gathered, arriving[0], out, state)
+        out, state, direct = forward(tick, gathered, out, state)
+        out, direct_back, _ = backward(tick, gathered, out, state)
     whole = shape_of((1, ticks, share, rank), LOW)
     return call(
         functools.partial(last_kernel, ticks - 1),

time: 199 us -> 175 us (0.88); the launches traced: 196 us -> 174 us
  blocking collectives: 88.8 us -> 117 us
  starting transfers between devices: 36.6 us -> 16.8 us
  local copies, waits for them, and re-layouts: 18.2 us -> 2.14 us
  other arithmetic: 7.74 us -> 0 us
  waiting for transfers between devices: 9.59 us -> 3.18 us
    all_to_all x6 -> x7, blocking collectives: 88.8 us -> 117 us  [exchanged(): return lax.all_to_all(tiles, axis, split_axis=0, concat_axis=0, tiled=True)]
    all_to_all x1 -> x0, starting transfers between devices: 23.4 us -> none  [exchanged(): return lax.all_to_all(tiles, axis, split_axis=0, concat_axis=0, tiled=True)]
    unnamed x44 -> x22, local copies, waits for them, and re-layouts: 11.8 us -> 2.14 us
    ppermute x4, waiting for transfers between devices: 5.45 us -> 0.01 us  [passed_along(): return lax.ppermute(x, axis, pairs)]
    ppermute x4, starting transfers between devices: 5.23 us -> 8.95 us  [passed_along(): return lax.ppermute(x, axis, pairs)]
    add x3 -> x0, other arithmetic: 3.47 us -> none  [the longest x2 2.02 us: brought_to_first(): x = x + beside[0, 0]]
    gather x1 -> x0, local copies, waits for them, and re-layouts: 2.66 us -> none  [picked_rows(): looked = jnp.take(table, local, axis=0, mode='clip')]
    pallas_call x15 -> x19, Pallas kernels: 34 us -> 34 us  [run(): kernel(*[pltpu.with_memory_space_constraint(arg, pltpu.HBM) if spec is HB...]
  transfers between devices with their start and end apart: 11 -> 10, of which waited for: 4 -> 1; matrix products, arithmetic and copies ran while one was open for 2% -> 0% of each run, Pallas kernels for 7% -> 8%
where the time goes in v4:
time: 175 us; the launch traced here: 174 us
  blocking collectives  117 us (67%)
  Pallas kernels  34 us (19%)
  starting transfers between devices  16.8 us (10%)
  waiting for transfers between devices  3.18 us (2%)
  local copies, waits for them, and re-layouts  2.14 us (1%)
    all_to_all x7, blocking collectives, exchanged(): return lax.all_to_all(tiles, axis, split_axis=0, concat_axis=0, tiled=True)  117 us
    pallas_call x19, Pallas kernels, run(): kernel(*[pltpu.with_memory_space_constraint(arg, pltpu.HBM) if spec is HB...  34 us
    ppermute x4, starting transfers between devices, passed_along(): return lax.ppermute(x, axis, pairs)  8.95 us
    ppermute x6, starting transfers between devices, sent_down(): got.append(lax.ppermute(x, axis, pairs))  7.85 us
  transfers between devices with their start and end apart: 10, of which 1 were waited for; matrix products, arithmetic and copies ran while one was open for 0% of the time, Pallas kernels for 8%

profile of v4, /device:TPU:514, one launch (start us, length us, event | category | flops | bytes accessed | tf_op | source)
XLA Modules:
  0.0 174.0 jit_solution(16599258608462329104)
XLA Ops:
  0.7 1.2 copy-done.9
  1.9 0.9 copy-done.10
  2.8 0.8 shard_map.140
  3.6 32.3 %all_to_all.35.parts_ref = bf16[8,96,256]{2,1,0:T(8,128)(2,1)S(1)} all-to-all(bf16[8,96,256]{2,1,0:T(8,128)(2,1)S(1)} %shard_map.140), channel_id=1, replica_groups=mesh['groups'=2,'segment'=16,'head'=8] {'head'}, dimensions={0} | all-to-all | bytes 786432 | tf_op jit(solution)/shard_map/all_to_all | solution.py:378
  35.9 1.3 collective-permute-start.2
  37.2 1.3 collective-permute-start.1
  38.5 1.3 collective-permute-start
  39.9 0.0 copy-start
  39.9 0.0 copy-start.3
  39.9 0.0 copy-start.4
  39.9 0.0 copy-start.8
  39.9 2.1 %shard_map.142 = (f32[256,256]{1,0:T(8,128)S(1)}, bf16[512,256]{1,0:T(8,128)(2,1)S(1)}, bf16[2048,256]{1,0:T(8,128)(2,1)S(1)}) custom-call(bf16[32,256]{1,0:T(8,128)(2,1)S(1)} %get-tuple-element.62.order_ref, bf16[256,2048]{1,0:T(8,128)(2,1)S(1)} %bitcast.19, bf16[2048,256]{1,0:T(8,128)(2,1)S(1)} %bitcast.42, bf16[512,2048]{1,0:T(8,128)(2,1)S(1)} %bitcast.38, ...), custom_call_target="tpu_custom_call" | custom-call | flops 805306368 | bytes 1048576 | tf_op jit(solution)/shard_map/pallas_call | solution.py:367
  42.1 0.0 copy-start.2
  42.1 0.0 copy-start.6
  42.1 2.4 %shard_map.143 = (f32[2,4,256,512]{3,2,1,0:T(8,128)S(1)}, f32[2,256,128]{2,1,0:T(8,128)S(1)}, f32[2,4,256,128]{3,2,1,0:T(8,128)S(1)}, f32[2,256,128]{2,1,0:T(8,1...) custom-call(s32[1]{0:T(128)} %constant.2.clone.1.tick_ref, ...), custom_call_target="tpu_custom_call" | custom-call | flops 1073741824 | bytes 1048576 | tf_op jit(solution)/shard_map/pallas_call | solution.py:367
  44.6 0.0 collective-permute-done.2.refs_2_
  44.6 0.0 collective-permute-done.1.refs_1_
  44.6 0.0 collective-permute-done.refs_0_
  44.6 0.1 shard_map.144
  44.6 1.3 collective-permute-start.5
  46.0 1.3 collective-permute-start.4
  47.3 1.3 collective-permute-start.3
  48.6 4.1 %shard_map.145 = (bf16[8,64,256]{2,1,0:T(8,128)(2,1)S(1)}, f32[32,256]{1,0:T(8,128)S(1)}, bf16[16,128]{1,0:T(8,128)(2,1)S(1)}) custom-call(s32[1]{0:T(128)} %constant.2.clone.1.tick_ref, f32[4,1,512]{2,1,0:T(1,128)S(1)} %bitcast.44, f32[256,256]{1,0:T(8,128)S(1)} %get-tuple-element.63.basis_ref, ...), custom_call_target="tpu_custom_call", output_to_operand_aliasing={{0}: (10, {})} | custom-call | flops 1073741824 | bytes 1048576 | tf_op jit(solution)/shard_map/pallas_call | solution.py:367
  52.7 0.0 collective-permute-done.5.refs_2_
  52.8 3.1 %collective-permute-done.4.refs_1_ = bf16[96,256]{1,0:T(8,128)(2,1)S(1)} collective-permute-done((bf16[96,256]{1,0:T(8,128)(2,1)S(1)}, bf16[96,256]{1,0:T(8,128)(2,1)S(1)}, u32[]{:S(2)}, u32[]{:S(2)}) %collective-permute-start.4) | collective-permute-done | bytes 49184 | tf_op jit(solution)/shard_map/ppermute | solution.py:397
  55.9 0.0 collective-permute-done.3.refs_0_
  55.9 12.4 %all_to_all.36.rows_ref = bf16[8,64,256]{2,1,0:T(8,128)(2,1)S(1)} all-to-all(bf16[8,64,256]{2,1,0:T(8,128)(2,1)S(1)} %get-tuple-element.78), channel_id=1, replica_groups=mesh['groups'=2,'segment'=16,'head'=8] {'head'}, dimensions={0} | all-to-all | bytes 524288 | tf_op jit(solution)/shard_map/all_to_all | solution.py:378
  68.3 3.3 %shard_map.147 = (bf16[8,64,256]{2,1,0:T(8,128)(2,1)S(1)}, f32[2,4,256,512]{3,2,1,0:T(8,128)S(1)}, f32[2,256,128]{2,1,0:T(8,128)S(1)}, f32[2,4,256,128]{3,2,1,0:...) custom-call(s32[1]{0:T(128)} %constant.2.clone.1.tick_ref, ...), custom_call_target="tpu_custom_call", output_to_operand_aliasing={{0}: (9, {}), {1}: (10, {}), {2}: (11, {}), {3}: (12, {}), ... | custom-call | flops 1073741824 | bytes 1048576 | tf_op jit(solution)/shard_map/pallas_call | solution.py:367
  71.6 13.4 %all_to_all.37.parts_ref = bf16[8,64,256]{2,1,0:T(8,128)(2,1)S(1)} all-to-all(bf16[8,64,256]{2,1,0:T(8,128)(2,1)S(1)} %get-tuple-element.80.refs_0_), channel_id=1, replica_groups=mesh['groups'=2,'segment'=16,'head'=8] {'head'}, dimensions={0} | all-to-all | bytes 524288 | tf_op jit(solution)/shard_map/all_to_all | solution.py:378
  85.1 1.3 collective-permute-start.7
  86.4 3.3 %collective-permute-start.6 = (bf16[32,256]{1,0:T(8,128)(2,1)S(1)}, bf16[32,256]{1,0:T(8,128)(2,1)S(1)}, u32[]{:S(2)}, u32[]{:S(2)}) collective-permute-start(bf16[32,256]{1,0:T(8,128)(2,1)S(1)} %get-tuple-element.83.order_ref.refs_0_), channel_id=1, source_target_pairs={{0,8},{8,16},{16,24},{24,32},{32,40},{40,48},{48,56},{56,64},{64,7... | collective-permute-start | bytes 49160 | tf_op jit(solution)/shard_map/ppermute | solution.py:384
  89.7 2.4 %shard_map.149 = (f32[2,4,256,512]{3,2,1,0:T(8,128)S(1)}, f32[2,256,128]{2,1,0:T(8,128)S(1)}, f32[2,4,256,128]{3,2,1,0:T(8,128)S(1)}, f32[2,256,128]{2,1,0:T(8,1...) custom-call(s32[1]{0:T(128)} %constant.1.clone.1.tick_ref, ...), custom_call_target="tpu_custom_call" | custom-call | flops 1073741824 | bytes 1048576 | tf_op jit(solution)/shard_map/pallas_call | solution.py:367
  92.1 0.0 collective-permute-done.7.got_back_ref
  92.1 0.0 collective-permute-done.6.got_ref
  92.1 14.8 %all_to_all.38.rows_ref = bf16[8,64,256]{2,1,0:T(8,128)(2,1)S(1)} all-to-all(bf16[8,64,256]{2,1,0:T(8,128)(2,1)S(1)} %shard_map.150), channel_id=1, replica_groups=mesh['groups'=2,'segment'=16,'head'=8] {'head'}, dimensions={0} | all-to-all | bytes 524288 | tf_op jit(solution)/shard_map/all_to_all | solution.py:378
  106.9 3.2 %shard_map.151 = (bf16[8,64,256]{2,1,0:T(8,128)(2,1)S(1)}, f32[2,4,256,512]{3,2,1,0:T(8,128)S(1)}, f32[2,256,128]{2,1,0:T(8,128)S(1)}, f32[2,4,256,128]{3,2,1,0:...) custom-call(s32[1]{0:T(128)} %constant.1.clone.1.tick_ref, ...), custom_call_target="tpu_custom_call", output_to_operand_aliasing={{0}: (9, {}), {1}: (10, {}), {2}: (11, {}), {3}: (12, {}), ... | custom-call | flops 1073741824 | bytes 1048576 | tf_op jit(solution)/shard_map/pallas_call | solution.py:367
  110.2 4.5 %shard_map.152 = (bf16[8,64,256]{2,1,0:T(8,128)(2,1)S(1)}, f32[32,256]{1,0:T(8,128)S(1)}, bf16[16,128]{1,0:T(8,128)(2,1)}) custom-call(s32[1]{0:T(128)} %constant.1.clone.1.tick_ref, f32[4,1,512]{2,1,0:T(1,128)S(1)} %bitcast.48, f32[256,256]{1,0:T(8,128)S(1)} %get-tuple-element.63.basis_ref, ...), custom_call_target="tpu_custom_call", output_to_operand_aliasing={{0}: (10, {})} | custom-call | flops 1073741824 | bytes 1048576 | tf_op jit(solution)/shard_map/pallas_call | solution.py:367
  114.7 14.3 %all_to_all.39.parts_ref = bf16[8,64,256]{2,1,0:T(8,128)(2,1)S(1)} all-to-all(bf16[8,64,256]{2,1,0:T(8,128)(2,1)S(1)} %get-tuple-element.100.refs_0_), channel_id=1, replica_groups=mesh['groups'=2,'segment'=16,'head'=8] {'head'}, dimensions={0} | all-to-all | bytes 524288 | tf_op jit(solution)/shard_map/all_to_all | solution.py:378
  129.0 1.3 collective-permute-start.9
  130.3 3.1 %collective-permute-start.8 = (bf16[32,256]{1,0:T(8,128)(2,1)S(1)}, bf16[32,256]{1,0:T(8,128)(2,1)S(1)}, u32[]{:S(2)}, u32[]{:S(2)}) collective-permute-start(bf16[32,256]{1,0:T(8,128)(2,1)S(1)} %get-tuple-element.103.order_ref.refs_1_), channel_id=1, source_target_pairs={{0,8},{8,16},{16,24},{24,32},{32,40},{40,48},{48,56},{56,64},{64,7... | collective-permute-start | bytes 49160 | tf_op jit(solution)/shard_map/ppermute | solution.py:384
  133.4 2.4 %shard_map.154 = (f32[2,4,256,512]{3,2,1,0:T(8,128)S(1)}, f32[2,256,128]{2,1,0:T(8,128)S(1)}, f32[2,4,256,128]{3,2,1,0:T(8,128)S(1)}, f32[2,256,128]{2,1,0:T(8,1...) custom-call(s32[1]{0:T(128)} %constant.0.clone.1.tick_ref, ...), custom_call_target="tpu_custom_call" | custom-call | flops 1073741824 | bytes 1048576 | tf_op jit(solution)/shard_map/pallas_call | solution.py:367
  135.8 0.0 collective-permute-done.9.got_back_ref
  135.8 0.0 collective-permute-done.8.got_ref
  135.9 15.6 %all_to_all.40.rows_ref = bf16[8,64,256]{2,1,0:T(8,128)(2,1)S(1)} all-to-all(bf16[8,64,256]{2,1,0:T(8,128)(2,1)S(1)} %shard_map.155), channel_id=1, replica_groups=mesh['groups'=2,'segment'=16,'head'=8] {'head'}, dimensions={0} | all-to-all | bytes 524288 | tf_op jit(solution)/shard_map/all_to_all | solution.py:378
  151.5 3.3 %shard_map.156 = (bf16[8,64,256]{2,1,0:T(8,128)(2,1)S(1)}, f32[2,4,256,512]{3,2,1,0:T(8,128)S(1)}, f32[2,256,128]{2,1,0:T(8,128)S(1)}, f32[2,4,256,128]{3,2,1,0:...) custom-call(s32[1]{0:T(128)} %constant.0.clone.1.tick_ref, ...), custom_call_target="tpu_custom_call", output_to_operand_aliasing={{0}: (9, {}), {1}: (10, {}), {2}: (11, {}), {3}: (12, {}), ... | custom-call | flops 1073741824 | bytes 1048576 | tf_op jit(solution)/shard_map/pallas_call | solution.py:367
  154.8 4.5 %shard_map.157 = (bf16[8,64,256]{2,1,0:T(8,128)(2,1)S(1)}, f32[32,256]{1,0:T(8,128)S(1)}, bf16[16,128]{1,0:T(8,128)(2,1)}) custom-call(s32[1]{0:T(128)} %constant.0.clone.1.tick_ref, f32[4,1,512]{2,1,0:T(1,128)S(1)} %bitcast.51, f32[256,256]{1,0:T(8,128)S(1)} %get-tuple-element.63.basis_ref, ...), custom_call_target="tpu_custom_call", output_to_operand_aliasing={{0}: (10, {})} | custom-call | flops 1073741824 | bytes 1048576 | tf_op jit(solution)/shard_map/pallas_call | solution.py:367
  159.3 14.1 %all_to_all.41.parts_ref = bf16[8,64,256]{2,1,0:T(8,128)(2,1)S(1)} all-to-all(bf16[8,64,256]{2,1,0:T(8,128)(2,1)S(1)} %get-tuple-element.119), channel_id=1, replica_groups=mesh['groups'=2,'segment'=16,'head'=8] {'head'}, dimensions={0} | all-to-all | bytes 524288 | tf_op jit(solution)/shard_map/all_to_all | solution.py:378
  173.4 0.7 shard_map.158
  (20 shorter events, 0.2 us)
Async XLA Ops:
  0.6 39.2 %copy-start.5 = (bf16[1,512,2048]{2,1,0:T(8,128)(2,1)S(1)}, bf16[1,512,2048]{2,1,0:T(8,128)(2,1)}, u32[]{:S(2)}) copy-start(bf16[1,512,2048]{2,1,0:T(8,128)(2,1)} %param.25) | copy-start | bytes 6291460
  0.6 39.2 %copy-start.7 = (bf16[1,2048,256]{2,1,0:T(8,128)(2,1)S(1)}, bf16[1,2048,256]{2,1,0:T(8,128)(2,1)}, u32[]{:S(2)}) copy-start(bf16[1,2048,256]{2,1,0:T(8,128)(2,1)} %param.20) | copy-start | bytes 3145732
  0.7 39.2 %copy-start.1 = (bf16[1,256,2048]{2,1,0:T(8,128)(2,1)S(1)}, bf16[1,256,2048]{2,1,0:T(8,128)(2,1)}, u32[]{:S(2)}) copy-start(bf16[1,256,2048]{2,1,0:T(8,128)(2,1)} %param.19) | copy-start | bytes 3145732
  0.7 1.2 copy-start.9
  1.9 0.9 copy-start.10
  35.9 8.6 %collective-permute-start.2 = (bf16[96,256]{1,0:T(8,128)(2,1)S(1)}, bf16[96,256]{1,0:T(8,128)(2,1)S(1)}, u32[]{:S(2)}, u32[]{:S(2)}) collective-permute-start(bf16[96,256]{1,0:T(8,128)(2,1)S(1)} %get-tuple-element.64.rows_ref), channel_id=1, source_target_pairs={{24,0},{56,32},{88,64},{120,96},{25,1},{57,33},{89,65},{121,97},{2... | collective-permute-start | bytes 147464 | tf_op jit(solution)/shard_map/ppermute | solution.py:397
  37.2 7.3 %collective-permute-start.1 = (bf16[96,256]{1,0:T(8,128)(2,1)S(1)}, bf16[96,256]{1,0:T(8,128)(2,1)S(1)}, u32[]{:S(2)}, u32[]{:S(2)}) collective-permute-start(bf16[96,256]{1,0:T(8,128)(2,1)S(1)} %get-tuple-element.64.rows_ref), channel_id=1, source_target_pairs={{16,0},{48,32},{80,64},{112,96},{17,1},{49,33},{81,65},{113,97},{1... | collective-permute-start | bytes 147464 | tf_op jit(solution)/shard_map/ppermute | solution.py:397
  38.5 6.0 %collective-permute-start = (bf16[96,256]{1,0:T(8,128)(2,1)S(1)}, bf16[96,256]{1,0:T(8,128)(2,1)S(1)}, u32[]{:S(2)}, u32[]{:S(2)}) collective-permute-start(bf16[96,256]{1,0:T(8,128)(2,1)S(1)} %get-tuple-element.64.rows_ref), channel_id=1, source_target_pairs={{8,0},{40,32},{72,64},{104,96},{9,1},{41,33},{73,65},{105,97},{10,... | collective-permute-start | bytes 147464 | tf_op jit(solution)/shard_map/ppermute | solution.py:397
  39.9 2.2 %copy-start = (bf16[1,2048,512]{2,1,0:T(8,128)(2,1)S(1)}, bf16[1,2048,512]{2,1,0:T(8,128)(2,1)}, u32[]{:S(2)}) copy-start(bf16[1,2048,512]{2,1,0:T(8,128)(2,1)} %param.22) | copy-start | bytes 6291460
  39.9 2.2 %copy-start.3 = (bf16[1,256,256]{2,1,0:T(8,128)(2,1)S(1)}, bf16[1,256,256]{2,1,0:T(8,128)(2,1)}, u32[]{:S(2)}) copy-start(bf16[1,256,256]{2,1,0:T(8,128)(2,1)} %param.15) | copy-start | bytes 393220
  39.9 2.2 %copy-start.4 = (bf16[1,3,256,256]{3,2,1,0:T(8,128)(2,1)S(1)}, bf16[1,3,256,256]{3,2,1,0:T(8,128)(2,1)}, u32[]{:S(2)}) copy-start(bf16[1,3,256,256]{3,2,1,0:T(8,128)(2,1)} %param.17) | copy-start | bytes 1179652
  39.9 2.2 %copy-start.8 = (f32[1,2048]{1,0:T(1,128)S(1)}, f32[1,2048]{1,0:T(1,128)}, u32[]{:S(2)}) copy-start(f32[1,2048]{1,0:T(1,128)} %param.21) | copy-start | bytes 24580
  42.1 6.5 %copy-start.2 = (bf16[3,256,256]{2,1,0:T(8,128)(2,1)S(1)}, bf16[3,256,256]{2,1,0:T(8,128)(2,1)}, u32[]{:S(2)}) copy-start(bf16[3,256,256]{2,1,0:T(8,128)(2,1)} %seed_ref.9) | copy-start | bytes 1179652
  42.1 6.5 %copy-start.6 = (bf16[1,256,256]{2,1,0:T(8,128)(2,1)S(1)}, bf16[1,256,256]{2,1,0:T(8,128)(2,1)}, u32[]{:S(2)}) copy-start(bf16[1,256,256]{2,1,0:T(8,128)(2,1)} %param.16) | copy-start | bytes 393220
  44.6 8.1 %collective-permute-start.5 = (bf16[96,256]{1,0:T(8,128)(2,1)S(1)}, bf16[96,256]{1,0:T(8,128)(2,1)S(1)}, u32[]{:S(2)}, u32[]{:S(2)}) collective-permute-start(bf16[96,256]{1,0:T(8,128)(2,1)S(1)} %get-tuple-element.67.rows_ref), channel_id=1, source_target_pairs={{96,0},{97,1},{98,2},{99,3},{100,4},{101,5},{102,6},{103,7},{224,1... | collective-permute-start | bytes 147464 | tf_op jit(solution)/shard_map/ppermute | solution.py:397
  46.0 9.9 %collective-permute-start.4 = (bf16[96,256]{1,0:T(8,128)(2,1)S(1)}, bf16[96,256]{1,0:T(8,128)(2,1)S(1)}, u32[]{:S(2)}, u32[]{:S(2)}) collective-permute-start(bf16[96,256]{1,0:T(8,128)(2,1)S(1)} %get-tuple-element.67.rows_ref), channel_id=1, source_target_pairs={{64,0},{65,1},{66,2},{67,3},{68,4},{69,5},{70,6},{71,7},{192,128},... | collective-permute-start | bytes 147464 | tf_op jit(solution)/shard_map/ppermute | solution.py:397
  47.3 8.6 %collective-permute-start.3 = (bf16[96,256]{1,0:T(8,128)(2,1)S(1)}, bf16[96,256]{1,0:T(8,128)(2,1)S(1)}, u32[]{:S(2)}, u32[]{:S(2)}) collective-permute-start(bf16[96,256]{1,0:T(8,128)(2,1)S(1)} %get-tuple-element.67.rows_ref), channel_id=1, source_target_pairs={{32,0},{33,1},{34,2},{35,3},{36,4},{37,5},{38,6},{39,7},{160,128},... | collective-permute-start | bytes 147464 | tf_op jit(solution)/shard_map/ppermute | solution.py:397
  85.1 7.0 %collective-permute-start.7 = (bf16[32,256]{1,0:T(8,128)(2,1)S(1)}, bf16[32,256]{1,0:T(8,128)(2,1)S(1)}, u32[]{:S(2)}, u32[]{:S(2)}) collective-permute-start(bf16[32,256]{1,0:T(8,128)(2,1)S(1)} %get-tuple-element.84.refs_2_), channel_id=1, source_target_pairs={{8,0},{16,8},{24,16},{32,24},{40,32},{48,40},{56,48},{64,56},{72,6... | collective-permute-start | bytes 49160 | tf_op jit(solution)/shard_map/ppermute | solution.py:384
  86.4 5.7 %collective-permute-start.6 = (bf16[32,256]{1,0:T(8,128)(2,1)S(1)}, bf16[32,256]{1,0:T(8,128)(2,1)S(1)}, u32[]{:S(2)}, u32[]{:S(2)}) collective-permute-start(bf16[32,256]{1,0:T(8,128)(2,1)S(1)} %get-tuple-element.83.order_ref.refs_0_), channel_id=1, source_target_pairs={{0,8},{8,16},{16,24},{24,32},{32,40},{40,48},{48,56},{56,64},{64,7... | collective-permute-start | bytes 49160 | tf_op jit(solution)/shard_map/ppermute | solution.py:384
  129.0 6.8 %collective-permute-start.9 = (bf16[32,256]{1,0:T(8,128)(2,1)S(1)}, bf16[32,256]{1,0:T(8,128)(2,1)S(1)}, u32[]{:S(2)}, u32[]{:S(2)}) collective-permute-start(bf16[32,256]{1,0:T(8,128)(2,1)S(1)} %get-tuple-element.104.refs_3_), channel_id=1, source_target_pairs={{8,0},{16,8},{24,16},{32,24},{40,32},{48,40},{56,48},{64,56},{72,6... | collective-permute-start | bytes 49160 | tf_op jit(solution)/shard_map/ppermute | solution.py:384
  130.3 5.5 %collective-permute-start.8 = (bf16[32,256]{1,0:T(8,128)(2,1)S(1)}, bf16[32,256]{1,0:T(8,128)(2,1)S(1)}, u32[]{:S(2)}, u32[]{:S(2)}) collective-permute-start(bf16[32,256]{1,0:T(8,128)(2,1)S(1)} %get-tuple-element.103.order_ref.refs_1_), channel_id=1, source_target_pairs={{0,8},{8,16},{16,24},{24,32},{32,40},{40,48},{48,56},{56,64},{64,7... | collective-permute-start | bytes 49160 | tf_op jit(solution)/shard_map/ppermute | solution.py:384

commit v5 on v4

--- a/solution.py
+++ b/solution.py
@@ -67,27 +67,34 @@
     ]
 
 
+def folded_lanes(matrix):
+    total = matrix[:, :LANES]
+    for at in range(LANES, matrix.shape[1], LANES):
+        total += matrix[:, at : at + LANES]
+    return total
+
+
 def spread(coeffs, gain_ref, expand_ref, query_ref, kv_ref, state):
     hidden, scale, queries, keys, values, _ = state
     count = hidden.shape[0]
     span = coeffs.shape[0]
-    squares = jnp.zeros((span, 1), WIDE)
+    squares = jnp.zeros((span, LANES), WIDE)
+    wide_q = jnp.zeros((span, query_ref.shape[1]), WIDE)
+    wide_kv = jnp.zeros((span, kv_ref.shape[1]), WIDE)
     for place in range(count):
         part = dot(coeffs, expand_ref[:, block(place, CHUNK)])
         hidden[place] = part
-        squares += jnp.sum(part * part, axis=-1, keepdims=True)
-    scaling = lax.rsqrt(squares / (count * CHUNK) + EPS)
-    scale[...] = jnp.broadcast_to(scaling, scale.shape)
-    wide_q = jnp.zeros((span, query_ref.shape[1]), WIDE)
-    wide_kv = jnp.zeros((span, kv_ref.shape[1]), WIDE)
-    for place in range(count):
-        normed = (hidden[place] * scaling * gain_ref[place]).astype(LOW)
-        wide_q += dot(normed, query_ref[block(place, CHUNK), :])
-        wide_kv += dot(normed, kv_ref[block(place, CHUNK), :])
+        squares += folded_lanes(part * part)
+        gained = (part * gain_ref[place]).astype(LOW)
+        wide_q += dot(gained, query_ref[block(place, CHUNK), :])
+        wide_kv += dot(gained, kv_ref[block(place, CHUNK), :])
+    mean = jnp.sum(squares, axis=-1, keepdims=True) / (count * CHUNK)
+    scaling = jnp.broadcast_to(lax.rsqrt(mean + EPS), scale.shape)
+    scale[...] = scaling
     for head in range(queries.shape[0]):
-        queries[head] = wide_q[:, head * HEAD_SIZE : (head + 1) * HEAD_SIZE]
-    keys[...] = wide_kv[:, :HEAD_SIZE]
-    values[...] = wide_kv[:, HEAD_SIZE:].astype(LOW)
+        queries[head] = wide_q[:, head * HEAD_SIZE : (head + 1) * HEAD_SIZE] * scaling
+    keys[...] = wide_kv[:, :HEAD_SIZE] * scaling
+    values[...] = (wide_kv[:, HEAD_SIZE:] * scaling).astype(LOW)
 
 
 def hat(matrix):
@@ -100,7 +107,7 @@
     column = lax.broadcasted_iota(jnp.int32, (rows, rows), 1)
     row = lax.broadcasted_iota(jnp.int32, (rows, rows), 0)
     weights = jnp.where(column <= row, jnp.exp(scores), 0.0)
-    return weights / jnp.sum(weights, axis=-1, keepdims=True)
+    return weights * (1.0 / jnp.sum(weights, axis=-1, keepdims=True))
 
 
 def attend(folded_ref, state):
@@ -140,14 +147,15 @@
         [norm_back(keys_here, grad_khat).astype(LOW), grad_values.astype(LOW)], axis=1
     )
     scaling = scale[:, :1]
-    inner = jnp.zeros((keys_here.shape[0], 1), WIDE)
+    inner = jnp.zeros((keys_here.shape[0], LANES), WIDE)
     for place in range(count):
         grad_normed = dot_back(grad_q[...], query_ref[block(place, CHUNK), :]) + dot_back(
             grad_kv, kv_ref[block(place, CHUNK), :]
         )
         weighted = grad_normed * gain_ref[place]
         weighted_ref[place] = weighted
-        inner += jnp.sum(weighted * hidden[place], axis=-1, keepdims=True)
+        inner += folded_lanes(weighted * hidden[place])
+    inner = jnp.sum(inner, axis=-1, keepdims=True)
     factor = scaling**3 * (inner / (count * CHUNK))
     total = jnp.zeros(grads.shape, WIDE)
     for place in range(count):
@@ -249,31 +257,39 @@
     token_ref[...] = jnp.zeros(token_ref.shape, LOW)
 
 
-def pick_kernel(ids_ref, table_ref, out_ref):
+def pick_kernel(ids_hbm, table_hbm, out_ref, ids_ref, table_ref, hits_ref, sems):
+    ids_copy = pltpu.make_async_copy(ids_hbm, ids_ref, sems.at[0])
+    table_copy = pltpu.make_async_copy(table_hbm, table_ref, sems.at[1])
+    ids_copy.start()
+    table_copy.start()
     rows = table_ref.shape[0]
     full = rows // LANES * LANES
     ticks, span = ids_ref.shape
     share = out_ref.shape[1] // ticks
     own = lax.axis_index("segment") * lax.axis_size("head") + lax.axis_index("head")
     lane = lax.broadcasted_iota(jnp.int32, (LANES, LANES), 1).astype(WIDE)
-
-    def chosen(names, at):
-        return jnp.where(names == lane + float(at), 1.0, 0.0).astype(LOW)
-
-    for tick in range(ticks):
-        for at in range(0, span, LANES):
-            local = (ids_ref[tick : tick + 1, at : at + LANES] - own * rows).astype(WIDE)
-            names = jnp.broadcast_to(local, (LANES, LANES)).T
-            hits = jnp.concatenate([chosen(names, k) for k in range(0, full, LANES)], axis=1)
-            found = dot(hits, table_ref[pl.ds(0, full), :])
-            if rows > full:
-                found += dot(
-                    chosen(names, full)[:, : rows - full], table_ref[pl.ds(full, rows - full), :]
-                )
-            for place in range(LANES // share):
-                out_ref[at // share + place, pl.ds(tick * share, share), :] = found[
-                    place * share : (place + 1) * share
-                ].astype(LOW)
+    ids_copy.wait()
+    for place in range(ticks * span // LANES):
+        tick, at = place * LANES // span, place * LANES % span
+        local = (ids_ref[tick : tick + 1, at : at + LANES] - own * rows).astype(WIDE)
+        names = jnp.broadcast_to(local, (LANES, LANES)).T
+        for first in range(0, rows, LANES):
+            hits_ref[pl.ds(place * LANES, LANES), pl.ds(first, LANES)] = jnp.where(
+                names == lane + float(first), 1.0, 0.0
+            ).astype(LOW)
+    table_copy.wait()
+    for place in range(ticks * span // LANES):
+        tick, at = place * LANES // span, place * LANES % span
+        here = pl.ds(place * LANES, LANES)
+        found = dot(hits_ref[here, pl.ds(0, full)], table_ref[pl.ds(0, full), :])
+        if rows > full:
+            found += dot(
+                hits_ref[here, pl.ds(full, rows - full)], table_ref[pl.ds(full, rows - full), :]
+            )
+        for piece in range(LANES // share):
+            out_ref[at // share + piece, pl.ds(tick * share, share), :] = found[
+                piece * share : (piece + 1) * share
+            ].astype(LOW)
 
 
 def sum_kernel(parts_ref, out_ref, order_ref):
@@ -291,6 +307,9 @@
         total += ref[...]
     out_ref[...] = total
     for ref in tiles:
+        if len(ref.shape) == 2:
+            ref[...] = total[: ref.shape[0]]
+            continue
         for place in range(ref.shape[0]):
             ref[place] = total[: ref.shape[1]]
 
@@ -315,13 +334,24 @@
         copy.wait()
 
 
-def finish_kernel(parts_ref, direct_ref, direct_back_ref, out_ref, out_back_ref):
+def total_of(parts_ref, at, direct_ref):
     share = direct_ref.shape[0]
-    for at, direct, out in ((0, direct_ref, out_ref), (share, direct_back_ref, out_back_ref)):
-        summed = parts_ref[0, pl.ds(at, share), :].astype(WIDE)
-        for place in range(1, parts_ref.shape[0]):
-            summed += parts_ref[place, pl.ds(at, share), :].astype(WIDE)
-        out[...] = (summed + direct[...]).astype(LOW)
+    summed = parts_ref[0, pl.ds(at, share), :].astype(WIDE)
+    for place in range(1, parts_ref.shape[0]):
+        summed += parts_ref[place, pl.ds(at, share), :].astype(WIDE)
+    return (summed + direct_ref[...]).astype(LOW)
+
+
+def finish_kernel(
+    parts_ref, direct_ref, direct_back_ref, out_ref, out_back_ref, first_ref, second_ref
+):
+    ahead = total_of(parts_ref, 0, direct_ref)
+    back = total_of(parts_ref, direct_ref.shape[0], direct_back_ref)
+    even = lax.axis_index("segment") % 2 == 0
+    out_ref[...] = ahead
+    out_back_ref[...] = back
+    first_ref[...] = jnp.where(even, ahead, back)
+    second_ref[...] = jnp.where(even, back, ahead)
 
 
 def last_kernel(count, parts_ref, direct_ref, direct_back_ref, *refs):
@@ -330,18 +360,20 @@
     for place in range(count):
         out_ref[0, place] = before[place][...]
         out_back_ref[0, place] = before[count + place][...]
-    finish_kernel(
-        parts_ref, direct_ref, direct_back_ref, out_ref.at[0, count], out_back_ref.at[0, count]
-    )
-
-
-def mix_kernel(tick_ref, got_ref, got_back_ref, later_ref, seed_ref, token_ref, out_ref):
-    share = got_ref.shape[0]
+    out_ref[0, count] = total_of(parts_ref, 0, direct_ref)
+    out_back_ref[0, count] = total_of(parts_ref, share, direct_back_ref)
+
+
+def mix_kernel(tick_ref, first_ref, second_ref, later_ref, seed_ref, token_ref, out_ref):
+    share = first_ref.shape[0]
     tick = tick_ref[0]
     segment, last = place_in_line()
     later = later_ref[pl.ds(pl.multiple_of(tick * share, share), share), :]
-    rows = jnp.where(segment == 0, later, got_ref[...])
-    rows_back = jnp.where(segment == last, own_rows(seed_ref.at[tick], share), got_back_ref[...])
+    even = segment % 2 == 0
+    got = jnp.where(even, second_ref[...], first_ref[...])
+    got_back = jnp.where(even, first_ref[...], second_ref[...])
+    rows = jnp.where(segment == 0, later, got)
+    rows_back = jnp.where(segment == last, own_rows(seed_ref.at[tick], share), got_back)
     for place in range(out_ref.shape[0]):
         out_ref[place, pl.ds(0, share), :] = rows
         out_ref[place, pl.ds(share, share), :] = rows_back
@@ -378,10 +410,10 @@
     return lax.all_to_all(tiles, axis, split_axis=0, concat_axis=0, tiled=True)
 
 
-def passed_along(x, axis, by):
+def swapped(x, axis, start):
     length = lax.axis_size(axis)
-    pairs = [(i, i + by) for i in range(length) if 0 <= i + by < length]
-    return lax.ppermute(x, axis, pairs)
+    pairs = [(i, i + 1) for i in range(start, length - 1, 2)]
+    return lax.ppermute(x, axis, pairs + [(j, i) for i, j in pairs])
 
 
 def sent_down(x, axis, radix, step):
@@ -436,9 +468,19 @@
     work = 2 * span * width * (rank + queries + 2 * HEAD_SIZE)
     lines = pltpu.VMEM((span, rank), LOW)
 
-    picked = call(pick_kernel, shape_of((parts, ticks * share, rank), LOW), [VMEM] * 2, flops=work)(
-        token_ids, embed_table
-    )
+    table_rows = embed_table.shape[0]
+    picked = call(
+        pick_kernel,
+        shape_of((parts, ticks * share, rank), LOW),
+        [HBM] * 2,
+        [
+            pltpu.VMEM(token_ids.shape, jnp.int32),
+            pltpu.VMEM(embed_table.shape, LOW),
+            pltpu.VMEM((ticks * span, -(-table_rows // LANES) * LANES), LOW),
+            pltpu.SemaphoreType.DMA((2,)),
+        ],
+        flops=work,
+    )(token_ids, embed_table)
     rows, order = call(sum_kernel, (lot, piece), [VMEM], limit=4)(exchanged(picked, "head"))
 
     def folding(order):
@@ -487,14 +529,14 @@
     got = sent_down(rows, "segment", RADIX, 1)
     basis, folded, kv = folding(order)
     weights = (expand[0], w_query[0], kv, folded)
-    state, done = kept_of(0, order)
-    rows, spare, out = call(
+    rows, order, spare, out = call(
         functools.partial(join_kernel, len(got)),
-        (lot, payload, payload),
+        (lot, piece, payload, payload),
         [VMEM] * (2 + len(got)),
         limit=4,
-    )(rows, *got, done)
+    )(rows, *got, basis)
     got = sent_down(rows, "segment", RADIX, RADIX)
+    state, _ = kept_of(0, order)
     out, direct_back, done = backward(0, spare, out, state)
     rows, tiles = call(
         functools.partial(join_kernel, len(got)), (lot, payload), [VMEM] * (2 + len(got)), limit=4
@@ -503,15 +545,14 @@
 
     shares = []
     for tick in range(1, ticks):
-        sent, sent_back = call(finish_kernel, (piece, piece), [VMEM] * 3, limit=4)(
+        sent, sent_back, first, second = call(finish_kernel, (piece,) * 4, [VMEM] * 3, limit=4)(
             exchanged(out, "head"), direct, direct_back
         )
         shares.append((sent, sent_back))
-        arrived = passed_along(sent, "segment", 1)
-        arrived_back = passed_along(sent_back, "segment", -1)
+        first, second = swapped(first, "segment", 0), swapped(second, "segment", 1)
         state, done = kept_of(tick, sent)
         mixed = call(mix_kernel, payload, [SMEM] + [VMEM] * 5, limit=4)(
-            number(tick), arrived, arrived_back, rows, seed_grad, done
+            number(tick), first, second, rows, seed_grad, done
         )
         gathered = exchanged(mixed, "head")
         out, state, direct = forward(tick, gathered, out, state)

time: 175 us -> 169 us (0.966)
  the two profiles are of different devices: /device:TPU:514 before, /device:TPU:544 now
where the time goes in v5:
time: 169 us
  blocking collectives  108 us (64%)
  Pallas kernels  34.2 us (20%)
  starting transfers between devices  22.2 us (13%)
  waiting for transfers between devices  3.15 us (2%)
    all_to_all x7, blocking collectives, exchanged(): return lax.all_to_all(tiles, axis, split_axis=0, concat_axis=0, tiled=True)  108 us
    pallas_call x19, Pallas kernels, run(): kernel(*[pltpu.with_memory_space_constraint(arg, pltpu.HBM) if spec is HB...  34.2 us
    ppermute x6, starting transfers between devices, sent_down(): got.append(lax.ppermute(x, axis, pairs))  17.8 us
    ppermute x4, starting transfers between devices, swapped(): return lax.ppermute(x, axis, pairs + [(j, i) for i, j in pairs])  4.37 us
  transfers between devices with their start and end apart: 10, of which 3 were waited for; matrix products, arithmetic and copies ran while one was open for 0% of the time, Pallas kernels for 8%

profile of v5, /device:TPU:544, one launch (start us, length us, event | category | flops | bytes accessed | tf_op | source)
XLA Modules:
  0.0 168.7 jit_solution(8585720519739329352)
XLA Ops:
  0.6 0.0 copy-start.5
  0.6 0.0 copy-start.7
  0.7 2.1 %shard_map.140 = bf16[8,96,256]{2,1,0:T(8,128)(2,1)S(1)} custom-call(s32[3,256]{1,0:T(4,128)} %ids_hbm.1, bf16[1187,256]{1,0:T(8,128)(2,1)} %table_hbm.1), custom_call_target="tpu_custom_call" | custom-call | flops 1073741824 | bytes 1048576 | tf_op jit(solution)/shard_map/pallas_call | solution.py:399
  2.7 21.9 %all_to_all.35.parts_ref = bf16[8,96,256]{2,1,0:T(8,128)(2,1)S(1)} all-to-all(bf16[8,96,256]{2,1,0:T(8,128)(2,1)S(1)} %shard_map.140), channel_id=1, replica_groups=mesh['groups'=2,'segment'=16,'head'=8] {'head'}, dimensions={0} | all-to-all | bytes 786432 | tf_op jit(solution)/shard_map/all_to_all | solution.py:410
  24.6 1.3 collective-permute-start.2
  25.9 1.3 collective-permute-start.1
  27.3 1.3 collective-permute-start
  28.6 0.0 copy-start
  28.6 0.0 copy-start.3
  28.6 0.0 copy-start.4
  28.6 0.0 copy-start.8
  28.7 2.1 %shard_map.142 = (f32[256,256]{1,0:T(8,128)S(1)}, bf16[512,256]{1,0:T(8,128)(2,1)S(1)}, bf16[2048,256]{1,0:T(8,128)(2,1)S(1)}) custom-call(bf16[32,256]{1,0:T(8,128)(2,1)S(1)} %get-tuple-element.66.order_ref, bf16[256,2048]{1,0:T(8,128)(2,1)S(1)} %bitcast.19, bf16[2048,256]{1,0:T(8,128)(2,1)S(1)} %bitcast.42, bf16[512,2048]{1,0:T(8,128)(2,1)S(1)} %bitcast.38, ...), custom_call_target="tpu_custom_call" | custom-call | flops 805306368 | bytes 1048576 | tf_op jit(solution)/shard_map/pallas_call | solution.py:399
  30.8 0.0 collective-permute-done.2.refs_2_
  30.8 1.2 collective-permute-done.1.refs_1_
  32.0 0.0 collective-permute-done.refs_0_
  32.0 0.1 shard_map.143
  32.0 0.7 collective-permute-start.5
  32.7 0.7 collective-permute-start.4
  33.4 12.6 %collective-permute-start.3 = (bf16[96,256]{1,0:T(8,128)(2,1)S(1)}, bf16[96,256]{1,0:T(8,128)(2,1)S(1)}, u32[]{:S(2)}, u32[]{:S(2)}) collective-permute-start(bf16[96,256]{1,0:T(8,128)(2,1)S(1)} %get-tuple-element.69.rows_ref), channel_id=1, source_target_pairs={{32,0},{33,1},{34,2},{35,3},{36,4},{37,5},{38,6},{39,7},{160,128},... | collective-permute-start | bytes 147464 | tf_op jit(solution)/shard_map/ppermute | solution.py:429
  46.0 0.0 copy-start.2
  46.0 0.0 copy-start.6
  46.0 2.6 %shard_map.144 = (f32[2,4,256,512]{3,2,1,0:T(8,128)S(1)}, f32[2,256,128]{2,1,0:T(8,128)S(1)}, f32[2,4,256,128]{3,2,1,0:T(8,128)S(1)}, f32[2,256,128]{2,1,0:T(8,1...) custom-call(s32[1]{0:T(128)} %constant.2.clone.1.tick_ref, ...), custom_call_target="tpu_custom_call" | custom-call | flops 1073741824 | bytes 1048576 | tf_op jit(solution)/shard_map/pallas_call | solution.py:399
  48.6 4.2 %shard_map.145 = (bf16[8,64,256]{2,1,0:T(8,128)(2,1)S(1)}, f32[32,256]{1,0:T(8,128)S(1)}, bf16[16,128]{1,0:T(8,128)(2,1)S(1)}) custom-call(s32[1]{0:T(128)} %constant.2.clone.1.tick_ref, f32[4,1,512]{2,1,0:T(1,128)S(1)} %bitcast.44, f32[256,256]{1,0:T(8,128)S(1)} %get-tuple-element.67.refs_3_.basis_ref, ...), custom_call_target="tpu_custom_call", output_to_operand_aliasing={{0}: (10, {})} | custom-call | flops 1073741824 | bytes 1048576 | tf_op jit(solution)/shard_map/pallas_call | solution.py:399
  52.8 0.0 collective-permute-done.5.refs_2_
  52.8 0.0 collective-permute-done.4.refs_1_
  52.8 0.0 collective-permute-done.3.refs_0_
  52.9 13.8 %all_to_all.36.rows_ref = bf16[8,64,256]{2,1,0:T(8,128)(2,1)S(1)} all-to-all(bf16[8,64,256]{2,1,0:T(8,128)(2,1)S(1)} %get-tuple-element.82), channel_id=1, replica_groups=mesh['groups'=2,'segment'=16,'head'=8] {'head'}, dimensions={0} | all-to-all | bytes 524288 | tf_op jit(solution)/shard_map/all_to_all | solution.py:410
  66.7 3.0 %shard_map.147 = (bf16[8,64,256]{2,1,0:T(8,128)(2,1)S(1)}, f32[2,4,256,512]{3,2,1,0:T(8,128)S(1)}, f32[2,256,128]{2,1,0:T(8,128)S(1)}, f32[2,4,256,128]{3,2,1,0:...) custom-call(s32[1]{0:T(128)} %constant.2.clone.1.tick_ref, ...), custom_call_target="tpu_custom_call", output_to_operand_aliasing={{0}: (9, {}), {1}: (10, {}), {2}: (11, {}), {3}: (12, {}), ... | custom-call | flops 1073741824 | bytes 1048576 | tf_op jit(solution)/shard_map/pallas_call | solution.py:399
  69.7 13.2 %all_to_all.37.parts_ref = bf16[8,64,256]{2,1,0:T(8,128)(2,1)S(1)} all-to-all(bf16[8,64,256]{2,1,0:T(8,128)(2,1)S(1)} %get-tuple-element.84.refs_0_), channel_id=1, replica_groups=mesh['groups'=2,'segment'=16,'head'=8] {'head'}, dimensions={0} | all-to-all | bytes 524288 | tf_op jit(solution)/shard_map/all_to_all | solution.py:410
  82.9 0.1 collective-permute-start.6
  83.1 2.1 %collective-permute-start.7 = (bf16[32,256]{1,0:T(8,128)(2,1)S(1)}, bf16[32,256]{1,0:T(8,128)(2,1)S(1)}, u32[]{:S(2)}, u32[]{:S(2)}) collective-permute-start(bf16[32,256]{1,0:T(8,128)(2,1)S(1)} %get-tuple-element.88), channel_id=1, source_target_pairs={{8,16},{24,32},{40,48},{56,64},{72,80},{88,96},{104,112},{16,8},{3... | collective-permute-start | bytes 49160 | tf_op jit(solution)/shard_map/ppermute | solution.py:416
  85.2 2.1 %shard_map.149 = (f32[2,4,256,512]{3,2,1,0:T(8,128)S(1)}, f32[2,256,128]{2,1,0:T(8,128)S(1)}, f32[2,4,256,128]{3,2,1,0:T(8,128)S(1)}, f32[2,256,128]{2,1,0:T(8,1...) custom-call(s32[1]{0:T(128)} %constant.1.clone.1.tick_ref, ...), custom_call_target="tpu_custom_call" | custom-call | flops 1073741824 | bytes 1048576 | tf_op jit(solution)/shard_map/pallas_call | solution.py:399
  87.3 0.0 collective-permute-done.6.first_ref
  87.3 0.9 collective-permute-done.7.second_ref
  88.2 15.2 %all_to_all.38.rows_ref = bf16[8,64,256]{2,1,0:T(8,128)(2,1)S(1)} all-to-all(bf16[8,64,256]{2,1,0:T(8,128)(2,1)S(1)} %shard_map.150), channel_id=1, replica_groups=mesh['groups'=2,'segment'=16,'head'=8] {'head'}, dimensions={0} | all-to-all | bytes 524288 | tf_op jit(solution)/shard_map/all_to_all | solution.py:410
  103.4 3.0 %shard_map.151 = (bf16[8,64,256]{2,1,0:T(8,128)(2,1)S(1)}, f32[2,4,256,512]{3,2,1,0:T(8,128)S(1)}, f32[2,256,128]{2,1,0:T(8,128)S(1)}, f32[2,4,256,128]{3,2,1,0:...) custom-call(s32[1]{0:T(128)} %constant.1.clone.1.tick_ref, ...), custom_call_target="tpu_custom_call", output_to_operand_aliasing={{0}: (9, {}), {1}: (10, {}), {2}: (11, {}), {3}: (12, {}), ... | custom-call | flops 1073741824 | bytes 1048576 | tf_op jit(solution)/shard_map/pallas_call | solution.py:399
  106.5 4.6 %shard_map.152 = (bf16[8,64,256]{2,1,0:T(8,128)(2,1)S(1)}, f32[32,256]{1,0:T(8,128)S(1)}, bf16[16,128]{1,0:T(8,128)(2,1)}) custom-call(s32[1]{0:T(128)} %constant.1.clone.1.tick_ref, f32[4,1,512]{2,1,0:T(1,128)S(1)} %bitcast.48, f32[256,256]{1,0:T(8,128)S(1)} %get-tuple-element.67.refs_3_.basis_ref, ...), custom_call_target="tpu_custom_call", output_to_operand_aliasing={{0}: (10, {})} | custom-call | flops 1073741824 | bytes 1048576 | tf_op jit(solution)/shard_map/pallas_call | solution.py:399
  111.1 14.8 %all_to_all.39.parts_ref = bf16[8,64,256]{2,1,0:T(8,128)(2,1)S(1)} all-to-all(bf16[8,64,256]{2,1,0:T(8,128)(2,1)S(1)} %get-tuple-element.105.refs_0_), channel_id=1, replica_groups=mesh['groups'=2,'segment'=16,'head'=8] {'head'}, dimensions={0} | all-to-all | bytes 524288 | tf_op jit(solution)/shard_map/all_to_all | solution.py:410
  125.9 0.1 collective-permute-start.8
  126.1 2.0 %collective-permute-start.9 = (bf16[32,256]{1,0:T(8,128)(2,1)S(1)}, bf16[32,256]{1,0:T(8,128)(2,1)S(1)}, u32[]{:S(2)}, u32[]{:S(2)}) collective-permute-start(bf16[32,256]{1,0:T(8,128)(2,1)S(1)} %get-tuple-element.109), channel_id=1, source_target_pairs={{8,16},{24,32},{40,48},{56,64},{72,80},{88,96},{104,112},{16,8},{3... | collective-permute-start | bytes 49160 | tf_op jit(solution)/shard_map/ppermute | solution.py:416
  128.0 2.1 %shard_map.154 = (f32[2,4,256,512]{3,2,1,0:T(8,128)S(1)}, f32[2,256,128]{2,1,0:T(8,128)S(1)}, f32[2,4,256,128]{3,2,1,0:T(8,128)S(1)}, f32[2,256,128]{2,1,0:T(8,1...) custom-call(s32[1]{0:T(128)} %constant.0.clone.1.tick_ref, ...), custom_call_target="tpu_custom_call" | custom-call | flops 1073741824 | bytes 1048576 | tf_op jit(solution)/shard_map/pallas_call | solution.py:399
  130.1 0.0 collective-permute-done.8.first_ref
  130.1 1.1 collective-permute-done.9.second_ref
  131.2 15.3 %all_to_all.40.rows_ref = bf16[8,64,256]{2,1,0:T(8,128)(2,1)S(1)} all-to-all(bf16[8,64,256]{2,1,0:T(8,128)(2,1)S(1)} %shard_map.155), channel_id=1, replica_groups=mesh['groups'=2,'segment'=16,'head'=8] {'head'}, dimensions={0} | all-to-all | bytes 524288 | tf_op jit(solution)/shard_map/all_to_all | solution.py:410
  146.4 3.0 %shard_map.156 = (bf16[8,64,256]{2,1,0:T(8,128)(2,1)S(1)}, f32[2,4,256,512]{3,2,1,0:T(8,128)S(1)}, f32[2,256,128]{2,1,0:T(8,128)S(1)}, f32[2,4,256,128]{3,2,1,0:...) custom-call(s32[1]{0:T(128)} %constant.0.clone.1.tick_ref, ...), custom_call_target="tpu_custom_call", output_to_operand_aliasing={{0}: (9, {}), {1}: (10, {}), {2}: (11, {}), {3}: (12, {}), ... | custom-call | flops 1073741824 | bytes 1048576 | tf_op jit(solution)/shard_map/pallas_call | solution.py:399
  149.5 4.6 %shard_map.157 = (bf16[8,64,256]{2,1,0:T(8,128)(2,1)S(1)}, f32[32,256]{1,0:T(8,128)S(1)}, bf16[16,128]{1,0:T(8,128)(2,1)}) custom-call(s32[1]{0:T(128)} %constant.0.clone.1.tick_ref, f32[4,1,512]{2,1,0:T(1,128)S(1)} %bitcast.51, f32[256,256]{1,0:T(8,128)S(1)} %get-tuple-element.67.refs_3_.basis_ref, ...), custom_call_target="tpu_custom_call", output_to_operand_aliasing={{0}: (10, {})} | custom-call | flops 1073741824 | bytes 1048576 | tf_op jit(solution)/shard_map/pallas_call | solution.py:399
  154.1 13.9 %all_to_all.41.parts_ref = bf16[8,64,256]{2,1,0:T(8,128)(2,1)S(1)} all-to-all(bf16[8,64,256]{2,1,0:T(8,128)(2,1)S(1)} %get-tuple-element.125), channel_id=1, replica_groups=mesh['groups'=2,'segment'=16,'head'=8] {'head'}, dimensions={0} | all-to-all | bytes 524288 | tf_op jit(solution)/shard_map/all_to_all | solution.py:410
  168.0 0.7 shard_map.158
  (16 shorter events, 0.2 us)
Async XLA Ops:
  0.6 27.9 %copy-start.5 = (bf16[1,512,2048]{2,1,0:T(8,128)(2,1)S(1)}, bf16[1,512,2048]{2,1,0:T(8,128)(2,1)}, u32[]{:S(2)}) copy-start(bf16[1,512,2048]{2,1,0:T(8,128)(2,1)} %param.25) | copy-start | bytes 6291460
  0.6 27.9 %copy-start.7 = (bf16[1,2048,256]{2,1,0:T(8,128)(2,1)S(1)}, bf16[1,2048,256]{2,1,0:T(8,128)(2,1)}, u32[]{:S(2)}) copy-start(bf16[1,2048,256]{2,1,0:T(8,128)(2,1)} %param.20) | copy-start | bytes 3145732
  0.7 27.9 %copy-start.1 = (bf16[1,256,2048]{2,1,0:T(8,128)(2,1)S(1)}, bf16[1,256,2048]{2,1,0:T(8,128)(2,1)}, u32[]{:S(2)}) copy-start(bf16[1,256,2048]{2,1,0:T(8,128)(2,1)} %param.19) | copy-start | bytes 3145732
  24.6 6.1 %collective-permute-start.2 = (bf16[96,256]{1,0:T(8,128)(2,1)S(1)}, bf16[96,256]{1,0:T(8,128)(2,1)S(1)}, u32[]{:S(2)}, u32[]{:S(2)}) collective-permute-start(bf16[96,256]{1,0:T(8,128)(2,1)S(1)} %get-tuple-element.68.rows_ref), channel_id=1, source_target_pairs={{24,0},{56,32},{88,64},{120,96},{25,1},{57,33},{89,65},{121,97},{2... | collective-permute-start | bytes 147464 | tf_op jit(solution)/shard_map/ppermute | solution.py:429
  25.9 6.0 %collective-permute-start.1 = (bf16[96,256]{1,0:T(8,128)(2,1)S(1)}, bf16[96,256]{1,0:T(8,128)(2,1)S(1)}, u32[]{:S(2)}, u32[]{:S(2)}) collective-permute-start(bf16[96,256]{1,0:T(8,128)(2,1)S(1)} %get-tuple-element.68.rows_ref), channel_id=1, source_target_pairs={{16,0},{48,32},{80,64},{112,96},{17,1},{49,33},{81,65},{113,97},{1... | collective-permute-start | bytes 147464 | tf_op jit(solution)/shard_map/ppermute | solution.py:429
  27.3 4.7 %collective-permute-start = (bf16[96,256]{1,0:T(8,128)(2,1)S(1)}, bf16[96,256]{1,0:T(8,128)(2,1)S(1)}, u32[]{:S(2)}, u32[]{:S(2)}) collective-permute-start(bf16[96,256]{1,0:T(8,128)(2,1)S(1)} %get-tuple-element.68.rows_ref), channel_id=1, source_target_pairs={{8,0},{40,32},{72,64},{104,96},{9,1},{41,33},{73,65},{105,97},{10,... | collective-permute-start | bytes 147464 | tf_op jit(solution)/shard_map/ppermute | solution.py:429
  28.6 17.4 %copy-start = (bf16[1,2048,512]{2,1,0:T(8,128)(2,1)S(1)}, bf16[1,2048,512]{2,1,0:T(8,128)(2,1)}, u32[]{:S(2)}) copy-start(bf16[1,2048,512]{2,1,0:T(8,128)(2,1)} %param.22) | copy-start | bytes 6291460
  28.6 17.4 %copy-start.3 = (bf16[1,256,256]{2,1,0:T(8,128)(2,1)S(1)}, bf16[1,256,256]{2,1,0:T(8,128)(2,1)}, u32[]{:S(2)}) copy-start(bf16[1,256,256]{2,1,0:T(8,128)(2,1)} %param.15) | copy-start | bytes 393220
  28.6 17.4 %copy-start.4 = (bf16[1,3,256,256]{3,2,1,0:T(8,128)(2,1)S(1)}, bf16[1,3,256,256]{3,2,1,0:T(8,128)(2,1)}, u32[]{:S(2)}) copy-start(bf16[1,3,256,256]{3,2,1,0:T(8,128)(2,1)} %param.17) | copy-start | bytes 1179652
  28.6 17.3 %copy-start.8 = (f32[1,2048]{1,0:T(1,128)S(1)}, f32[1,2048]{1,0:T(1,128)}, u32[]{:S(2)}) copy-start(f32[1,2048]{1,0:T(1,128)} %param.21) | copy-start | bytes 24580
  32.0 20.8 %collective-permute-start.5 = (bf16[96,256]{1,0:T(8,128)(2,1)S(1)}, bf16[96,256]{1,0:T(8,128)(2,1)S(1)}, u32[]{:S(2)}, u32[]{:S(2)}) collective-permute-start(bf16[96,256]{1,0:T(8,128)(2,1)S(1)} %get-tuple-element.69.rows_ref), channel_id=1, source_target_pairs={{96,0},{97,1},{98,2},{99,3},{100,4},{101,5},{102,6},{103,7},{224,1... | collective-permute-start | bytes 147464 | tf_op jit(solution)/shard_map/ppermute | solution.py:429
  32.7 20.1 %collective-permute-start.4 = (bf16[96,256]{1,0:T(8,128)(2,1)S(1)}, bf16[96,256]{1,0:T(8,128)(2,1)S(1)}, u32[]{:S(2)}, u32[]{:S(2)}) collective-permute-start(bf16[96,256]{1,0:T(8,128)(2,1)S(1)} %get-tuple-element.69.rows_ref), channel_id=1, source_target_pairs={{64,0},{65,1},{66,2},{67,3},{68,4},{69,5},{70,6},{71,7},{192,128},... | collective-permute-start | bytes 147464 | tf_op jit(solution)/shard_map/ppermute | solution.py:429
  33.4 19.5 %collective-permute-start.3 = (bf16[96,256]{1,0:T(8,128)(2,1)S(1)}, bf16[96,256]{1,0:T(8,128)(2,1)S(1)}, u32[]{:S(2)}, u32[]{:S(2)}) collective-permute-start(bf16[96,256]{1,0:T(8,128)(2,1)S(1)} %get-tuple-element.69.rows_ref), channel_id=1, source_target_pairs={{32,0},{33,1},{34,2},{35,3},{36,4},{37,5},{38,6},{39,7},{160,128},... | collective-permute-start | bytes 147464 | tf_op jit(solution)/shard_map/ppermute | solution.py:429
  46.0 2.6 %copy-start.2 = (bf16[3,256,256]{2,1,0:T(8,128)(2,1)S(1)}, bf16[3,256,256]{2,1,0:T(8,128)(2,1)}, u32[]{:S(2)}) copy-start(bf16[3,256,256]{2,1,0:T(8,128)(2,1)} %seed_ref.9) | copy-start | bytes 1179652
  46.0 2.6 %copy-start.6 = (bf16[1,256,256]{2,1,0:T(8,128)(2,1)S(1)}, bf16[1,256,256]{2,1,0:T(8,128)(2,1)}, u32[]{:S(2)}) copy-start(bf16[1,256,256]{2,1,0:T(8,128)(2,1)} %param.16) | copy-start | bytes 393220
  82.9 4.4 %collective-permute-start.6 = (bf16[32,256]{1,0:T(8,128)(2,1)S(1)}, bf16[32,256]{1,0:T(8,128)(2,1)S(1)}, u32[]{:S(2)}, u32[]{:S(2)}) collective-permute-start(bf16[32,256]{1,0:T(8,128)(2,1)S(1)} %get-tuple-element.87), channel_id=1, source_target_pairs={{0,8},{16,24},{32,40},{48,56},{64,72},{80,88},{96,104},{112,120},{... | collective-permute-start | bytes 49160 | tf_op jit(solution)/shard_map/ppermute | solution.py:416
  83.1 5.1 %collective-permute-start.7 = (bf16[32,256]{1,0:T(8,128)(2,1)S(1)}, bf16[32,256]{1,0:T(8,128)(2,1)S(1)}, u32[]{:S(2)}, u32[]{:S(2)}) collective-permute-start(bf16[32,256]{1,0:T(8,128)(2,1)S(1)} %get-tuple-element.88), channel_id=1, source_target_pairs={{8,16},{24,32},{40,48},{56,64},{72,80},{88,96},{104,112},{16,8},{3... | collective-permute-start | bytes 49160 | tf_op jit(solution)/shard_map/ppermute | solution.py:416
  125.9 4.2 %collective-permute-start.8 = (bf16[32,256]{1,0:T(8,128)(2,1)S(1)}, bf16[32,256]{1,0:T(8,128)(2,1)S(1)}, u32[]{:S(2)}, u32[]{:S(2)}) collective-permute-start(bf16[32,256]{1,0:T(8,128)(2,1)S(1)} %get-tuple-element.108), channel_id=1, source_target_pairs={{0,8},{16,24},{32,40},{48,56},{64,72},{80,88},{96,104},{112,120},{... | collective-permute-start | bytes 49160 | tf_op jit(solution)/shard_map/ppermute | solution.py:416
  126.1 5.1 %collective-permute-start.9 = (bf16[32,256]{1,0:T(8,128)(2,1)S(1)}, bf16[32,256]{1,0:T(8,128)(2,1)S(1)}, u32[]{:S(2)}, u32[]{:S(2)}) collective-permute-start(bf16[32,256]{1,0:T(8,128)(2,1)S(1)} %get-tuple-element.109), channel_id=1, source_target_pairs={{8,16},{24,32},{40,48},{56,64},{72,80},{88,96},{104,112},{16,8},{3... | collective-permute-start | bytes 49160 | tf_op jit(solution)/shard_map/ppermute | solution.py:416

commit v6 on v5

--- a/solution.py
+++ b/solution.py
@@ -15,7 +15,7 @@
 EPS = 1e-06
 CHUNK = 512
 LANES = 128
-RADIX = 4
+ROUNDS = ((2, 1), (4, 2), (2, 8))
 LOW = jnp.bfloat16
 WIDE = jnp.float32
 
@@ -110,17 +110,20 @@
     return weights * (1.0 / jnp.sum(weights, axis=-1, keepdims=True))
 
 
-def attend(folded_ref, state):
+def attend(folded_ref, state, attended_ref):
     _, _, queries, keys, values, probs = state
+    heads = range(queries.shape[0])
     k_hat = hat(keys[...])
-    total = None if folded_ref is None else jnp.zeros((keys.shape[0], folded_ref.shape[1]), WIDE)
-    for head in range(queries.shape[0]):
-        chances = probabilities(hat(queries[head]), k_hat)
-        probs[head] = chances
-        if folded_ref is not None:
-            attended = dot(chances.astype(LOW), values[...]).astype(LOW)
-            total += dot(attended, folded_ref[block(head, HEAD_SIZE), :])
-    return total
+    q_hats = [hat(queries[head]) for head in heads]
+    for head in heads:
+        probs[head] = probabilities(q_hats[head], k_hat)
+    if folded_ref is None:
+        return None
+    for head in heads:
+        attended_ref[:, block(head, HEAD_SIZE)] = dot(
+            probs[head].astype(LOW), values[...]
+        ).astype(LOW)
+    return dot(attended_ref[...], folded_ref[...])
 
 
 def go_back(grads, gain_ref, expand_ref, query_ref, kv_ref, folded_ref, state, grad_q, weighted_ref):
@@ -129,22 +132,32 @@
     keys_here = keys[...]
     k_hat = hat(keys_here)
     values_here = values[...]
-    grad_khat = jnp.zeros(keys_here.shape, WIDE)
-    grad_values = jnp.zeros(keys_here.shape, WIDE)
-    for head in range(queries.shape[0]):
-        upstream = queries[head]
-        q_hat = hat(upstream)
+    grad_attended_all = dot_back(grads, folded_ref[...]).astype(LOW)
+    grad_khat = jnp.zeros(keys_here.shape[::-1], WIDE)
+    grad_values = jnp.zeros(keys_here.shape[::-1], WIDE)
+    heads = range(queries.shape[0])
+    grad_chances = [
+        dot_back(grad_attended_all[:, head * HEAD_SIZE : (head + 1) * HEAD_SIZE], values_here)
+        for head in heads
+    ]
+    for head in heads:
+        grad_values += dot_turned(
+            grad_attended_all[:, head * HEAD_SIZE : (head + 1) * HEAD_SIZE], probs[head].astype(LOW)
+        )
+    grad_scores = []
+    for head in heads:
         chances = probs[head]
-        grad_attended = dot_back(grads, folded_ref[block(head, HEAD_SIZE), :]).astype(LOW)
-        grad_chances = dot_back(grad_attended, values_here)
-        inner = jnp.sum(grad_chances * chances, axis=-1, keepdims=True)
-        grad_scores = chances * (grad_chances - inner) * (1.0 / math.sqrt(HEAD_SIZE))
-        grad_scores = grad_scores.astype(LOW)
-        grad_q[:, block(head, HEAD_SIZE)] = norm_back(upstream, dot(grad_scores, k_hat)).astype(LOW)
-        grad_khat += dot_turned(grad_scores, q_hat)
-        grad_values += dot_turned(chances.astype(LOW), grad_attended)
+        inner = jnp.sum(grad_chances[head] * chances, axis=-1, keepdims=True)
+        scores = chances * (grad_chances[head] - inner) * (1.0 / math.sqrt(HEAD_SIZE))
+        grad_scores.append(scores.astype(LOW))
+    q_hats = [hat(queries[head]) for head in heads]
+    grad_qhats = [dot(grad_scores[head], k_hat) for head in heads]
+    for head in heads:
+        grad_khat += dot_turned(q_hats[head], grad_scores[head])
+    for head in heads:
+        grad_q[:, block(head, HEAD_SIZE)] = norm_back(queries[head], grad_qhats[head]).astype(LOW)
     grad_kv = jnp.concatenate(
-        [norm_back(keys_here, grad_khat).astype(LOW), grad_values.astype(LOW)], axis=1
+        [norm_back(keys_here, grad_khat.T).astype(LOW), grad_values.T.astype(LOW)], axis=1
     )
     scaling = scale[:, :1]
     inner = jnp.zeros((keys_here.shape[0], LANES), WIDE)
@@ -208,21 +221,22 @@
     use_other = 2 * (last - segment) == tick_ref[0]
     coeffs = jnp.where(use_other, other_ref[...], stash_ref[tick_ref[0]])
     spread(coeffs, gain_ref, expand_ref, query_ref, kv_ref, state)
-    attend(None, state)
+    attend(None, state, None)
     refs[STATE][...] = jnp.zeros(refs[STATE].shape, LOW)
 
 
 def forward_kernel(
     tick_ref, gain_ref, basis_ref, rows_ref, other_ref, expand_ref, query_ref, kv_ref, folded_ref, *refs
 ):
-    payload_ref, direct_ref, coeffs_ref = refs[1 + STATE], refs[2 + 2 * STATE], refs[3 + 2 * STATE]
+    payload_ref = refs[1 + STATE]
+    direct_ref, coeffs_ref, attended_ref = refs[2 + 2 * STATE :]
     state = [ref.at[0] for ref in refs[2 + STATE : 2 + 2 * STATE]]
     segment, _ = place_in_line()
     use_other = (tick_ref[0] == 0) & (segment != 0)
     take_tiles(rows_ref, 0, other_ref, use_other, coeffs_ref)
     direct_ref[...] = direct_of(own_rows(coeffs_ref, direct_ref.shape[0]), basis_ref, False)
     spread(coeffs_ref[...], gain_ref, expand_ref, query_ref, kv_ref, state)
-    put_tiles(payload_ref, attend(folded_ref, state), 0)
+    put_tiles(payload_ref, attend(folded_ref, state, attended_ref), 0)
 
 
 def backward_kernel(
@@ -445,7 +459,7 @@
     value_weight,
     w_out,
 ):
-    if lax.axis_size("segment") != RADIX**2:
+    if lax.axis_size("segment") != math.prod(radix for radix, _ in ROUNDS):
         raise ValueError("segments")
     parts = lax.axis_size("head")
     ticks, span = token_ids.shape
@@ -510,7 +524,7 @@
             forward_kernel,
             (payload, *state_outs, wide_piece),
             [SMEM] + [VMEM] * (9 + STATE),
-            [lines],
+            [lines, pltpu.VMEM((span, queries), LOW)],
             flops=work,
             aliases={9 + place: place for place in range(1 + STATE)},
         )(number(tick), gain, basis, gathered, arriving[0], *weights, out, *state)
@@ -526,21 +540,21 @@
             aliases={10: 0},
         )(number(tick), gain, basis, gathered, returning[0], seed_grad, *weights, out, *state)
 
-    got = sent_down(rows, "segment", RADIX, 1)
+    def joined(outs, rows, got, done):
+        return call(
+            functools.partial(join_kernel, len(got)), outs, [VMEM] * (2 + len(got)), limit=4
+        )(rows, *got, done)
+
+    got = sent_down(rows, "segment", *ROUNDS[0])
     basis, folded, kv = folding(order)
     weights = (expand[0], w_query[0], kv, folded)
-    rows, order, spare, out = call(
-        functools.partial(join_kernel, len(got)),
-        (lot, piece, payload, payload),
-        [VMEM] * (2 + len(got)),
-        limit=4,
-    )(rows, *got, basis)
-    got = sent_down(rows, "segment", RADIX, RADIX)
-    state, _ = kept_of(0, order)
+    rows, order = joined((lot, piece), rows, got, basis)
+    got = sent_down(rows, "segment", *ROUNDS[1])
+    state, done = kept_of(0, order)
+    rows, spare, out = joined((lot, payload, payload), rows, got, done)
+    got = sent_down(rows, "segment", *ROUNDS[2])
     out, direct_back, done = backward(0, spare, out, state)
-    rows, tiles = call(
-        functools.partial(join_kernel, len(got)), (lot, payload), [VMEM] * (2 + len(got)), limit=4
-    )(rows, *got, done)
+    rows, tiles = joined((lot, payload), rows, got, done)
     out, state, direct = forward(0, exchanged(tiles, "head"), out, state)
 
     shares = []

time: 169 us -> 168 us (level)
  the two profiles are of different devices: /device:TPU:544 before, /device:TPU:514 now
where the time goes in v6:
time: 168 us; the launch traced here: 165 us
  blocking collectives  117 us (70%)
  Pallas kernels  30.2 us (18%)
  starting transfers between devices  9.36 us (6%)
  waiting for transfers between devices  7.8 us (5%)
    all_to_all x7, blocking collectives, exchanged(): return lax.all_to_all(tiles, axis, split_axis=0, concat_axis=0, tiled=True)  117 us
    pallas_call x20, Pallas kernels, run(): kernel(*[pltpu.with_memory_space_constraint(arg, pltpu.HBM) if spec is HB...  30.2 us
    ppermute x5, waiting for transfers between devices, sent_down(): got.append(lax.ppermute(x, axis, pairs))  7.79 us
    ppermute x5, starting transfers between devices, sent_down(): got.append(lax.ppermute(x, axis, pairs))  6.54 us
  transfers between devices with their start and end apart: 9, of which 4 were waited for; matrix products, arithmetic and copies ran while one was open for 0% of the time, Pallas kernels for 7%

profile of v6, /device:TPU:514, one launch (start us, length us, event | category | flops | bytes accessed | tf_op | source)
XLA Modules:
  0.0 165.1 jit_solution(1687217841847710639)
XLA Ops:
  0.6 0.0 copy-start.5
  0.6 0.0 copy-start.7
  0.7 0.0 copy-start.1
  0.7 2.1 %shard_map.140 = bf16[8,96,256]{2,1,0:T(8,128)(2,1)S(1)} custom-call(s32[3,256]{1,0:T(4,128)} %ids_hbm.1, bf16[1187,256]{1,0:T(8,128)(2,1)} %table_hbm.1), custom_call_target="tpu_custom_call" | custom-call | flops 1073741824 | bytes 1048576 | tf_op jit(solution)/shard_map/pallas_call | solution.py:413
  2.7 32.3 %all_to_all.35.parts_ref = bf16[8,96,256]{2,1,0:T(8,128)(2,1)S(1)} all-to-all(bf16[8,96,256]{2,1,0:T(8,128)(2,1)S(1)} %shard_map.140), channel_id=1, replica_groups=mesh['groups'=2,'segment'=16,'head'=8] {'head'}, dimensions={0} | all-to-all | bytes 786432 | tf_op jit(solution)/shard_map/all_to_all | solution.py:424
  35.0 1.3 collective-permute-start
  36.4 0.0 copy-done.5
  36.4 0.0 copy-start
  36.4 0.0 copy-start.3
  36.4 0.0 copy-start.4
  36.4 0.0 copy-start.8
  36.4 2.1 %shard_map.142 = (f32[256,256]{1,0:T(8,128)S(1)}, bf16[512,256]{1,0:T(8,128)(2,1)S(1)}, bf16[2048,256]{1,0:T(8,128)(2,1)S(1)}) custom-call(bf16[32,256]{1,0:T(8,128)(2,1)S(1)} %get-tuple-element.68.order_ref, bf16[256,2048]{1,0:T(8,128)(2,1)S(1)} %bitcast.19, bf16[2048,256]{1,0:T(8,128)(2,1)S(1)} %bitcast.42, bf16[512,2048]{1,0:T(8,128)(2,1)S(1)} %bitcast.38, ...), custom_call_target="tpu_custom_call" | custom-call | flops 805306368 | bytes 1048576 | tf_op jit(solution)/shard_map/pallas_call | solution.py:413
  38.5 0.0 collective-permute-done.refs_0_
  38.6 1.3 collective-permute-start.3
  39.9 1.3 collective-permute-start.2
  41.2 1.3 collective-permute-start.1
  42.5 0.0 copy-start.2
  42.6 0.0 copy-start.6
  42.6 2.1 %shard_map.144 = (f32[2,4,256,512]{3,2,1,0:T(8,128)S(1)}, f32[2,256,128]{2,1,0:T(8,128)S(1)}, f32[2,4,256,128]{3,2,1,0:T(8,128)S(1)}, f32[2,256,128]{2,1,0:T(8,1...) custom-call(s32[1]{0:T(128)} %constant.2.clone.1.tick_ref, ...), custom_call_target="tpu_custom_call" | custom-call | flops 1073741824 | bytes 1048576 | tf_op jit(solution)/shard_map/pallas_call | solution.py:413
  44.6 1.8 %collective-permute-done.3.refs_2_ = bf16[96,256]{1,0:T(8,128)(2,1)S(1)} collective-permute-done((bf16[96,256]{1,0:T(8,128)(2,1)S(1)}, bf16[96,256]{1,0:T(8,128)(2,1)S(1)}, u32[]{:S(2)}, u32[]{:S(2)}) %collective-permute-start.3) | collective-permute-done | bytes 49184 | tf_op jit(solution)/shard_map/ppermute | solution.py:443
  46.4 0.5 collective-permute-done.2.refs_1_
  46.9 0.5 collective-permute-done.1.refs_0_
  47.4 0.1 shard_map.145
  47.5 1.3 collective-permute-start.4
  48.8 3.6 %shard_map.146 = (bf16[8,64,256]{2,1,0:T(8,128)(2,1)S(1)}, f32[32,256]{1,0:T(8,128)S(1)}, bf16[16,128]{1,0:T(8,128)(2,1)S(1)}) custom-call(s32[1]{0:T(128)} %constant.2.clone.1.tick_ref, f32[4,1,512]{2,1,0:T(1,128)S(1)} %bitcast.44, f32[256,256]{1,0:T(8,128)S(1)} %get-tuple-element.69.refs_1_.basis_ref, ...), custom_call_target="tpu_custom_call", output_to_operand_aliasing={{0}: (10, {})} | custom-call | flops 1073741824 | bytes 1048576 | tf_op jit(solution)/shard_map/pallas_call | solution.py:413
  52.4 5.0 %collective-permute-done.4.refs_0_ = bf16[96,256]{1,0:T(8,128)(2,1)S(1)} collective-permute-done((bf16[96,256]{1,0:T(8,128)(2,1)S(1)}, bf16[96,256]{1,0:T(8,128)(2,1)S(1)}, u32[]{:S(2)}, u32[]{:S(2)}) %collective-permute-start.4) | collective-permute-done | bytes 49184 | tf_op jit(solution)/shard_map/ppermute | solution.py:443
  57.4 12.9 %all_to_all.36.rows_ref = bf16[8,64,256]{2,1,0:T(8,128)(2,1)S(1)} all-to-all(bf16[8,64,256]{2,1,0:T(8,128)(2,1)S(1)} %get-tuple-element.86), channel_id=1, replica_groups=mesh['groups'=2,'segment'=16,'head'=8] {'head'}, dimensions={0} | all-to-all | bytes 524288 | tf_op jit(solution)/shard_map/all_to_all | solution.py:424
  70.4 2.4 %shard_map.148 = (bf16[8,64,256]{2,1,0:T(8,128)(2,1)S(1)}, f32[2,4,256,512]{3,2,1,0:T(8,128)S(1)}, f32[2,256,128]{2,1,0:T(8,128)S(1)}, f32[2,4,256,128]{3,2,1,0:...) custom-call(s32[1]{0:T(128)} %constant.2.clone.1.tick_ref, ...), custom_call_target="tpu_custom_call", output_to_operand_aliasing={{0}: (9, {}), {1}: (10, {}), {2}: (11, {}), {3}: (12, {}), ... | custom-call | flops 1073741824 | bytes 1048576 | tf_op jit(solution)/shard_map/pallas_call | solution.py:413
  72.8 13.1 %all_to_all.37.parts_ref = bf16[8,64,256]{2,1,0:T(8,128)(2,1)S(1)} all-to-all(bf16[8,64,256]{2,1,0:T(8,128)(2,1)S(1)} %get-tuple-element.88.refs_0_), channel_id=1, replica_groups=mesh['groups'=2,'segment'=16,'head'=8] {'head'}, dimensions={0} | all-to-all | bytes 524288 | tf_op jit(solution)/shard_map/all_to_all | solution.py:424
  86.0 0.1 collective-permute-start.5
  86.1 0.8 collective-permute-start.6
  87.0 2.1 %shard_map.150 = (f32[2,4,256,512]{3,2,1,0:T(8,128)S(1)}, f32[2,256,128]{2,1,0:T(8,128)S(1)}, f32[2,4,256,128]{3,2,1,0:T(8,128)S(1)}, f32[2,256,128]{2,1,0:T(8,1...) custom-call(s32[1]{0:T(128)} %constant.1.clone.1.tick_ref, ...), custom_call_target="tpu_custom_call" | custom-call | flops 1073741824 | bytes 1048576 | tf_op jit(solution)/shard_map/pallas_call | solution.py:413
  89.0 0.0 collective-permute-done.5.first_ref
  89.0 0.0 collective-permute-done.6.second_ref
  89.1 13.1 %all_to_all.38.rows_ref = bf16[8,64,256]{2,1,0:T(8,128)(2,1)S(1)} all-to-all(bf16[8,64,256]{2,1,0:T(8,128)(2,1)S(1)} %shard_map.151), channel_id=1, replica_groups=mesh['groups'=2,'segment'=16,'head'=8] {'head'}, dimensions={0} | all-to-all | bytes 524288 | tf_op jit(solution)/shard_map/all_to_all | solution.py:424
  102.2 2.4 %shard_map.152 = (bf16[8,64,256]{2,1,0:T(8,128)(2,1)S(1)}, f32[2,4,256,512]{3,2,1,0:T(8,128)S(1)}, f32[2,256,128]{2,1,0:T(8,128)S(1)}, f32[2,4,256,128]{3,2,1,0:...) custom-call(s32[1]{0:T(128)} %constant.1.clone.1.tick_ref, ...), custom_call_target="tpu_custom_call", output_to_operand_aliasing={{0}: (9, {}), {1}: (10, {}), {2}: (11, {}), {3}: (12, {}), ... | custom-call | flops 1073741824 | bytes 1048576 | tf_op jit(solution)/shard_map/pallas_call | solution.py:413
  104.6 4.0 %shard_map.153 = (bf16[8,64,256]{2,1,0:T(8,128)(2,1)S(1)}, f32[32,256]{1,0:T(8,128)S(1)}, bf16[16,128]{1,0:T(8,128)(2,1)}) custom-call(s32[1]{0:T(128)} %constant.1.clone.1.tick_ref, f32[4,1,512]{2,1,0:T(1,128)S(1)} %bitcast.48, f32[256,256]{1,0:T(8,128)S(1)} %get-tuple-element.69.refs_1_.basis_ref, ...), custom_call_target="tpu_custom_call", output_to_operand_aliasing={{0}: (10, {})} | custom-call | flops 1073741824 | bytes 1048576 | tf_op jit(solution)/shard_map/pallas_call | solution.py:413
  108.6 15.5 %all_to_all.39.parts_ref = bf16[8,64,256]{2,1,0:T(8,128)(2,1)S(1)} all-to-all(bf16[8,64,256]{2,1,0:T(8,128)(2,1)S(1)} %get-tuple-element.109.refs_0_), channel_id=1, replica_groups=mesh['groups'=2,'segment'=16,'head'=8] {'head'}, dimensions={0} | all-to-all | bytes 524288 | tf_op jit(solution)/shard_map/all_to_all | solution.py:424
  124.2 1.2 collective-permute-start.7
  125.4 0.7 collective-permute-start.8
  126.0 2.1 %shard_map.155 = (f32[2,4,256,512]{3,2,1,0:T(8,128)S(1)}, f32[2,256,128]{2,1,0:T(8,128)S(1)}, f32[2,4,256,128]{3,2,1,0:T(8,128)S(1)}, f32[2,256,128]{2,1,0:T(8,1...) custom-call(s32[1]{0:T(128)} %constant.0.clone.1.tick_ref, ...), custom_call_target="tpu_custom_call" | custom-call | flops 1073741824 | bytes 1048576 | tf_op jit(solution)/shard_map/pallas_call | solution.py:413
  128.1 0.0 collective-permute-done.7.first_ref
  128.1 0.0 collective-permute-done.8.second_ref
  128.2 13.2 %all_to_all.40.rows_ref = bf16[8,64,256]{2,1,0:T(8,128)(2,1)S(1)} all-to-all(bf16[8,64,256]{2,1,0:T(8,128)(2,1)S(1)} %shard_map.156), channel_id=1, replica_groups=mesh['groups'=2,'segment'=16,'head'=8] {'head'}, dimensions={0} | all-to-all | bytes 524288 | tf_op jit(solution)/shard_map/all_to_all | solution.py:424
  141.4 2.4 %shard_map.157 = (bf16[8,64,256]{2,1,0:T(8,128)(2,1)S(1)}, f32[2,4,256,512]{3,2,1,0:T(8,128)S(1)}, f32[2,256,128]{2,1,0:T(8,128)S(1)}, f32[2,4,256,128]{3,2,1,0:...) custom-call(s32[1]{0:T(128)} %constant.0.clone.1.tick_ref, ...), custom_call_target="tpu_custom_call", output_to_operand_aliasing={{0}: (9, {}), {1}: (10, {}), {2}: (11, {}), {3}: (12, {}), ... | custom-call | flops 1073741824 | bytes 1048576 | tf_op jit(solution)/shard_map/pallas_call | solution.py:413
  143.9 4.0 %shard_map.158 = (bf16[8,64,256]{2,1,0:T(8,128)(2,1)S(1)}, f32[32,256]{1,0:T(8,128)S(1)}, bf16[16,128]{1,0:T(8,128)(2,1)}) custom-call(s32[1]{0:T(128)} %constant.0.clone.1.tick_ref, f32[4,1,512]{2,1,0:T(1,128)S(1)} %bitcast.51, f32[256,256]{1,0:T(8,128)S(1)} %get-tuple-element.69.refs_1_.basis_ref, ...), custom_call_target="tpu_custom_call", output_to_operand_aliasing={{0}: (10, {})} | custom-call | flops 1073741824 | bytes 1048576 | tf_op jit(solution)/shard_map/pallas_call | solution.py:413
  147.9 16.5 %all_to_all.41.parts_ref = bf16[8,64,256]{2,1,0:T(8,128)(2,1)S(1)} all-to-all(bf16[8,64,256]{2,1,0:T(8,128)(2,1)S(1)} %get-tuple-element.129), channel_id=1, replica_groups=mesh['groups'=2,'segment'=16,'head'=8] {'head'}, dimensions={0} | all-to-all | bytes 524288 | tf_op jit(solution)/shard_map/all_to_all | solution.py:424
  164.4 0.7 shard_map.159
  (15 shorter events, 0.2 us)
Async XLA Ops:
  0.6 35.7 %copy-start.5 = (bf16[1,512,2048]{2,1,0:T(8,128)(2,1)S(1)}, bf16[1,512,2048]{2,1,0:T(8,128)(2,1)}, u32[]{:S(2)}) copy-start(bf16[1,512,2048]{2,1,0:T(8,128)(2,1)} %param.25) | copy-start | bytes 6291460
  0.6 35.7 %copy-start.7 = (bf16[1,2048,256]{2,1,0:T(8,128)(2,1)S(1)}, bf16[1,2048,256]{2,1,0:T(8,128)(2,1)}, u32[]{:S(2)}) copy-start(bf16[1,2048,256]{2,1,0:T(8,128)(2,1)} %param.20) | copy-start | bytes 3145732
  0.7 35.7 %copy-start.1 = (bf16[1,256,2048]{2,1,0:T(8,128)(2,1)S(1)}, bf16[1,256,2048]{2,1,0:T(8,128)(2,1)}, u32[]{:S(2)}) copy-start(bf16[1,256,2048]{2,1,0:T(8,128)(2,1)} %param.19) | copy-start | bytes 3145732
  35.0 3.5 %collective-permute-start = (bf16[96,256]{1,0:T(8,128)(2,1)S(1)}, bf16[96,256]{1,0:T(8,128)(2,1)S(1)}, u32[]{:S(2)}, u32[]{:S(2)}) collective-permute-start(bf16[96,256]{1,0:T(8,128)(2,1)S(1)} %get-tuple-element.70.rows_ref), channel_id=1, source_target_pairs={{8,0},{24,16},{40,32},{56,48},{72,64},{88,80},{104,96},{120,112},{... | collective-permute-start | bytes 147464 | tf_op jit(solution)/shard_map/ppermute | solution.py:443
  36.4 6.1 %copy-start = (bf16[1,2048,512]{2,1,0:T(8,128)(2,1)S(1)}, bf16[1,2048,512]{2,1,0:T(8,128)(2,1)}, u32[]{:S(2)}) copy-start(bf16[1,2048,512]{2,1,0:T(8,128)(2,1)} %param.22) | copy-start | bytes 6291460
  36.4 6.1 %copy-start.3 = (bf16[1,256,256]{2,1,0:T(8,128)(2,1)S(1)}, bf16[1,256,256]{2,1,0:T(8,128)(2,1)}, u32[]{:S(2)}) copy-start(bf16[1,256,256]{2,1,0:T(8,128)(2,1)} %param.15) | copy-start | bytes 393220
  36.4 6.1 %copy-start.4 = (bf16[1,3,256,256]{3,2,1,0:T(8,128)(2,1)S(1)}, bf16[1,3,256,256]{3,2,1,0:T(8,128)(2,1)}, u32[]{:S(2)}) copy-start(bf16[1,3,256,256]{3,2,1,0:T(8,128)(2,1)} %param.17) | copy-start | bytes 1179652
  36.4 6.1 %copy-start.8 = (f32[1,2048]{1,0:T(1,128)S(1)}, f32[1,2048]{1,0:T(1,128)}, u32[]{:S(2)}) copy-start(f32[1,2048]{1,0:T(1,128)} %param.21) | copy-start | bytes 24580
  38.6 7.8 %collective-permute-start.3 = (bf16[96,256]{1,0:T(8,128)(2,1)S(1)}, bf16[96,256]{1,0:T(8,128)(2,1)S(1)}, u32[]{:S(2)}, u32[]{:S(2)}) collective-permute-start(bf16[96,256]{1,0:T(8,128)(2,1)S(1)} %get-tuple-element.71.rows_ref), channel_id=1, source_target_pairs={{48,0},{112,64},{49,1},{113,65},{50,2},{114,66},{51,3},{115,67},{5... | collective-permute-start | bytes 147464 | tf_op jit(solution)/shard_map/ppermute | solution.py:443
  39.9 7.0 %collective-permute-start.2 = (bf16[96,256]{1,0:T(8,128)(2,1)S(1)}, bf16[96,256]{1,0:T(8,128)(2,1)S(1)}, u32[]{:S(2)}, u32[]{:S(2)}) collective-permute-start(bf16[96,256]{1,0:T(8,128)(2,1)S(1)} %get-tuple-element.71.rows_ref), channel_id=1, source_target_pairs={{32,0},{96,64},{33,1},{97,65},{34,2},{98,66},{35,3},{99,67},{36,4}... | collective-permute-start | bytes 147464 | tf_op jit(solution)/shard_map/ppermute | solution.py:443
  41.2 6.2 %collective-permute-start.1 = (bf16[96,256]{1,0:T(8,128)(2,1)S(1)}, bf16[96,256]{1,0:T(8,128)(2,1)S(1)}, u32[]{:S(2)}, u32[]{:S(2)}) collective-permute-start(bf16[96,256]{1,0:T(8,128)(2,1)S(1)} %get-tuple-element.71.rows_ref), channel_id=1, source_target_pairs={{16,0},{80,64},{17,1},{81,65},{18,2},{82,66},{19,3},{83,67},{20,4}... | collective-permute-start | bytes 147464 | tf_op jit(solution)/shard_map/ppermute | solution.py:443
  42.5 6.3 %copy-start.2 = (bf16[3,256,256]{2,1,0:T(8,128)(2,1)S(1)}, bf16[3,256,256]{2,1,0:T(8,128)(2,1)}, u32[]{:S(2)}) copy-start(bf16[3,256,256]{2,1,0:T(8,128)(2,1)} %seed_ref.9) | copy-start | bytes 1179652
  42.6 6.3 %copy-start.6 = (bf16[1,256,256]{2,1,0:T(8,128)(2,1)S(1)}, bf16[1,256,256]{2,1,0:T(8,128)(2,1)}, u32[]{:S(2)}) copy-start(bf16[1,256,256]{2,1,0:T(8,128)(2,1)} %param.16) | copy-start | bytes 393220
  47.5 9.9 %collective-permute-start.4 = (bf16[96,256]{1,0:T(8,128)(2,1)S(1)}, bf16[96,256]{1,0:T(8,128)(2,1)S(1)}, u32[]{:S(2)}, u32[]{:S(2)}) collective-permute-start(bf16[96,256]{1,0:T(8,128)(2,1)S(1)} %get-tuple-element.75.rows_ref), channel_id=1, source_target_pairs={{64,0},{65,1},{66,2},{67,3},{68,4},{69,5},{70,6},{71,7},{192,128},... | collective-permute-start | bytes 147464 | tf_op jit(solution)/shard_map/ppermute | solution.py:443
  86.0 3.1 %collective-permute-start.5 = (bf16[32,256]{1,0:T(8,128)(2,1)S(1)}, bf16[32,256]{1,0:T(8,128)(2,1)S(1)}, u32[]{:S(2)}, u32[]{:S(2)}) collective-permute-start(bf16[32,256]{1,0:T(8,128)(2,1)S(1)} %get-tuple-element.91), channel_id=1, source_target_pairs={{0,8},{16,24},{32,40},{48,56},{64,72},{80,88},{96,104},{112,120},{... | collective-permute-start | bytes 49160 | tf_op jit(solution)/shard_map/ppermute | solution.py:430
  86.1 2.9 %collective-permute-start.6 = (bf16[32,256]{1,0:T(8,128)(2,1)S(1)}, bf16[32,256]{1,0:T(8,128)(2,1)S(1)}, u32[]{:S(2)}, u32[]{:S(2)}) collective-permute-start(bf16[32,256]{1,0:T(8,128)(2,1)S(1)} %get-tuple-element.92), channel_id=1, source_target_pairs={{8,16},{24,32},{40,48},{56,64},{72,80},{88,96},{104,112},{16,8},{3... | collective-permute-start | bytes 49160 | tf_op jit(solution)/shard_map/ppermute | solution.py:430
  124.2 3.9 %collective-permute-start.7 = (bf16[32,256]{1,0:T(8,128)(2,1)S(1)}, bf16[32,256]{1,0:T(8,128)(2,1)S(1)}, u32[]{:S(2)}, u32[]{:S(2)}) collective-permute-start(bf16[32,256]{1,0:T(8,128)(2,1)S(1)} %get-tuple-element.112), channel_id=1, source_target_pairs={{0,8},{16,24},{32,40},{48,56},{64,72},{80,88},{96,104},{112,120},{... | collective-permute-start | bytes 49160 | tf_op jit(solution)/shard_map/ppermute | solution.py:430
  125.4 2.7 %collective-permute-start.8 = (bf16[32,256]{1,0:T(8,128)(2,1)S(1)}, bf16[32,256]{1,0:T(8,128)(2,1)S(1)}, u32[]{:S(2)}, u32[]{:S(2)}) collective-permute-start(bf16[32,256]{1,0:T(8,128)(2,1)S(1)} %get-tuple-element.113), channel_id=1, source_target_pairs={{8,16},{24,32},{40,48},{56,64},{72,80},{88,96},{104,112},{16,8},{3... | collective-permute-start | bytes 49160 | tf_op jit(solution)/shard_map/ppermute | solution.py:430
